TPU v7x, 512 devices: a 8x2x16 block of a 8x8x16 slice. The times are simulated.
512 devices in a mesh: groups: 2 (over y), branch: 2 (over core), tok: 128 (over x, z).
Axes of the slice: x: 8, y: 2, z: 16, core: 2. Of those that a mesh axis runs over, the one named last changes fastest.
The devices are a block of a 8x8x16 slice.
Arguments:
- queries: bfloat16 [8192, 4096], P(('groups', 'tok')), parts along dimension 0, may hold values from -8 to 8
- keys: bfloat16 [8192, 4096], P(('groups', 'tok')), parts along dimension 0, may hold values from -8 to 8
- values: bfloat16 [8192, 4096], P(('groups', 'tok')), parts along dimension 0, may hold values from -6 to 6
- keyboard: int32 [16], P('groups'), parts along dimension 0, may hold values from 0 to 15
- mouse: int32 [16], P('groups'), parts along dimension 0, may hold values from 0 to 31
- key_table: bfloat16 [16, 2, 4096], replicated, may hold values from -3 to 3
- mouse_table: bfloat16 [32, 2, 4096], replicated, may hold values from -3 to 3
- guidance: float32 [4], replicated, may hold values from 0.5 to 1.5
- out_weight: bfloat16 [4096, 64], replicated, may hold values from -0.09375 to 0.09375
- latent: float32 [8192, 64], P(('groups', 'tok')), parts along dimension 0, may hold values from -6 to 6
- conv_in: bfloat16 [3, 3, 16, 384], replicated, may hold values from -0.5 to 0.5
- gain: float32 [384], replicated, may hold values from 0.5 to 1.5
- conv_out: bfloat16 [3, 3, 384, 3], replicated, may hold values from -0.109375 to 0.109375
Outputs:
- velocity: float32 [8192, 64], P(('groups', 'tok')), parts along dimension 0
- frames_rgb: float32 [3, 512, 64], P(None, ('groups', 'tok')), parts along dimension 1
There are 2 independent parts, one for each index of `groups`. A program takes and returns all parts, laid end to end along the dimension named above; an argument that names none is the same for every part. Nothing has to cross between parts.
All inputs are finite; a program needn't handle non-finite values.
Results may differ from a plain program's by a relative error of at most 0.012.
Values may be sent and summed in bfloat16 or wider, within the bound.
No kernel may reach another device: no remote copies, remote signals or barrier semaphores. Data moves between devices by JAX's collectives and lax.ppermute only.
A program may use at most 64 MiB of HBM per device.

v0:
```python
import jax
import jax.numpy as jnp
from jax import lax
from jax.sharding import PartitionSpec as P

HEAD_DIM = 128


step_size = 0.25
norm_eps = 1e-06


def passed_along(value, axis, steps):
    count = lax.axis_size(axis)
    pairs = [(source, (source + steps) % count) for source in range(count)]
    return lax.ppermute(value, axis, pairs)


def in_one_piece(arrays, axis, split_dim, concat_dim, along):
    ends, at = ([], 0)
    for a in arrays[:-1]:
        at += a.shape[along]
        ends.append(at)
    both = jnp.concatenate(arrays, axis=along)
    return tuple(
        jnp.split(
            lax.all_to_all(both, axis, split_axis=split_dim, concat_axis=concat_dim, tiled=True),
            ends,
            axis=along,
        )
    )


def from_everyone(x, axis):
    devices = lax.axis_size(axis)
    return lax.all_to_all(jnp.broadcast_to(x[None], (devices, *x.shape)), axis, 0, 0, tiled=True)


def of_everyone(x, axis):
    return from_everyone(x, axis).sum(axis=0)


def with_halo(block, sides, width):
    for axis, dim in sides:
        count = lax.axis_size(axis)
        forward = [(i, i + 1) for i in range(count - 1)]
        backward = [(target, source) for source, target in forward]
        low = lax.ppermute(
            lax.slice_in_dim(block, block.shape[dim] - width, None, axis=dim), axis, forward
        )
        high = lax.ppermute(lax.slice_in_dim(block, 0, width, axis=dim), axis, backward)
        block = jnp.concatenate([low, block, high], axis=dim)
    return block


def action_terms(keyboard, mouse, key_table, mouse_table, branch):
    flag_key = jnp.where(branch % 2 == 0, 1.0, 0.0).astype(jnp.float32)
    flag_mouse = jnp.where(branch < 2, 1.0, 0.0).astype(jnp.float32)
    pick_key = (
        keyboard[:, None] == jnp.arange(key_table.shape[0], dtype=jnp.int32)[None, :]
    ).astype(jnp.bfloat16)
    pick_mouse = (
        mouse[:, None] == jnp.arange(mouse_table.shape[0], dtype=jnp.int32)[None, :]
    ).astype(jnp.bfloat16)
    rows_key = jnp.einsum("fk,kcd->fcd", pick_key, key_table, preferred_element_type=jnp.float32)
    rows_mouse = jnp.einsum(
        "fk,kcd->fcd", pick_mouse, mouse_table, preferred_element_type=jnp.float32
    )
    return flag_key * rows_key + flag_mouse * rows_mouse


def pick_heads(array, first, taken, sets):
    lead = array.shape[:-1]
    split = array.reshape(lead + (sets, -1, HEAD_DIM))
    kept = lax.dynamic_slice_in_dim(split, first, taken, len(lead) + 1)
    return kept.reshape(lead + (sets * taken * HEAD_DIM,))


def heads_layout(array, rounds, sets):
    rows, width = array.shape
    piece = rows // rounds
    grouped = array.reshape(rounds, piece, sets, width // sets)
    return grouped.transpose(0, 2, 1, 3).reshape(rows * sets, width // sets)


def tokens_layout(array, rounds, sets):
    rows, width = array.shape
    piece = rows // (rounds * sets)
    grouped = array.reshape(rounds, sets, piece, width)
    return grouped.transpose(0, 2, 1, 3).reshape(rounds * piece, sets * width)


def attend(local_q, local_k, local_v, key_bias, value_term, rounds, sets):
    rows, width = local_q.shape
    heads_here = width // HEAD_DIM
    count_branches = key_bias.shape[0]
    frames = key_bias.shape[1]
    block = rows // frames
    scale = HEAD_DIM ** (-0.5)
    query = local_q.reshape(rows, heads_here, HEAD_DIM)
    bias_heads = key_bias.reshape(count_branches, frames, heads_here, HEAD_DIM)
    frame_scores = jnp.einsum(
        "qhd,bfhd->bhqf", query, bias_heads, preferred_element_type=jnp.float32
    )

    def visit(block_keys, block_values, carry):
        top, total, summed = carry
        base = jnp.einsum(
            "qhd,khd->hqk",
            query,
            block_keys.reshape(rows, heads_here, HEAD_DIM),
            preferred_element_type=jnp.float32,
        )
        grouped = base.reshape(heads_here, rows, frames, block)
        plain_values = block_values.astype(jnp.float32).reshape(frames, block, width)
        tops, totals, sums = ([], [], [])
        for which in range(count_branches):
            scores = (grouped + frame_scores[which][..., None]).reshape(
                heads_here, rows, rows
            ) * scale
            fresh = jnp.maximum(top[which], jnp.max(scores, axis=-1))
            shrink = jnp.exp(top[which] - fresh)
            raised = jnp.exp(scores - fresh[..., None])
            shifted = (plain_values + value_term[which][:, None, :]).astype(jnp.bfloat16)
            shifted = shifted.reshape(rows, heads_here, HEAD_DIM)
            product = jnp.einsum(
                "hqk,khd->hqd",
                raised.astype(jnp.bfloat16),
                shifted,
                preferred_element_type=jnp.float32,
            )
            tops.append(fresh)
            totals.append(total[which] * shrink + jnp.sum(raised, axis=-1))
            sums.append(summed[which] * shrink[..., None] + product)
        return (jnp.stack(tops), jnp.stack(totals), jnp.stack(sums))

    start = (
        jnp.full((count_branches, heads_here, rows), -jnp.inf, jnp.float32),
        jnp.zeros((count_branches, heads_here, rows), jnp.float32),
        jnp.zeros((count_branches, heads_here, rows, HEAD_DIM), jnp.float32),
    )
    carry = visit(local_k, local_v, start)

    def turn(step, state):
        block_keys, block_values, inner = state
        block_keys, block_values = passed_along((block_keys, block_values), "tok", sets)
        return (block_keys, block_values, visit(block_keys, block_values, inner))

    _, _, carry = lax.fori_loop(0, rounds - 1, turn, (local_k, local_v, carry))
    _, total, summed = carry
    attended = (summed / total[..., None]).astype(jnp.bfloat16)
    return attended.transpose(0, 2, 1, 3).reshape(count_branches, rows, heads_here * HEAD_DIM)


def clear_rows(array, depth, top_edge, bottom_edge):
    height = array.shape[0]
    place = jnp.arange(height, dtype=jnp.int32)
    drop = (place < depth) & top_edge | (place >= height - depth) & bottom_edge
    return jnp.where(drop[:, None, None], jnp.zeros_like(array), array)


def convolve(array, weight):
    rows = array.shape[0] - 2
    cols = array.shape[1]
    padded = jnp.pad(array, ((0, 0), (1, 1), (0, 0)))
    total = jnp.zeros((rows, cols, weight.shape[-1]), jnp.float32)
    for first in range(3):
        for second in range(3):
            window = padded[first : first + rows, second : second + cols, :]
            total = total + jnp.einsum(
                "rci,io->rco", window, weight[first, second], preferred_element_type=jnp.float32
            )
    return total


def normalize(features, gain):
    scaled = (
        features
        * lax.rsqrt(jnp.mean(features * features, axis=-1, keepdims=True) + norm_eps)
        * gain
    )
    return jax.nn.silu(scaled).astype(jnp.bfloat16)


def shards(
    queries,
    keys,
    values,
    keyboard,
    mouse,
    key_table,
    mouse_table,
    guidance,
    out_weight,
    latent,
    conv_in,
    gain,
    conv_out,
):
    count = lax.axis_size("tok")
    index = lax.axis_index("tok")
    branch = lax.axis_index("branch")
    sets = min(16, count)
    rounds = count // sets
    group = index % sets
    tok_dev, width = queries.shape
    per_group = width // (sets * HEAD_DIM)
    taken = per_group // 2
    first = branch * taken
    branches = [0, 1, 2, 3]
    spread_q = heads_layout(pick_heads(queries, first, taken, sets), rounds, sets)
    spread_k = heads_layout(pick_heads(keys, first, taken, sets), rounds, sets)
    spread_v = heads_layout(pick_heads(values, first, taken, sets), rounds, sets)
    local_q, local_k, local_v = in_one_piece((spread_q, spread_k, spread_v), "tok", 0, 0, 1)
    terms = jnp.stack(
        [action_terms(keyboard, mouse, key_table, mouse_table, which) for which in branches]
    )
    mine = pick_heads(terms, first, taken, sets)
    mine = mine.reshape(mine.shape[:-1] + (sets, -1))
    mine = lax.dynamic_index_in_dim(mine, group, 3, keepdims=False)
    key_bias = mine[:, :, 0].astype(jnp.bfloat16)
    value_term = mine[:, :, 1]
    outputs = attend(local_q, local_k, local_v, key_bias, value_term, rounds, sets)
    factors = [guidance[which] for which in branches]
    partial_value = factors[0] * outputs[0].astype(jnp.float32)
    for which in range(1, len(branches)):
        partial_value = partial_value + factors[which] * outputs[which].astype(jnp.float32)
    returned = lax.all_to_all(
        partial_value.astype(jnp.bfloat16), "tok", split_axis=0, concat_axis=0, tiled=True
    )
    split_weight = out_weight.reshape(sets, per_group, HEAD_DIM, -1)
    rows_weight = lax.dynamic_slice_in_dim(split_weight, first, taken, 1).reshape(
        sets * taken * HEAD_DIM, -1
    )
    projected = jnp.dot(
        tokens_layout(returned, rounds, sets), rows_weight, preferred_element_type=jnp.float32
    )
    velocity = of_everyone(projected, "branch")
    stepped = latent - step_size * velocity
    grid = (
        stepped.reshape(tok_dev, 2, 2, -1)
        .transpose(1, 0, 2, 3)
        .reshape(2, 2 * tok_dev, -1)
        .astype(jnp.bfloat16)
    )
    top_edge = index == 0
    bottom_edge = index == count - 1
    widened = with_halo(grid, (("tok", 0),), 2)
    widened = clear_rows(widened, 2, top_edge, bottom_edge)
    hidden = normalize(convolve(widened, conv_in), gain)
    hidden = clear_rows(hidden, 1, top_edge, bottom_edge)
    colours = convolve(hidden, conv_out)
    return (velocity, colours.transpose(2, 0, 1))


def solution(mesh):
    placed = (
        P(("groups", "tok"), None),
        P(("groups", "tok"), None),
        P(("groups", "tok"), None),
        P("groups"),
        P("groups"),
        P(),
        P(),
        P(),
        P(),
        P(("groups", "tok"), None),
        P(),
        P(),
        P(),
    )
    return jax.shard_map(
        shards,
        mesh=mesh,
        in_specs=placed,
        out_specs=(P(("groups", "tok"), None), P(None, ("groups", "tok"), None)),
        check_vma=False,
    )
```

profile of v0, /device:TPU:80, one launch (start us, length us, event | category | flops | bytes accessed | tf_op | source)
XLA Modules:
  0.0 228.6 jit_solution(801402997376585778)
XLA Ops:
  0.7 1.2 reshape.723
  2.7 0.9 copy-done.3
  4.2 1.0 copy.90
  5.2 54.9 %all-to-all-start = ((bf16[128,4,384]{2,1,0:T(4,128)(2,1)}), bf16[128,4,384]{2,1,0:T(4,128)(2,1)S(1)}, u32[]{:S(2)}, u32[]{:S(2)}) async-start(bf16[128,4,384]{2,1,0:T(4,128)(2,1)} %copy.90), calls=%async_computation | async-start | bytes 786432 | tf_op jit(solution)/shard_map/all_to_all | solution.py:27
  62.2 24.4 %all-to-all-done = bf16[128,4,384]{2,1,0:T(4,128)(2,1)S(1)} async-done(((bf16[128,4,384]{2,1,0:T(4,128)(2,1)}), bf16[128,4,384]{2,1,0:T(4,128)(2,1)S(1)}, u32[]{:S(2)}, u32[]{:S(2)}) %all-to-all-start) | async-done | bytes 393248 | tf_op jit(solution)/shard_map/all_to_all | solution.py:27
  87.6 0.9 fusion.46
  90.2 87.3 %while.18 = (s32[]{:T(128)}, bf16[512,128]{1,0:T(8,128)(2,1)S(1)}, bf16[512,128]{1,0:T(8,128)(2,1)S(1)}, f32[4,1,512]{2,1,0:T(1,128)S(1)}, f32[4,1,512]{2,1,0:T(...) while((s32[]{:T(128)}, bf16[512,128]{1,0:T(8,128)(2,1)S(1)}, ...), condition=%wide.region_17.18_spmd, body=%wide.region_8.17_spmd.sunk | while | flops 345853952 | bytes 13975733 | solution.py:149
  90.2 2.8 %collective-permute-start = (bf16[512,128]{1,0:T(8,128)(2,1)S(1)}, bf16[512,128]{1,0:T(8,128)(2,1)S(1)}, u32[]{:S(2)}, u32[]{:S(2)}) collective-permute-start(bf16[512,128]{1,0:T(8,128)(2,1)S(1)} %get-tuple-element.387), channel_id=1, source_target_pairs={{0,16},{1,17},{2,18},{3,19},{4,20},{5,21},{6,22},{7,23},{8,24},{9,... | collective-permute-start | bytes 393224 | tf_op jit(solution)/shard_map/while/body/eval_jaxpr/ppermute | solution.py:16
  93.0 2.8 %collective-permute-start.1 = (bf16[512,128]{1,0:T(8,128)(2,1)S(1)}, bf16[512,128]{1,0:T(8,128)(2,1)S(1)}, u32[]{:S(2)}, u32[]{:S(2)}) collective-permute-start(bf16[512,128]{1,0:T(8,128)(2,1)S(1)} %get-tuple-element.388), channel_id=1, source_target_pairs={{0,16},{1,17},{2,18},{3,19},{4,20},{5,21},{6,22},{7,23},{8,24},{9,... | collective-permute-start | bytes 393224 | tf_op jit(solution)/shard_map/while/body/eval_jaxpr/ppermute | solution.py:16
  95.9 2.4 %collective-permute-done = bf16[512,128]{1,0:T(8,128)(2,1)S(1)} collective-permute-done((bf16[512,128]{1,0:T(8,128)(2,1)S(1)}, bf16[512,128]{1,0:T(8,128)(2,1)S(1)}, u32[]{:S(2)}, u32[]{:S(2)}) %collective-permute-start) | collective-permute-done | bytes 131104 | tf_op jit(solution)/shard_map/while/body/eval_jaxpr/ppermute | solution.py:16
  98.9 0.9 fusion.215
  99.9 1.3 collective-permute-done.1
  102.8 2.0 collective-permute-start
  104.8 2.4 %collective-permute-start.1 = (bf16[512,128]{1,0:T(8,128)(2,1)S(1)}, bf16[512,128]{1,0:T(8,128)(2,1)S(1)}, u32[]{:S(2)}, u32[]{:S(2)}) collective-permute-start(bf16[512,128]{1,0:T(8,128)(2,1)S(1)} %get-tuple-element.388), channel_id=1, source_target_pairs={{0,16},{1,17},{2,18},{3,19},{4,20},{5,21},{6,22},{7,23},{8,24},{9,... | collective-permute-start | bytes 393224 | tf_op jit(solution)/shard_map/while/body/eval_jaxpr/ppermute | solution.py:16
  107.2 3.7 %collective-permute-done = bf16[512,128]{1,0:T(8,128)(2,1)S(1)} collective-permute-done((bf16[512,128]{1,0:T(8,128)(2,1)S(1)}, bf16[512,128]{1,0:T(8,128)(2,1)S(1)}, u32[]{:S(2)}, u32[]{:S(2)}) %collective-permute-start) | collective-permute-done | bytes 131104 | tf_op jit(solution)/shard_map/while/body/eval_jaxpr/ppermute | solution.py:16
  111.6 0.9 fusion.215
  114.6 2.0 collective-permute-start
  116.5 2.1 collective-permute-start.1
  118.6 4.0 %collective-permute-done = bf16[512,128]{1,0:T(8,128)(2,1)S(1)} collective-permute-done((bf16[512,128]{1,0:T(8,128)(2,1)S(1)}, bf16[512,128]{1,0:T(8,128)(2,1)S(1)}, u32[]{:S(2)}, u32[]{:S(2)}) %collective-permute-start) | collective-permute-done | bytes 131104 | tf_op jit(solution)/shard_map/while/body/eval_jaxpr/ppermute | solution.py:16
  123.3 0.9 fusion.215
  126.3 2.0 collective-permute-start
  128.3 2.9 %collective-permute-start.1 = (bf16[512,128]{1,0:T(8,128)(2,1)S(1)}, bf16[512,128]{1,0:T(8,128)(2,1)S(1)}, u32[]{:S(2)}, u32[]{:S(2)}) collective-permute-start(bf16[512,128]{1,0:T(8,128)(2,1)S(1)} %get-tuple-element.388), channel_id=1, source_target_pairs={{0,16},{1,17},{2,18},{3,19},{4,20},{5,21},{6,22},{7,23},{8,24},{9,... | collective-permute-start | bytes 393224 | tf_op jit(solution)/shard_map/while/body/eval_jaxpr/ppermute | solution.py:16
  131.2 3.3 %collective-permute-done = bf16[512,128]{1,0:T(8,128)(2,1)S(1)} collective-permute-done((bf16[512,128]{1,0:T(8,128)(2,1)S(1)}, bf16[512,128]{1,0:T(8,128)(2,1)S(1)}, u32[]{:S(2)}, u32[]{:S(2)}) %collective-permute-start) | collective-permute-done | bytes 131104 | tf_op jit(solution)/shard_map/while/body/eval_jaxpr/ppermute | solution.py:16
  135.1 0.9 fusion.215
  136.1 1.2 collective-permute-done.1
  139.0 2.2 collective-permute-start
  141.2 2.8 %collective-permute-start.1 = (bf16[512,128]{1,0:T(8,128)(2,1)S(1)}, bf16[512,128]{1,0:T(8,128)(2,1)S(1)}, u32[]{:S(2)}, u32[]{:S(2)}) collective-permute-start(bf16[512,128]{1,0:T(8,128)(2,1)S(1)} %get-tuple-element.388), channel_id=1, source_target_pairs={{0,16},{1,17},{2,18},{3,19},{4,20},{5,21},{6,22},{7,23},{8,24},{9,... | collective-permute-start | bytes 393224 | tf_op jit(solution)/shard_map/while/body/eval_jaxpr/ppermute | solution.py:16
  144.1 3.5 %collective-permute-done = bf16[512,128]{1,0:T(8,128)(2,1)S(1)} collective-permute-done((bf16[512,128]{1,0:T(8,128)(2,1)S(1)}, bf16[512,128]{1,0:T(8,128)(2,1)S(1)}, u32[]{:S(2)}, u32[]{:S(2)}) %collective-permute-start) | collective-permute-done | bytes 131104 | tf_op jit(solution)/shard_map/while/body/eval_jaxpr/ppermute | solution.py:16
  148.1 0.9 fusion.215
  149.1 1.6 collective-permute-done.1
  152.3 2.0 collective-permute-start
  154.3 3.4 %collective-permute-start.1 = (bf16[512,128]{1,0:T(8,128)(2,1)S(1)}, bf16[512,128]{1,0:T(8,128)(2,1)S(1)}, u32[]{:S(2)}, u32[]{:S(2)}) collective-permute-start(bf16[512,128]{1,0:T(8,128)(2,1)S(1)} %get-tuple-element.388), channel_id=1, source_target_pairs={{0,16},{1,17},{2,18},{3,19},{4,20},{5,21},{6,22},{7,23},{8,24},{9,... | collective-permute-start | bytes 393224 | tf_op jit(solution)/shard_map/while/body/eval_jaxpr/ppermute | solution.py:16
  157.8 4.1 %collective-permute-done = bf16[512,128]{1,0:T(8,128)(2,1)S(1)} collective-permute-done((bf16[512,128]{1,0:T(8,128)(2,1)S(1)}, bf16[512,128]{1,0:T(8,128)(2,1)S(1)}, u32[]{:S(2)}, u32[]{:S(2)}) %collective-permute-start) | collective-permute-done | bytes 131104 | tf_op jit(solution)/shard_map/while/body/eval_jaxpr/ppermute | solution.py:16
  162.5 0.9 fusion.215
  163.4 0.7 collective-permute-done.1
  165.8 2.0 collective-permute-start
  167.8 3.0 %collective-permute-start.1 = (bf16[512,128]{1,0:T(8,128)(2,1)S(1)}, bf16[512,128]{1,0:T(8,128)(2,1)S(1)}, u32[]{:S(2)}, u32[]{:S(2)}) collective-permute-start(bf16[512,128]{1,0:T(8,128)(2,1)S(1)} %get-tuple-element.388), channel_id=1, source_target_pairs={{0,16},{1,17},{2,18},{3,19},{4,20},{5,21},{6,22},{7,23},{8,24},{9,... | collective-permute-start | bytes 393224 | tf_op jit(solution)/shard_map/while/body/eval_jaxpr/ppermute | solution.py:16
  170.8 3.1 %collective-permute-done = bf16[512,128]{1,0:T(8,128)(2,1)S(1)} collective-permute-done((bf16[512,128]{1,0:T(8,128)(2,1)S(1)}, bf16[512,128]{1,0:T(8,128)(2,1)S(1)}, u32[]{:S(2)}, u32[]{:S(2)}) %collective-permute-start) | collective-permute-done | bytes 131104 | tf_op jit(solution)/shard_map/while/body/eval_jaxpr/ppermute | solution.py:16
  174.6 0.9 fusion.215
  177.9 3.4 %add_convert_fusion = bf16[1,1,512,128]{3,2,1,0:T(8,128)(2,1)} fusion(bf16[4,1,512,128]{3,2,1,0:T(8,128)(2,1)S(1)} %divide_convert_fusion, f32[]{:T(128)} %bitcast.89, f32[]{:T(128)} %bitcast.88, f32[]{:T(128)} %bitcast.87, f32[]{:T(128)} %bitcast.37), kind=kLoop, calls=%fused_computation.143 | loop fusion | flops 786432 | bytes 655376 | tf_op jit(solution)/shard_map/convert_element_type | solution.py:229
  181.3 11.1 %all-to-all-start.1 = ((bf16[128,4,128]{2,1,0:T(4,128)(2,1)}), bf16[128,4,128]{2,1,0:T(4,128)(2,1)S(1)}, u32[]{:S(2)}, u32[]{:S(2)}) async-start(bf16[128,4,128]{2,1,0:T(4,128)(2,1)} %bitcast.90), calls=%async_computation.1 | async-start | bytes 262144 | tf_op jit(solution)/shard_map/all_to_all | solution.py:228
  192.8 1.5 dynamic-slice_reduce_fusion
  194.4 12.7 %all-to-all-done.1 = bf16[128,4,128]{2,1,0:T(4,128)(2,1)S(1)} async-done(((bf16[128,4,128]{2,1,0:T(4,128)(2,1)}), bf16[128,4,128]{2,1,0:T(4,128)(2,1)S(1)}, u32[]{:S(2)}, u32[]{:S(2)}) %all-to-all-start.1) | async-done | bytes 131104 | tf_op jit(solution)/shard_map/all_to_all | solution.py:228
  207.4 3.7 %all_to_all.20 = f32[2,1,2048]{2,1,0:T(1,128)S(1)} all-to-all(f32[2,1,2048]{2,1,0:T(1,128)S(1)} %reshape.756), channel_id=1, replica_groups=mesh['groups'=2,'branch'=2,'tok'=128] {'branch'}, dimensions={0} | all-to-all | bytes 32768 | tf_op jit(solution)/shard_map/all_to_all | solution.py:36
  212.4 0.7 copy-done.8
  214.0 2.7 %collective-permute-start.2 = (bf16[2,64,16]{1,2,0:T(8,128)(2,1)S(1)}, bf16[2,64,16]{1,2,0:T(8,128)(2,1)S(1)}, u32[]{:S(2)}, u32[]{:S(2)}) collective-permute-start(bf16[2,64,16]{1,2,0:T(8,128)(2,1)S(1)} %copy.100), channel_id=1, source_target_pairs={{0,1},{1,2},{2,3},{3,4},{4,5},{5,6},{6,7},{7,8},{8,9},{9,10},{10,1... | collective-permute-start | bytes 12296 | tf_op jit(solution)/shard_map/ppermute | solution.py:48
  216.7 1.3 collective-permute-start.3
  218.0 4.2 %collective-permute-done.3 = bf16[2,64,16]{1,2,0:T(8,128)(2,1)S(1)} collective-permute-done((bf16[2,64,16]{1,2,0:T(8,128)(2,1)S(1)}, bf16[2,64,16]{1,2,0:T(8,128)(2,1)S(1)}, u32[]{:S(2)}, u32[]{:S(2)}) %collective-permute-start.3) | collective-permute-done | bytes 4128 | tf_op jit(solution)/shard_map/ppermute | solution.py:51
  (225 shorter events, 32.1 us)
Async XLA Ops:
  0.6 60.2 %copy-start = (bf16[32,2,4096]{2,1,0:T(2,128)(2,1)S(1)}, bf16[32,2,4096]{2,1,0:T(2,128)(2,1)}, u32[]{:S(2)}) copy-start(bf16[32,2,4096]{2,1,0:T(2,128)(2,1)} %param.21) | copy-start | bytes 1572868
  0.7 1.2 copy-start.2
  2.6 1.0 copy-start.3
  5.2 54.9 %copy-start.9 = (f32[4]{0:T(128)S(1)}, f32[4]{0:T(128)}, u32[]{:S(2)}) copy-start(f32[4]{0:T(128)} %param.22) | copy-start | bytes 52
  5.2 81.4 %all-to-all-start = ((bf16[128,4,384]{2,1,0:T(4,128)(2,1)}), bf16[128,4,384]{2,1,0:T(4,128)(2,1)S(1)}, u32[]{:S(2)}, u32[]{:S(2)}) async-start(bf16[128,4,384]{2,1,0:T(4,128)(2,1)} %copy.90), calls=%async_computation | async-start | bytes 786432 | tf_op jit(solution)/shard_map/all_to_all | solution.py:27
  60.1 0.7 copy-start.12
  60.8 1.0 copy-start.4
  60.8 0.9 copy-start.11
  90.2 8.1 %collective-permute-start = (bf16[512,128]{1,0:T(8,128)(2,1)S(1)}, bf16[512,128]{1,0:T(8,128)(2,1)S(1)}, u32[]{:S(2)}, u32[]{:S(2)}) collective-permute-start(bf16[512,128]{1,0:T(8,128)(2,1)S(1)} %get-tuple-element.387), channel_id=1, source_target_pairs={{0,16},{1,17},{2,18},{3,19},{4,20},{5,21},{6,22},{7,23},{8,24},{9,... | collective-permute-start | bytes 393224 | tf_op jit(solution)/shard_map/while/body/eval_jaxpr/ppermute | solution.py:16
  93.0 8.1 %collective-permute-start.1 = (bf16[512,128]{1,0:T(8,128)(2,1)S(1)}, bf16[512,128]{1,0:T(8,128)(2,1)S(1)}, u32[]{:S(2)}, u32[]{:S(2)}) collective-permute-start(bf16[512,128]{1,0:T(8,128)(2,1)S(1)} %get-tuple-element.388), channel_id=1, source_target_pairs={{0,16},{1,17},{2,18},{3,19},{4,20},{5,21},{6,22},{7,23},{8,24},{9,... | collective-permute-start | bytes 393224 | tf_op jit(solution)/shard_map/while/body/eval_jaxpr/ppermute | solution.py:16
  102.8 8.1 %collective-permute-start = (bf16[512,128]{1,0:T(8,128)(2,1)S(1)}, bf16[512,128]{1,0:T(8,128)(2,1)S(1)}, u32[]{:S(2)}, u32[]{:S(2)}) collective-permute-start(bf16[512,128]{1,0:T(8,128)(2,1)S(1)} %get-tuple-element.387), channel_id=1, source_target_pairs={{0,16},{1,17},{2,18},{3,19},{4,20},{5,21},{6,22},{7,23},{8,24},{9,... | collective-permute-start | bytes 393224 | tf_op jit(solution)/shard_map/while/body/eval_jaxpr/ppermute | solution.py:16
  104.8 8.1 %collective-permute-start.1 = (bf16[512,128]{1,0:T(8,128)(2,1)S(1)}, bf16[512,128]{1,0:T(8,128)(2,1)S(1)}, u32[]{:S(2)}, u32[]{:S(2)}) collective-permute-start(bf16[512,128]{1,0:T(8,128)(2,1)S(1)} %get-tuple-element.388), channel_id=1, source_target_pairs={{0,16},{1,17},{2,18},{3,19},{4,20},{5,21},{6,22},{7,23},{8,24},{9,... | collective-permute-start | bytes 393224 | tf_op jit(solution)/shard_map/while/body/eval_jaxpr/ppermute | solution.py:16
  114.6 8.1 %collective-permute-start = (bf16[512,128]{1,0:T(8,128)(2,1)S(1)}, bf16[512,128]{1,0:T(8,128)(2,1)S(1)}, u32[]{:S(2)}, u32[]{:S(2)}) collective-permute-start(bf16[512,128]{1,0:T(8,128)(2,1)S(1)} %get-tuple-element.387), channel_id=1, source_target_pairs={{0,16},{1,17},{2,18},{3,19},{4,20},{5,21},{6,22},{7,23},{8,24},{9,... | collective-permute-start | bytes 393224 | tf_op jit(solution)/shard_map/while/body/eval_jaxpr/ppermute | solution.py:16
  116.5 8.1 %collective-permute-start.1 = (bf16[512,128]{1,0:T(8,128)(2,1)S(1)}, bf16[512,128]{1,0:T(8,128)(2,1)S(1)}, u32[]{:S(2)}, u32[]{:S(2)}) collective-permute-start(bf16[512,128]{1,0:T(8,128)(2,1)S(1)} %get-tuple-element.388), channel_id=1, source_target_pairs={{0,16},{1,17},{2,18},{3,19},{4,20},{5,21},{6,22},{7,23},{8,24},{9,... | collective-permute-start | bytes 393224 | tf_op jit(solution)/shard_map/while/body/eval_jaxpr/ppermute | solution.py:16
  126.3 8.2 %collective-permute-start = (bf16[512,128]{1,0:T(8,128)(2,1)S(1)}, bf16[512,128]{1,0:T(8,128)(2,1)S(1)}, u32[]{:S(2)}, u32[]{:S(2)}) collective-permute-start(bf16[512,128]{1,0:T(8,128)(2,1)S(1)} %get-tuple-element.387), channel_id=1, source_target_pairs={{0,16},{1,17},{2,18},{3,19},{4,20},{5,21},{6,22},{7,23},{8,24},{9,... | collective-permute-start | bytes 393224 | tf_op jit(solution)/shard_map/while/body/eval_jaxpr/ppermute | solution.py:16
  128.3 9.1 %collective-permute-start.1 = (bf16[512,128]{1,0:T(8,128)(2,1)S(1)}, bf16[512,128]{1,0:T(8,128)(2,1)S(1)}, u32[]{:S(2)}, u32[]{:S(2)}) collective-permute-start(bf16[512,128]{1,0:T(8,128)(2,1)S(1)} %get-tuple-element.388), channel_id=1, source_target_pairs={{0,16},{1,17},{2,18},{3,19},{4,20},{5,21},{6,22},{7,23},{8,24},{9,... | collective-permute-start | bytes 393224 | tf_op jit(solution)/shard_map/while/body/eval_jaxpr/ppermute | solution.py:16
  139.0 8.5 %collective-permute-start = (bf16[512,128]{1,0:T(8,128)(2,1)S(1)}, bf16[512,128]{1,0:T(8,128)(2,1)S(1)}, u32[]{:S(2)}, u32[]{:S(2)}) collective-permute-start(bf16[512,128]{1,0:T(8,128)(2,1)S(1)} %get-tuple-element.387), channel_id=1, source_target_pairs={{0,16},{1,17},{2,18},{3,19},{4,20},{5,21},{6,22},{7,23},{8,24},{9,... | collective-permute-start | bytes 393224 | tf_op jit(solution)/shard_map/while/body/eval_jaxpr/ppermute | solution.py:16
  141.2 9.5 %collective-permute-start.1 = (bf16[512,128]{1,0:T(8,128)(2,1)S(1)}, bf16[512,128]{1,0:T(8,128)(2,1)S(1)}, u32[]{:S(2)}, u32[]{:S(2)}) collective-permute-start(bf16[512,128]{1,0:T(8,128)(2,1)S(1)} %get-tuple-element.388), channel_id=1, source_target_pairs={{0,16},{1,17},{2,18},{3,19},{4,20},{5,21},{6,22},{7,23},{8,24},{9,... | collective-permute-start | bytes 393224 | tf_op jit(solution)/shard_map/while/body/eval_jaxpr/ppermute | solution.py:16
  152.3 9.5 %collective-permute-start = (bf16[512,128]{1,0:T(8,128)(2,1)S(1)}, bf16[512,128]{1,0:T(8,128)(2,1)S(1)}, u32[]{:S(2)}, u32[]{:S(2)}) collective-permute-start(bf16[512,128]{1,0:T(8,128)(2,1)S(1)} %get-tuple-element.387), channel_id=1, source_target_pairs={{0,16},{1,17},{2,18},{3,19},{4,20},{5,21},{6,22},{7,23},{8,24},{9,... | collective-permute-start | bytes 393224 | tf_op jit(solution)/shard_map/while/body/eval_jaxpr/ppermute | solution.py:16
  154.3 9.8 %collective-permute-start.1 = (bf16[512,128]{1,0:T(8,128)(2,1)S(1)}, bf16[512,128]{1,0:T(8,128)(2,1)S(1)}, u32[]{:S(2)}, u32[]{:S(2)}) collective-permute-start(bf16[512,128]{1,0:T(8,128)(2,1)S(1)} %get-tuple-element.388), channel_id=1, source_target_pairs={{0,16},{1,17},{2,18},{3,19},{4,20},{5,21},{6,22},{7,23},{8,24},{9,... | collective-permute-start | bytes 393224 | tf_op jit(solution)/shard_map/while/body/eval_jaxpr/ppermute | solution.py:16
  165.8 8.1 %collective-permute-start = (bf16[512,128]{1,0:T(8,128)(2,1)S(1)}, bf16[512,128]{1,0:T(8,128)(2,1)S(1)}, u32[]{:S(2)}, u32[]{:S(2)}) collective-permute-start(bf16[512,128]{1,0:T(8,128)(2,1)S(1)} %get-tuple-element.387), channel_id=1, source_target_pairs={{0,16},{1,17},{2,18},{3,19},{4,20},{5,21},{6,22},{7,23},{8,24},{9,... | collective-permute-start | bytes 393224 | tf_op jit(solution)/shard_map/while/body/eval_jaxpr/ppermute | solution.py:16
  167.8 8.1 %collective-permute-start.1 = (bf16[512,128]{1,0:T(8,128)(2,1)S(1)}, bf16[512,128]{1,0:T(8,128)(2,1)S(1)}, u32[]{:S(2)}, u32[]{:S(2)}) collective-permute-start(bf16[512,128]{1,0:T(8,128)(2,1)S(1)} %get-tuple-element.388), channel_id=1, source_target_pairs={{0,16},{1,17},{2,18},{3,19},{4,20},{5,21},{6,22},{7,23},{8,24},{9,... | collective-permute-start | bytes 393224 | tf_op jit(solution)/shard_map/while/body/eval_jaxpr/ppermute | solution.py:16
  177.9 14.5 %copy-start.1 = (bf16[4096,64]{0,1:T(8,128)(2,1)S(1)}, bf16[4096,64]{0,1:T(8,128)(2,1)}, u32[]{:S(2)}) copy-start(bf16[4096,64]{0,1:T(8,128)(2,1)} %param.23) | copy-start | bytes 1572868
  181.3 25.7 %all-to-all-start.1 = ((bf16[128,4,128]{2,1,0:T(4,128)(2,1)}), bf16[128,4,128]{2,1,0:T(4,128)(2,1)S(1)}, u32[]{:S(2)}, u32[]{:S(2)}) async-start(bf16[128,4,128]{2,1,0:T(4,128)(2,1)} %bitcast.90), calls=%async_computation.1 | async-start | bytes 262144 | tf_op jit(solution)/shard_map/all_to_all | solution.py:228
  212.4 0.7 copy-start.8
  213.2 0.6 copy-start.6
  213.2 9.2 %copy-start.5 = (bf16[3,3,16,384]{3,2,1,0:T(8,128)(2,1)S(1)}, bf16[3,3,16,384]{3,2,1,0:T(8,128)(2,1)}, u32[]{:S(2)}) copy-start(bf16[3,3,16,384]{3,2,1,0:T(8,128)(2,1)} %param.25) | copy-start | bytes 331780
  214.0 4.0 %collective-permute-start.2 = (bf16[2,64,16]{1,2,0:T(8,128)(2,1)S(1)}, bf16[2,64,16]{1,2,0:T(8,128)(2,1)S(1)}, u32[]{:S(2)}, u32[]{:S(2)}) collective-permute-start(bf16[2,64,16]{1,2,0:T(8,128)(2,1)S(1)} %copy.100), channel_id=1, source_target_pairs={{0,1},{1,2},{2,3},{3,4},{4,5},{5,6},{6,7},{7,8},{8,9},{9,10},{10,1... | collective-permute-start | bytes 12296 | tf_op jit(solution)/shard_map/ppermute | solution.py:48
  216.7 5.6 %collective-permute-start.3 = (bf16[2,64,16]{1,2,0:T(8,128)(2,1)S(1)}, bf16[2,64,16]{1,2,0:T(8,128)(2,1)S(1)}, u32[]{:S(2)}, u32[]{:S(2)}) collective-permute-start(bf16[2,64,16]{1,2,0:T(8,128)(2,1)S(1)} %copy.100), channel_id=1, source_target_pairs={{1,0},{2,1},{3,2},{4,3},{5,4},{6,5},{7,6},{8,7},{9,8},{10,9},{11,1... | collective-permute-start | bytes 12296 | tf_op jit(solution)/shard_map/ppermute | solution.py:51
  225.1 0.7 copy-start.10
  225.8 0.7 copy-start.7
where the time goes:
time: 230 us; the launch traced here: 229 us
  starting transfers between devices  104 us (45%)
  waiting for transfers between devices  71.5 us (31%)
  matrix products  21.1 us (9%)
  other arithmetic  14.1 us (6%)
  local copies, waits for them, and re-layouts  11.8 us (5%)
  blocking collectives  3.74 us (2%)
    all_to_all x1, starting transfers between devices, in_one_piece(): lax.all_to_all(both, axis, split_axis=split_dim, concat_axis=concat_dim,...  54.9 us
    ppermute x14, starting transfers between devices, passed_along(): return lax.ppermute(value, axis, pairs)  34.2 us
    ppermute x14, waiting for transfers between devices, passed_along(): return lax.ppermute(value, axis, pairs)  30.2 us
    all_to_all x1, waiting for transfers between devices, in_one_piece(): lax.all_to_all(both, axis, split_axis=split_dim, concat_axis=concat_dim,...  24.4 us
    all_to_all x1, waiting for transfers between devices, shards(): lax.all_to_all(partial_value.astype(jnp.bfloat16), 'tok', split_axis=0, c...  12.7 us
    all_to_all x1, starting transfers between devices, shards(): lax.all_to_all(partial_value.astype(jnp.bfloat16), 'tok', split_axis=0, c...  11.1 us
    dot_general x32, matrix products, visit(): jnp.einsum('hqk,khd->hqd', raised.astype(jnp.bfloat16), shifted, preferre...  10.8 us
    reduce_sum x8, other arithmetic, visit(): totals.append(total[which] * shrink + jnp.sum(raised, axis=-1))  7.43 us
  transfers between devices with their start and end apart: 18, of which 17 were waited for; matrix products, arithmetic and copies ran while one was open for 6% of the time, Pallas kernels for 0%

commit v1 on v0

v1 whole, which is shorter than its diff:
```python
import functools
import math

import jax
import jax.numpy as jnp
from jax import lax
from jax.experimental import pallas as pl
from jax.experimental.pallas import tpu as pltpu
from jax.sharding import Mesh
from jax.sharding import PartitionSpec as P

HEAD_DIM = 128

step_size = 0.25
norm_eps = 1e-06
TO_EXP2 = HEAD_DIM ** (-0.5) / math.log(2.0)
BF = jnp.bfloat16
F32 = jnp.float32


def dot(a, b, dims, **kw):
    return lax.dot_general(a, b, (dims, ((), ())), preferred_element_type=F32, **kw)


def pack_kernel(core_ref, q_ref, k_ref, v_ref, w_ref, out_ref):
    sets, _, hd = out_ref.shape
    rows = q_ref.shape[0]
    half = rows // 2
    for z in range(sets):
        cols = slice(z * hd, (z + 1) * hd)
        out_ref[z, 0:rows, :] = q_ref[:, cols]
        out_ref[z, rows : 2 * rows, :] = k_ref[:, cols]
        projected = dot(v_ref[:, cols], w_ref[cols, :], ((1,), (0,))).astype(BF)
        out_ref[z, 2 * rows :, :] = jnp.concatenate([projected[:half], projected[half:]], axis=1)


def pack(core, queries, keys, values, out_weight, sets):
    rows = queries.shape[0]
    cols = sets * HEAD_DIM
    outs = out_weight.shape[1]
    block = pl.BlockSpec((rows, cols), lambda i, c: (0, c[0]))
    return pl.pallas_call(
        pack_kernel,
        grid_spec=pltpu.PrefetchScalarGridSpec(
            num_scalar_prefetch=1,
            grid=(1,),
            in_specs=[block, block, block, pl.BlockSpec((cols, outs), lambda i, c: (c[0], 0))],
            out_specs=pl.BlockSpec((sets, 2 * rows + rows // 2, HEAD_DIM), lambda i, c: (0, 0, 0)),
        ),
        out_shape=jax.ShapeDtypeStruct((sets, 2 * rows + rows // 2, HEAD_DIM), BF),
        name="pack",
    )(core[None], queries, keys, values, out_weight)


def terms_kernel(kb_ref, ms_ref, head_ref, key_ref, mouse_ref, w_ref, bias_ref, term_ref):
    frames = term_ref.shape[0] // 2
    rows_key = jnp.concatenate([key_ref[pl.ds(kb_ref[j], 1)] for j in range(frames)], axis=0)
    rows_mouse = jnp.concatenate([mouse_ref[pl.ds(ms_ref[j], 1)] for j in range(frames)], axis=0)
    rows_key = rows_key.astype(F32)
    rows_mouse = rows_mouse.astype(F32)
    bias_key, bias_mouse = rows_key[:, 0, :], rows_mouse[:, 0, :]
    bias = [bias_key + bias_mouse, bias_mouse, bias_key, jnp.zeros_like(bias_key)]
    bias_ref[...] = jnp.concatenate(bias, axis=0).astype(BF)
    terms = jnp.concatenate([rows_key[:, 1, :], rows_mouse[:, 1, :]], axis=0).astype(BF)
    term_ref[...] = dot(terms, w_ref[...], ((1,), (0,)))


def action_terms(head, kb, ms, key_table, mouse_table, out_weight):
    frames = kb.shape[0]
    outs = out_weight.shape[1]
    return pl.pallas_call(
        terms_kernel,
        grid_spec=pltpu.PrefetchScalarGridSpec(
            num_scalar_prefetch=3,
            grid=(1,),
            in_specs=[
                pl.BlockSpec(key_table.shape[:2] + (HEAD_DIM,), lambda i, a, b, h: (0, 0, h[0])),
                pl.BlockSpec(mouse_table.shape[:2] + (HEAD_DIM,), lambda i, a, b, h: (0, 0, h[0])),
                pl.BlockSpec((HEAD_DIM, outs), lambda i, a, b, h: (h[0], 0)),
            ],
            out_specs=[
                pl.BlockSpec((4 * frames, HEAD_DIM), lambda i, a, b, h: (0, 0)),
                pl.BlockSpec((2 * frames, outs), lambda i, a, b, h: (0, 0)),
            ],
        ),
        out_shape=[
            jax.ShapeDtypeStruct((4 * frames, HEAD_DIM), BF),
            jax.ShapeDtypeStruct((2 * frames, outs), F32),
        ],
        name="terms",
    )(kb, ms, head[None], key_table, mouse_table, out_weight)


def frame_kernel(rows, at, own_ref, *refs):
    kv_refs, (sum_ref, stat_ref) = refs[:-2], refs[-2:]
    sets, _, hd = own_ref.shape
    half = rows // 2
    outs = sum_ref.shape[0]
    query = own_ref[:, 0:rows, :].reshape(sets * rows, hd)

    def gathered(first, last):
        parts = [r[:, first:last, :].reshape(-1, hd) for r in kv_refs]
        return parts[0] if len(parts) == 1 else jnp.concatenate(parts, axis=0)

    key_low = gathered(at, at + half)
    key_high = gathered(at + half, at + rows)
    both = gathered(at + rows, at + rows + half)
    score_low = dot(key_low, query, ((1,), (1,)))
    score_high = dot(key_high, query, ((1,), (1,)))
    top = jnp.maximum(
        jnp.max(score_low, axis=0, keepdims=True), jnp.max(score_high, axis=0, keepdims=True)
    )
    raised_low = jnp.exp2((score_low - top) * TO_EXP2)
    raised_high = jnp.exp2((score_high - top) * TO_EXP2)
    total = jnp.sum(raised_low, axis=0, keepdims=True) + jnp.sum(raised_high, axis=0, keepdims=True)
    summed = dot(both[:, :outs], raised_low.astype(BF), ((0,), (0,)))
    summed = summed + dot(both[:, outs:], raised_high.astype(BF), ((0,), (0,)))
    sum_ref[...] = summed
    stat_ref[0:1, :] = top
    stat_ref[1:2, :] = total


def frame_attention(own, pieces, rows, at, outs):
    tokens = own.shape[0] * rows
    flops = 2 * tokens * tokens * (HEAD_DIM + outs)
    return pl.pallas_call(
        functools.partial(frame_kernel, rows, at),
        out_shape=[
            jax.ShapeDtypeStruct((outs, tokens), F32),
            jax.ShapeDtypeStruct((2, tokens), F32),
        ],
        cost_estimate=pl.CostEstimate(
            flops=flops, transcendentals=tokens * tokens, bytes_accessed=1 << 20
        ),
        name="frame",
    )(own, *pieces)


def guide_kernel(rows, count, guide_ref, own_ref, bias_ref, term_ref, *refs):
    sum_refs, stat_refs, out_ref = refs[:count], refs[count : 2 * count], refs[-1]
    sets, _, hd = own_ref.shape
    half = rows // 2
    query = own_ref[:, 0:rows, :].reshape(sets * rows, hd)
    shift = dot(bias_ref[...], query, ((1,), (1,)))
    tops = jnp.concatenate([r[0:1, :] for r in stat_refs], axis=0)
    totals = jnp.concatenate([r[1:2, :] for r in stat_refs], axis=0)
    parts = []
    for b in range(4):
        height = (tops + shift[b * count : (b + 1) * count]) * TO_EXP2
        factor = jnp.exp2(height - jnp.max(height, axis=0, keepdims=True))
        total = jnp.sum(factor * totals, axis=0, keepdims=True)
        parts.append(factor * (guide_ref[b] / total))
    mix = (parts[0] + parts[1]) + (parts[2] + parts[3])
    loads = jnp.concatenate(
        [(parts[0] + parts[2]) * totals, (parts[0] + parts[1]) * totals], axis=0
    )
    result = dot(term_ref[...], loads, ((0,), (0,)), precision=lax.Precision.HIGHEST)
    for j in range(count):
        result = result + mix[j : j + 1, :] * sum_refs[j][...]
    by_token = jnp.transpose(result).reshape(sets, rows, -1)
    out_ref[...] = jnp.concatenate([by_token[:, :half], by_token[:, half:]], axis=2).astype(BF)


def guide(guidance, own, bias, term, sums, stats, rows, outs):
    sets = own.shape[0]
    count = len(sums)
    vmem = pl.BlockSpec(memory_space=pltpu.VMEM)
    return pl.pallas_call(
        functools.partial(guide_kernel, rows, count),
        in_specs=[pl.BlockSpec(memory_space=pltpu.SMEM)] + [vmem] * (3 + 2 * count),
        out_specs=vmem,
        out_shape=jax.ShapeDtypeStruct((sets, rows // 2, 2 * outs), BF),
        name="guide",
    )(guidance, own, bias, term, *sums, *stats)


def ring(count, steps):
    return [(i, (i + steps) % count) for i in range(count)]


def clear_rows(array, depth, top_edge, bottom_edge):
    height = array.shape[0]
    place = jnp.arange(height, dtype=jnp.int32)
    drop = (place < depth) & top_edge | (place >= height - depth) & bottom_edge
    return jnp.where(drop[:, None, None], jnp.zeros_like(array), array)


def convolve(array, weight):
    rows = array.shape[0] - 2
    cols = array.shape[1]
    padded = jnp.pad(array, ((0, 0), (1, 1), (0, 0)))
    total = jnp.zeros((rows, cols, weight.shape[-1]), F32)
    for first in range(3):
        for second in range(3):
            window = padded[first : first + rows, second : second + cols, :]
            total = total + jnp.einsum(
                "rci,io->rco", window, weight[first, second], preferred_element_type=F32
            )
    return total


def normalize(features, gain):
    scaled = (
        features
        * lax.rsqrt(jnp.mean(features * features, axis=-1, keepdims=True) + norm_eps)
        * gain
    )
    return jax.nn.silu(scaled).astype(BF)


def shards(
    queries,
    keys,
    values,
    keyboard,
    mouse,
    key_table,
    mouse_table,
    guidance,
    out_weight,
    latent,
    conv_in,
    gain,
    conv_out,
):
    rounds = lax.axis_size("x")
    sets = lax.axis_size("z")
    x = lax.axis_index("x")
    z = lax.axis_index("z")
    core = lax.axis_index("branch")
    rows = queries.shape[0]
    outs = out_weight.shape[1]
    frames = keyboard.shape[0]
    assert frames == rounds and rounds % 2 == 0

    packed = pack(core, queries, keys, values, out_weight, sets)
    own = lax.all_to_all(packed, "z", 0, 0, tiled=True)

    offsets = [0]
    for step in range(1, rounds // 2):
        offsets += [-step, step]
    offsets.append(rounds // 2)
    order = (x + jnp.array(offsets, dtype=jnp.int32)) % rounds
    bias, term = action_terms(
        core * sets + z, keyboard[order], mouse[order], key_table, mouse_table, out_weight
    )

    moving = own[:, rows:, :]
    results = [frame_attention(own, [own], rows, rows, outs)]
    low = high = moving
    for step in range(1, rounds // 2):
        low = lax.ppermute(low, "x", ring(rounds, 1))
        high = lax.ppermute(high, "x", ring(rounds, -1))
        results.append(frame_attention(own, [low], rows, 0, outs))
        results.append(frame_attention(own, [high], rows, 0, outs))
    cut = sets // 2
    low = lax.ppermute(low[:cut], "x", ring(rounds, 1))
    high = lax.ppermute(high[cut:], "x", ring(rounds, -1))
    results.append(frame_attention(own, [low, high], rows, 0, outs))
    sums, stats = zip(*results)
    part = guide(guidance, own, bias, term, sums, stats, rows, outs)
    returned = lax.all_to_all(part, "z", 0, 0, tiled=True)
    mine = jnp.sum(returned.astype(F32), axis=0)
    other = lax.ppermute(mine, "branch", [(0, 1), (1, 0)])
    both = mine + other
    velocity = jnp.concatenate([both[:, :outs], both[:, outs:]], axis=0)

    stepped = (latent - step_size * velocity).astype(BF)
    half = rows // 2
    flat = jnp.concatenate([stepped[:half], stepped[half:]], axis=1)
    count = rounds * sets
    index = x * sets + z
    forward = [(i, i + 1) for i in range(count - 1)]
    backward = [(i + 1, i) for i in range(count - 1)]
    before = lax.ppermute(flat, ("x", "z"), forward)
    after = lax.ppermute(flat, ("x", "z"), backward)

    def as_grid(block):
        block = jnp.concatenate([block[:, :outs], block[:, outs:]], axis=0)
        return block.reshape(rows, 2, 2, -1).transpose(1, 0, 2, 3).reshape(2, 2 * rows, -1)

    top_edge = index == 0
    bottom_edge = index == count - 1
    widened = jnp.concatenate([as_grid(before), as_grid(flat), as_grid(after)], axis=0)
    widened = clear_rows(widened, 2, top_edge, bottom_edge)
    hidden = normalize(convolve(widened, conv_in), gain)
    hidden = clear_rows(hidden, 1, top_edge, bottom_edge)
    colours = convolve(hidden, conv_out)
    return (velocity, colours.transpose(2, 0, 1))


def solution(mesh):
    cores = mesh.shape["branch"]
    tok = mesh.shape["tok"]

    def run(*arrays):
        sets = min(arrays[0].shape[1] // (HEAD_DIM * cores), tok)
        fine = Mesh(
            mesh.devices.reshape(mesh.shape["groups"], cores, tok // sets, sets),
            ("groups", "branch", "x", "z"),
        )
        tokens = P(("groups", "x", "z"), None)
        placed = (
            tokens,
            tokens,
            tokens,
            P("groups"),
            P("groups"),
            P(),
            P(),
            P(),
            P(),
            tokens,
            P(),
            P(),
            P(),
        )
        return jax.shard_map(
            shards,
            mesh=fine,
            in_specs=placed,
            out_specs=(tokens, P(None, ("groups", "x", "z"), None)),
            check_vma=False,
        )(*arrays)

    return run
```

time: 230 us -> 176 us (0.77)
  the two profiles are of different devices: /device:TPU:80 before, /device:TPU:72 now
where the time goes in v1:
time: 176 us; the launch traced here: 175 us
  blocking collectives  64.5 us (37%)
  starting transfers between devices  41.1 us (23%)
  waiting for transfers between devices  27.5 us (16%)
  Pallas kernels  26.1 us (15%)
  local copies, waits for them, and re-layouts  9.82 us (6%)
  matrix products  4.18 us (2%)
    all_to_all x1, blocking collectives, shards(): own = lax.all_to_all(packed, 'z', 0, 0, tiled=True)  64.5 us
    pallas_call x8, Pallas kernels, frame_attention(): pl.pallas_call(functools.partial(frame_kernel, rows, at), out_shape=[jax....  18.9 us
    all_to_all x1, waiting for transfers between devices, shards(): returned = lax.all_to_all(part, 'z', 0, 0, tiled=True)  12.6 us
    ppermute x3, starting transfers between devices, shards(): high = lax.ppermute(high, 'x', ring(rounds, -1))  11.4 us
    ppermute x3, starting transfers between devices, shards(): low = lax.ppermute(low, 'x', ring(rounds, 1))  7.7 us
    ppermute x1, waiting for transfers between devices, shards(): before = lax.ppermute(flat, ('x', 'z'), forward)  6.75 us
    ppermute x3, waiting for transfers between devices, shards(): high = lax.ppermute(high, 'x', ring(rounds, -1))  6.69 us
    unnamed x34, local copies, waits for them, and re-layouts  6.69 us
  transfers between devices with their start and end apart: 12, of which 7 were waited for; matrix products, arithmetic and copies ran while one was open for 2% of the time, Pallas kernels for 11%

profile of v1, /device:TPU:72, one launch (start us, length us, event | category | flops | bytes accessed | tf_op | source)
XLA Modules:
  0.0 175.3 jit_solution(17194021649552639064)
XLA Ops:
  0.7 2.4 %copy.33.w_ref = bf16[4096,64]{1,0:T(8,128)(2,1)} copy(bf16[4096,64]{0,1:T(8,128)(2,1)} %param.22) | data formatting | bytes 1048576 | tf_op args[8]
  3.0 2.3 %pack.1 = bf16[16,80,128]{2,1,0:T(8,128)(2,1)} custom-call(s32[1]{0:T(128)} %bitcast.core_ref, bf16[32,4096]{1,0:T(8,128)(2,1)} %q_ref.1, bf16[32,4096]{1,0:T(8,128)(2,1)} %k_ref.1, bf16[32,4096]{1,0:T(8,128)(2,1)} %v_ref.1, bf16[4096,64]{1,0:T(8,128)(2,1)} %copy.33.w_ref), custom_call_target="tpu_custom_call" | custom-call | tf_op jit(solution)/shard_map/pack/pallas_call | solution.py:42
  5.3 64.5 %all_to_all.10.own_ref.refs_0_ = bf16[16,80,128]{2,1,0:T(8,128)(2,1)S(1)} all-to-all(bf16[16,80,128]{2,1,0:T(8,128)(2,1)} %pack.1), channel_id=1, replica_groups=mesh['groups'=2,'branch'=2,'x'=8,'z'=16] {'z'}, dimensions={0} | all-to-all | bytes 655360 | tf_op jit(solution)/shard_map/all_to_all | solution.py:237
  69.8 2.3 %collective-permute-start.1 = (bf16[16,48,128]{2,1,0:T(8,128)(2,1)S(1)}, bf16[16,48,128]{2,1,0:T(8,128)(2,1)S(1)}, u32[]{:S(2)}, u32[]{:S(2)}) collective-permute-start(bf16[16,48,128]{2,1,0:T(8,128)(2,1)S(1)} %slice.199), channel_id=1, source_target_pairs={{0,112},{16,0},{32,16},{48,32},{64,48},{80,64},{96,80},{112,96},{1... | collective-permute-start | bytes 589832 | tf_op jit(solution)/shard_map/ppermute | solution.py:253
  72.1 3.6 %collective-permute-start = (bf16[16,48,128]{2,1,0:T(8,128)(2,1)S(1)}, bf16[16,48,128]{2,1,0:T(8,128)(2,1)S(1)}, u32[]{:S(2)}, u32[]{:S(2)}) collective-permute-start(bf16[16,48,128]{2,1,0:T(8,128)(2,1)S(1)} %slice.199), channel_id=1, source_target_pairs={{0,16},{16,32},{32,48},{48,64},{64,80},{80,96},{96,112},{112,0},{1... | collective-permute-start | bytes 589832 | tf_op jit(solution)/shard_map/ppermute | solution.py:252
  75.7 3.2 %collective-permute-done.1.refs_0_ = bf16[16,48,128]{2,1,0:T(8,128)(2,1)S(1)} collective-permute-done((bf16[16,48,128]{2,1,0:T(8,128)(2,1)S(1)}, bf16[16,48,128]{2,1,0:T(8,128)(2,1)S(1)}, u32[]{:S(2)}, u32[]{:S(2)}) %collective-permute-start.1) | collective-permute-done | bytes 196640 | tf_op jit(solution)/shard_map/ppermute | solution.py:253
  78.9 3.5 %collective-permute-start.3 = (bf16[16,48,128]{2,1,0:T(8,128)(2,1)S(1)}, bf16[16,48,128]{2,1,0:T(8,128)(2,1)S(1)}, u32[]{:S(2)}, u32[]{:S(2)}) collective-permute-start(bf16[16,48,128]{2,1,0:T(8,128)(2,1)S(1)} %collective-permute-done.1.refs_0_), channel_id=1, source_target_pairs={{0,112},{16,0},{32,16},{48,32},{64,48},{80,64},{96,80},{112,96},{1... | collective-permute-start | bytes 589832 | tf_op jit(solution)/shard_map/ppermute | solution.py:253
  82.7 2.2 %collective-permute-start.2 = (bf16[16,48,128]{2,1,0:T(8,128)(2,1)S(1)}, bf16[16,48,128]{2,1,0:T(8,128)(2,1)S(1)}, u32[]{:S(2)}, u32[]{:S(2)}) collective-permute-start(bf16[16,48,128]{2,1,0:T(8,128)(2,1)S(1)} %collective-permute-done.refs_0_), channel_id=1, source_target_pairs={{0,16},{16,32},{32,48},{48,64},{64,80},{80,96},{96,112},{112,0},{1... | collective-permute-start | bytes 589832 | tf_op jit(solution)/shard_map/ppermute | solution.py:252
  84.9 2.3 %collective-permute-done.3.refs_0_ = bf16[16,48,128]{2,1,0:T(8,128)(2,1)S(1)} collective-permute-done((bf16[16,48,128]{2,1,0:T(8,128)(2,1)S(1)}, bf16[16,48,128]{2,1,0:T(8,128)(2,1)S(1)}, u32[]{:S(2)}, u32[]{:S(2)}) %collective-permute-start.3) | collective-permute-done | bytes 196640 | tf_op jit(solution)/shard_map/ppermute | solution.py:253
  87.2 5.6 %collective-permute-start.5 = (bf16[16,48,128]{2,1,0:T(8,128)(2,1)S(1)}, bf16[16,48,128]{2,1,0:T(8,128)(2,1)S(1)}, u32[]{:S(2)}, u32[]{:S(2)}) collective-permute-start(bf16[16,48,128]{2,1,0:T(8,128)(2,1)S(1)} %collective-permute-done.3.refs_0_), channel_id=1, source_target_pairs={{0,112},{16,0},{32,16},{48,32},{64,48},{80,64},{96,80},{112,96},{1... | collective-permute-start | bytes 589832 | tf_op jit(solution)/shard_map/ppermute | solution.py:253
  92.8 2.0 %collective-permute-start.4 = (bf16[16,48,128]{2,1,0:T(8,128)(2,1)S(1)}, bf16[16,48,128]{2,1,0:T(8,128)(2,1)S(1)}, u32[]{:S(2)}, u32[]{:S(2)}) collective-permute-start(bf16[16,48,128]{2,1,0:T(8,128)(2,1)S(1)} %collective-permute-done.2.refs_0_), channel_id=1, source_target_pairs={{0,16},{16,32},{32,48},{48,64},{64,80},{80,96},{96,112},{112,0},{1... | collective-permute-start | bytes 589832 | tf_op jit(solution)/shard_map/ppermute | solution.py:252
  94.8 1.2 collective-permute-done.5.refs_0_
  96.0 5.6 %collective-permute-start.7 = (bf16[8,48,128]{2,1,0:T(8,128)(2,1)S(1)}, bf16[8,48,128]{2,1,0:T(8,128)(2,1)S(1)}, u32[]{:S(2)}, u32[]{:S(2)}) collective-permute-start(bf16[8,48,128]{2,1,0:T(8,128)(2,1)S(1)} %slice.201), channel_id=1, source_target_pairs={{0,112},{16,0},{32,16},{48,32},{64,48},{80,64},{96,80},{112,96},{1... | collective-permute-start | bytes 294920 | tf_op jit(solution)/shard_map/ppermute | solution.py:258
  101.7 2.0 %collective-permute-start.6 = (bf16[8,48,128]{2,1,0:T(8,128)(2,1)S(1)}, bf16[8,48,128]{2,1,0:T(8,128)(2,1)S(1)}, u32[]{:S(2)}, u32[]{:S(2)}) collective-permute-start(bf16[8,48,128]{2,1,0:T(8,128)(2,1)S(1)} %slice.200), channel_id=1, source_target_pairs={{0,16},{16,32},{32,48},{48,64},{64,80},{80,96},{96,112},{112,0},{1... | collective-permute-start | bytes 294920 | tf_op jit(solution)/shard_map/ppermute | solution.py:257
  103.7 1.1 gather_fusion.1
  104.8 1.2 gather_fusion
  106.0 2.2 %terms.1 = (bf16[32,128]{1,0:T(8,128)(2,1)}, f32[16,64]{1,0:T(8,128)}) custom-call(s32[8]{0:T(128)} %gather_fusion, s32[8]{0:T(128)} %gather_fusion.1, s32[1]{0:T(128)} %bitcast.1.head_ref, bf16[16,2,4096]{2,1,0:T(2,128)(2,1)} %key_ref.1, bf16[32,2,4096]{2,1,0:T(2,128)(2,1)} %mouse_ref.1, bf16[4096,64]{1,0:T(8,128)(2,1)} %copy.33.w_ref), custom_call_target="tpu_custom_call" | custom-call | tf_op jit(solution)/shard_map/terms/pallas_call | solution.py:71
  108.2 2.4 %frame.8 = (f32[64,512]{1,0:T(8,128)}, f32[2,512]{1,0:T(2,128)}) custom-call(bf16[16,80,128]{2,1,0:T(8,128)(2,1)} %copy-done.2, bf16[16,80,128]{2,1,0:T(8,128)(2,1)} %copy-done.2), custom_call_target="tpu_custom_call" | custom-call | flops 100663296 | bytes 1048576 | tf_op jit(solution)/shard_map/frame/pallas_call | solution.py:126
  110.6 2.4 %frame.10 = (f32[64,512]{1,0:T(8,128)}, f32[2,512]{1,0:T(2,128)}) custom-call(bf16[16,80,128]{2,1,0:T(8,128)(2,1)} %copy-done.2, bf16[16,48,128]{2,1,0:T(8,128)(2,1)} %copy-done.5), custom_call_target="tpu_custom_call" | custom-call | flops 100663296 | bytes 1048576 | tf_op jit(solution)/shard_map/frame/pallas_call | solution.py:126
  112.9 2.4 %frame.9 = (f32[64,512]{1,0:T(8,128)}, f32[2,512]{1,0:T(2,128)}) custom-call(bf16[16,80,128]{2,1,0:T(8,128)(2,1)} %copy-done.2, bf16[16,48,128]{2,1,0:T(8,128)(2,1)} %copy-done.6), custom_call_target="tpu_custom_call" | custom-call | flops 100663296 | bytes 1048576 | tf_op jit(solution)/shard_map/frame/pallas_call | solution.py:126
  115.3 2.4 %frame.12 = (f32[64,512]{1,0:T(8,128)}, f32[2,512]{1,0:T(2,128)}) custom-call(bf16[16,80,128]{2,1,0:T(8,128)(2,1)} %copy-done.2, bf16[16,48,128]{2,1,0:T(8,128)(2,1)} %copy-done.7), custom_call_target="tpu_custom_call" | custom-call | flops 100663296 | bytes 1048576 | tf_op jit(solution)/shard_map/frame/pallas_call | solution.py:126
  117.6 2.4 %frame.11 = (f32[64,512]{1,0:T(8,128)}, f32[2,512]{1,0:T(2,128)}) custom-call(bf16[16,80,128]{2,1,0:T(8,128)(2,1)} %copy-done.2, bf16[16,48,128]{2,1,0:T(8,128)(2,1)} %copy-done.8), custom_call_target="tpu_custom_call" | custom-call | flops 100663296 | bytes 1048576 | tf_op jit(solution)/shard_map/frame/pallas_call | solution.py:126
  120.0 2.4 %frame.14 = (f32[64,512]{1,0:T(8,128)}, f32[2,512]{1,0:T(2,128)}) custom-call(bf16[16,80,128]{2,1,0:T(8,128)(2,1)} %copy-done.2, bf16[16,48,128]{2,1,0:T(8,128)(2,1)} %copy-done.3), custom_call_target="tpu_custom_call" | custom-call | flops 100663296 | bytes 1048576 | tf_op jit(solution)/shard_map/frame/pallas_call | solution.py:126
  122.3 2.4 %frame.13 = (f32[64,512]{1,0:T(8,128)}, f32[2,512]{1,0:T(2,128)}) custom-call(bf16[16,80,128]{2,1,0:T(8,128)(2,1)} %copy-done.2, bf16[16,48,128]{2,1,0:T(8,128)(2,1)} %copy-done.4), custom_call_target="tpu_custom_call" | custom-call | flops 100663296 | bytes 1048576 | tf_op jit(solution)/shard_map/frame/pallas_call | solution.py:126
  124.7 0.6 copy-done.10
  125.4 0.6 copy-done.11
  126.0 2.4 %frame.15 = (f32[64,512]{1,0:T(8,128)}, f32[2,512]{1,0:T(2,128)}) custom-call(bf16[16,80,128]{2,1,0:T(8,128)(2,1)} %copy-done.2, bf16[8,48,128]{2,1,0:T(8,128)(2,1)} %copy-done.11, bf16[8,48,128]{2,1,0:T(8,128)(2,1)} %copy-done.10), custom_call_target="tpu_custom_call" | custom-call | flops 100663296 | bytes 1048576 | tf_op jit(solution)/shard_map/frame/pallas_call | solution.py:126
  128.4 2.7 %guide.1 = bf16[16,16,128]{2,1,0:T(8,128)(2,1)} custom-call(f32[4]{0:T(128)} %guide_ref.1, bf16[16,80,128]{2,1,0:T(8,128)(2,1)} %copy-done.2, bf16[32,128]{1,0:T(8,128)(2,1)} %get-tuple-element.20.bias_ref, f32[16,64]{1,0:T(8,128)} %get-tuple-element.21.term_ref, f32[64,512]{1,0:T(8,128)} %get-tuple-element.22.refs_0_, f32[64,512]{1,0:T(8,128)} %get-tuple-element.23.refs_1_, ...), custom_call_target="tpu_custom_call" | custom-call | tf_op jit(solution)/shard_map/guide/pallas_call | solution.py:168
  131.1 4.5 %all-to-all-start.1 = ((bf16[16,16,128]{2,1,0:T(8,128)(2,1)}), bf16[16,16,128]{2,1,0:T(8,128)(2,1)S(1)}, u32[]{:S(2)}, u32[]{:S(2)}) async-start(bf16[16,16,128]{2,1,0:T(8,128)(2,1)} %guide.1), calls=%async_computation.1 | async-start | bytes 131072 | tf_op jit(solution)/shard_map/all_to_all | solution.py:262
  135.6 12.6 %all-to-all-done.1 = bf16[16,16,128]{2,1,0:T(8,128)(2,1)S(1)} async-done(((bf16[16,16,128]{2,1,0:T(8,128)(2,1)}), bf16[16,16,128]{2,1,0:T(8,128)(2,1)S(1)}, u32[]{:S(2)}, u32[]{:S(2)}) %all-to-all-start.1) | async-done | bytes 65568 | tf_op jit(solution)/shard_map/all_to_all | solution.py:262
  148.2 2.0 %collective-permute-start.8 = (f32[16,128]{1,0:T(8,128)S(1)}, f32[16,128]{1,0:T(8,128)S(1)}, u32[]{:S(2)}, u32[]{:S(2)}) collective-permute-start(f32[16,128]{1,0:T(8,128)S(1)} %convert_reduce_fusion), channel_id=1, source_target_pairs={{0,128},{128,0},{1,129},{129,1},{2,130},{130,2},{3,131},{131,3},{4... | collective-permute-start | bytes 24584 | tf_op jit(solution)/shard_map/ppermute | solution.py:264
  150.2 1.1 collective-permute-done.8
  151.4 0.6 copy-done.13
  152.0 0.6 subtract_convert_fusion
  152.9 6.0 %collective-permute-start.10 = (bf16[16,128]{0,1:T(8,128)(2,1)S(1)}, bf16[16,128]{0,1:T(8,128)(2,1)S(1)}, u32[]{:S(2)}, u32[]{:S(2)}) collective-permute-start(bf16[16,128]{0,1:T(8,128)(2,1)S(1)} %copy.35), channel_id=1, source_target_pairs={{1,0},{2,1},{3,2},{4,3},{5,4},{6,5},{7,6},{8,7},{9,8},{10,9},{11,1... | collective-permute-start | bytes 12296 | tf_op jit(solution)/shard_map/ppermute | solution.py:276
  159.0 1.9 %collective-permute-start.9 = (bf16[16,128]{0,1:T(8,128)(2,1)S(1)}, bf16[16,128]{0,1:T(8,128)(2,1)S(1)}, u32[]{:S(2)}, u32[]{:S(2)}) collective-permute-start(bf16[16,128]{0,1:T(8,128)(2,1)S(1)} %copy.35), channel_id=1, source_target_pairs={{0,1},{1,2},{2,3},{3,4},{4,5},{5,6},{6,7},{7,8},{8,9},{9,10},{10,1... | collective-permute-start | bytes 12296 | tf_op jit(solution)/shard_map/ppermute | solution.py:275
  161.4 6.7 %collective-permute-done.9 = bf16[16,128]{0,1:T(8,128)(2,1)S(1)} collective-permute-done((bf16[16,128]{0,1:T(8,128)(2,1)S(1)}, bf16[16,128]{0,1:T(8,128)(2,1)S(1)}, u32[]{:S(2)}, u32[]{:S(2)}) %collective-permute-start.9) | collective-permute-done | bytes 4128 | tf_op jit(solution)/shard_map/ppermute | solution.py:275
  168.5 0.6 copy-done.9
  169.1 0.3 fusion.22
  169.4 0.3 fusion.19
  169.7 0.3 fusion.16
  170.0 0.3 fusion.24
  170.6 0.3 convolution_add_fusion.4
  171.1 0.3 convolution_add_fusion.3
  171.5 0.3 multiply_reduce_fusion
  171.8 0.7 copy-done.14
  172.7 0.5 copy-done.12
  174.7 0.6 copy.44
  (70 shorter events, 3.8 us)
Async XLA Ops:
  0.6 103.0 %copy-start = (s32[8]{0:T(128)S(1)}, s32[8]{0:T(128)}, u32[]{:S(2)}) copy-start(s32[8]{0:T(128)} %param.18) | copy-start | bytes 100
  69.8 31.9 %copy-start.2 = (bf16[16,80,128]{2,1,0:T(8,128)(2,1)}, bf16[16,80,128]{2,1,0:T(8,128)(2,1)S(1)}, u32[]{:S(2)}) copy-start(bf16[16,80,128]{2,1,0:T(8,128)(2,1)S(1)} %all_to_all.10.own_ref.refs_0_) | copy-start | bytes 983044
  69.8 9.1 %collective-permute-start.1 = (bf16[16,48,128]{2,1,0:T(8,128)(2,1)S(1)}, bf16[16,48,128]{2,1,0:T(8,128)(2,1)S(1)}, u32[]{:S(2)}, u32[]{:S(2)}) collective-permute-start(bf16[16,48,128]{2,1,0:T(8,128)(2,1)S(1)} %slice.199), channel_id=1, source_target_pairs={{0,112},{16,0},{32,16},{48,32},{64,48},{80,64},{96,80},{112,96},{1... | collective-permute-start | bytes 589832 | tf_op jit(solution)/shard_map/ppermute | solution.py:253
  72.1 10.5 %collective-permute-start = (bf16[16,48,128]{2,1,0:T(8,128)(2,1)S(1)}, bf16[16,48,128]{2,1,0:T(8,128)(2,1)S(1)}, u32[]{:S(2)}, u32[]{:S(2)}) collective-permute-start(bf16[16,48,128]{2,1,0:T(8,128)(2,1)S(1)} %slice.199), channel_id=1, source_target_pairs={{0,16},{16,32},{32,48},{48,64},{64,80},{80,96},{96,112},{112,0},{1... | collective-permute-start | bytes 589832 | tf_op jit(solution)/shard_map/ppermute | solution.py:252
  78.9 22.7 %copy-start.5 = (bf16[16,48,128]{2,1,0:T(8,128)(2,1)}, bf16[16,48,128]{2,1,0:T(8,128)(2,1)S(1)}, u32[]{:S(2)}) copy-start(bf16[16,48,128]{2,1,0:T(8,128)(2,1)S(1)} %collective-permute-done.1.refs_0_) | copy-start | bytes 589828
  78.9 8.3 %collective-permute-start.3 = (bf16[16,48,128]{2,1,0:T(8,128)(2,1)S(1)}, bf16[16,48,128]{2,1,0:T(8,128)(2,1)S(1)}, u32[]{:S(2)}, u32[]{:S(2)}) collective-permute-start(bf16[16,48,128]{2,1,0:T(8,128)(2,1)S(1)} %collective-permute-done.1.refs_0_), channel_id=1, source_target_pairs={{0,112},{16,0},{32,16},{48,32},{64,48},{80,64},{96,80},{112,96},{1... | collective-permute-start | bytes 589832 | tf_op jit(solution)/shard_map/ppermute | solution.py:253
  82.6 23.3 %copy-start.6 = (bf16[16,48,128]{2,1,0:T(8,128)(2,1)}, bf16[16,48,128]{2,1,0:T(8,128)(2,1)S(1)}, u32[]{:S(2)}) copy-start(bf16[16,48,128]{2,1,0:T(8,128)(2,1)S(1)} %collective-permute-done.refs_0_) | copy-start | bytes 589828
  82.7 10.1 %collective-permute-start.2 = (bf16[16,48,128]{2,1,0:T(8,128)(2,1)S(1)}, bf16[16,48,128]{2,1,0:T(8,128)(2,1)S(1)}, u32[]{:S(2)}, u32[]{:S(2)}) collective-permute-start(bf16[16,48,128]{2,1,0:T(8,128)(2,1)S(1)} %collective-permute-done.refs_0_), channel_id=1, source_target_pairs={{0,16},{16,32},{32,48},{48,64},{64,80},{80,96},{96,112},{112,0},{1... | collective-permute-start | bytes 589832 | tf_op jit(solution)/shard_map/ppermute | solution.py:252
  84.9 9.9 %copy-start.15 = (s32[8]{0:T(128)S(1)}, s32[8]{0:T(128)}, u32[]{:S(2)}) copy-start(s32[8]{0:T(128)} %constant.62.clone) | copy-start | bytes 100
  87.2 18.8 %copy-start.7 = (bf16[16,48,128]{2,1,0:T(8,128)(2,1)}, bf16[16,48,128]{2,1,0:T(8,128)(2,1)S(1)}, u32[]{:S(2)}) copy-start(bf16[16,48,128]{2,1,0:T(8,128)(2,1)S(1)} %collective-permute-done.3.refs_0_) | copy-start | bytes 589828
  87.2 8.8 %collective-permute-start.5 = (bf16[16,48,128]{2,1,0:T(8,128)(2,1)S(1)}, bf16[16,48,128]{2,1,0:T(8,128)(2,1)S(1)}, u32[]{:S(2)}, u32[]{:S(2)}) collective-permute-start(bf16[16,48,128]{2,1,0:T(8,128)(2,1)S(1)} %collective-permute-done.3.refs_0_), channel_id=1, source_target_pairs={{0,112},{16,0},{32,16},{48,32},{64,48},{80,64},{96,80},{112,96},{1... | collective-permute-start | bytes 589832 | tf_op jit(solution)/shard_map/ppermute | solution.py:253
  92.8 13.2 %copy-start.8 = (bf16[16,48,128]{2,1,0:T(8,128)(2,1)}, bf16[16,48,128]{2,1,0:T(8,128)(2,1)S(1)}, u32[]{:S(2)}) copy-start(bf16[16,48,128]{2,1,0:T(8,128)(2,1)S(1)} %collective-permute-done.2.refs_0_) | copy-start | bytes 589828
  92.8 8.8 %collective-permute-start.4 = (bf16[16,48,128]{2,1,0:T(8,128)(2,1)S(1)}, bf16[16,48,128]{2,1,0:T(8,128)(2,1)S(1)}, u32[]{:S(2)}, u32[]{:S(2)}) collective-permute-start(bf16[16,48,128]{2,1,0:T(8,128)(2,1)S(1)} %collective-permute-done.2.refs_0_), channel_id=1, source_target_pairs={{0,16},{16,32},{32,48},{48,64},{64,80},{80,96},{96,112},{112,0},{1... | collective-permute-start | bytes 589832 | tf_op jit(solution)/shard_map/ppermute | solution.py:252
  95.9 5.7 %copy-start.3 = (bf16[16,48,128]{2,1,0:T(8,128)(2,1)}, bf16[16,48,128]{2,1,0:T(8,128)(2,1)S(1)}, u32[]{:S(2)}) copy-start(bf16[16,48,128]{2,1,0:T(8,128)(2,1)S(1)} %collective-permute-done.5.refs_0_) | copy-start | bytes 589828
  96.0 28.8 %collective-permute-start.7 = (bf16[8,48,128]{2,1,0:T(8,128)(2,1)S(1)}, bf16[8,48,128]{2,1,0:T(8,128)(2,1)S(1)}, u32[]{:S(2)}, u32[]{:S(2)}) collective-permute-start(bf16[8,48,128]{2,1,0:T(8,128)(2,1)S(1)} %slice.201), channel_id=1, source_target_pairs={{0,112},{16,0},{32,16},{48,32},{64,48},{80,64},{96,80},{112,96},{1... | collective-permute-start | bytes 294920 | tf_op jit(solution)/shard_map/ppermute | solution.py:258
  101.6 3.2 %copy-start.4 = (bf16[16,48,128]{2,1,0:T(8,128)(2,1)}, bf16[16,48,128]{2,1,0:T(8,128)(2,1)S(1)}, u32[]{:S(2)}) copy-start(bf16[16,48,128]{2,1,0:T(8,128)(2,1)S(1)} %collective-permute-done.4.refs_0_) | copy-start | bytes 589828
  101.7 23.0 %collective-permute-start.6 = (bf16[8,48,128]{2,1,0:T(8,128)(2,1)S(1)}, bf16[8,48,128]{2,1,0:T(8,128)(2,1)S(1)}, u32[]{:S(2)}, u32[]{:S(2)}) collective-permute-start(bf16[8,48,128]{2,1,0:T(8,128)(2,1)S(1)} %slice.200), channel_id=1, source_target_pairs={{0,16},{16,32},{32,48},{48,64},{64,80},{80,96},{96,112},{112,0},{1... | collective-permute-start | bytes 294920 | tf_op jit(solution)/shard_map/ppermute | solution.py:257
  103.7 1.1 copy-start.1
  124.7 0.7 copy-start.10
  125.4 0.6 copy-start.11
  131.1 17.1 %all-to-all-start.1 = ((bf16[16,16,128]{2,1,0:T(8,128)(2,1)}), bf16[16,16,128]{2,1,0:T(8,128)(2,1)S(1)}, u32[]{:S(2)}, u32[]{:S(2)}) async-start(bf16[16,16,128]{2,1,0:T(8,128)(2,1)} %guide.1), calls=%async_computation.1 | async-start | bytes 131072 | tf_op jit(solution)/shard_map/all_to_all | solution.py:262
  148.2 3.1 %collective-permute-start.8 = (f32[16,128]{1,0:T(8,128)S(1)}, f32[16,128]{1,0:T(8,128)S(1)}, u32[]{:S(2)}, u32[]{:S(2)}) collective-permute-start(f32[16,128]{1,0:T(8,128)S(1)} %convert_reduce_fusion), channel_id=1, source_target_pairs={{0,128},{128,0},{1,129},{129,1},{2,130},{130,2},{3,131},{131,3},{4... | collective-permute-start | bytes 24584 | tf_op jit(solution)/shard_map/ppermute | solution.py:264
  151.3 0.7 copy-start.13
  152.9 8.3 %collective-permute-start.10 = (bf16[16,128]{0,1:T(8,128)(2,1)S(1)}, bf16[16,128]{0,1:T(8,128)(2,1)S(1)}, u32[]{:S(2)}, u32[]{:S(2)}) collective-permute-start(bf16[16,128]{0,1:T(8,128)(2,1)S(1)} %copy.35), channel_id=1, source_target_pairs={{1,0},{2,1},{3,2},{4,3},{5,4},{6,5},{7,6},{8,7},{9,8},{10,9},{11,1... | collective-permute-start | bytes 12296 | tf_op jit(solution)/shard_map/ppermute | solution.py:276
  159.0 9.2 %collective-permute-start.9 = (bf16[16,128]{0,1:T(8,128)(2,1)S(1)}, bf16[16,128]{0,1:T(8,128)(2,1)S(1)}, u32[]{:S(2)}, u32[]{:S(2)}) collective-permute-start(bf16[16,128]{0,1:T(8,128)(2,1)S(1)} %copy.35), channel_id=1, source_target_pairs={{0,1},{1,2},{2,3},{3,4},{4,5},{5,6},{6,7},{7,8},{8,9},{9,10},{10,1... | collective-permute-start | bytes 12296 | tf_op jit(solution)/shard_map/ppermute | solution.py:275
  168.2 0.9 copy-start.9
  171.8 0.7 copy-start.14
  172.5 0.7 copy-start.12

commit v2 on v1

v2 whole, which is shorter than its diff:
```python
import functools
import math

import jax
import jax.numpy as jnp
from jax import lax
from jax.experimental import pallas as pl
from jax.experimental.pallas import tpu as pltpu
from jax.sharding import Mesh
from jax.sharding import PartitionSpec as P

HEAD_DIM = 128

step_size = 0.25
norm_eps = 1e-06
TO_EXP2 = HEAD_DIM ** (-0.5) / math.log(2.0)
BF = jnp.bfloat16
F32 = jnp.float32
VMEM = pl.BlockSpec(memory_space=pltpu.VMEM)
SMEM = pl.BlockSpec(memory_space=pltpu.SMEM)


def dot(a, b, dims, **kw):
    return lax.dot_general(a, b, (dims, ((), ())), preferred_element_type=F32, **kw)


def pack_kernel(core_ref, q_ref, k_ref, v_ref, w_ref, out_ref):
    sets, _, hd = out_ref.shape
    rows = q_ref.shape[0]
    half = rows // 2
    for z in range(sets):
        cols = slice(z * hd, (z + 1) * hd)
        out_ref[z, 0:rows, :] = q_ref[:, cols]
        out_ref[z, rows : 2 * rows, :] = k_ref[:, cols]
        projected = dot(v_ref[:, cols], w_ref[:, cols], ((1,), (1,))).astype(BF)
        out_ref[z, 2 * rows :, :] = jnp.concatenate([projected[:half], projected[half:]], axis=1)


def pack(core, queries, keys, values, weight_t, sets):
    rows = queries.shape[0]
    cols = sets * HEAD_DIM
    outs = weight_t.shape[0]
    block = pl.BlockSpec((rows, cols), lambda i, c: (0, c[0]))
    return pl.pallas_call(
        pack_kernel,
        grid_spec=pltpu.PrefetchScalarGridSpec(
            num_scalar_prefetch=1,
            grid=(1,),
            in_specs=[block, block, block, pl.BlockSpec((outs, cols), lambda i, c: (0, c[0]))],
            out_specs=VMEM,
        ),
        out_shape=jax.ShapeDtypeStruct((sets, 2 * rows + rows // 2, HEAD_DIM), BF),
        name="pack",
    )(core[None], queries, keys, values, weight_t)


def terms_kernel(offsets, kb_ref, ms_ref, x_ref, head_ref, key_ref, mouse_ref, w_ref, bias_ref, term_ref):
    frames = len(offsets)
    places = [lax.rem(x_ref[0] + (frames + offset), frames) for offset in offsets]
    rows_key = jnp.concatenate([key_ref[pl.ds(kb_ref[at], 1)] for at in places], axis=0)
    rows_mouse = jnp.concatenate([mouse_ref[pl.ds(ms_ref[at], 1)] for at in places], axis=0)
    rows_key = rows_key.astype(F32)
    rows_mouse = rows_mouse.astype(F32)
    bias_key, bias_mouse = rows_key[:, 0, :], rows_mouse[:, 0, :]
    bias = [bias_key + bias_mouse, bias_mouse, bias_key, jnp.zeros_like(bias_key)]
    bias_ref[...] = jnp.concatenate(bias, axis=0).astype(BF)
    terms = jnp.concatenate([rows_key[:, 1, :], rows_mouse[:, 1, :]], axis=0).astype(BF)
    term_ref[...] = dot(terms, w_ref[...], ((1,), (1,)))


def action_terms(offsets, x, head, keyboard, mouse, key_table, mouse_table, weight_t):
    frames = len(offsets)
    outs = weight_t.shape[0]
    return pl.pallas_call(
        functools.partial(terms_kernel, offsets),
        grid_spec=pltpu.PrefetchScalarGridSpec(
            num_scalar_prefetch=4,
            grid=(1,),
            in_specs=[
                pl.BlockSpec(key_table.shape[:2] + (HEAD_DIM,), lambda i, a, b, x, h: (0, 0, h[0])),
                pl.BlockSpec(mouse_table.shape[:2] + (HEAD_DIM,), lambda i, a, b, x, h: (0, 0, h[0])),
                pl.BlockSpec((outs, HEAD_DIM), lambda i, a, b, x, h: (0, h[0])),
            ],
            out_specs=[VMEM, VMEM],
        ),
        out_shape=[
            jax.ShapeDtypeStruct((4 * frames, HEAD_DIM), BF),
            jax.ShapeDtypeStruct((2 * frames, outs), F32),
        ],
        name="terms",
    )(keyboard, mouse, x[None], head[None], key_table, mouse_table, weight_t)


def frame_kernel(rows, at, own_ref, *refs):
    kv_refs, (sum_ref, stat_ref) = refs[:-2], refs[-2:]
    sets, _, hd = own_ref.shape
    half = rows // 2
    outs = sum_ref.shape[0]
    query = own_ref[:, 0:rows, :].reshape(sets * rows, hd)

    def gathered(first, last):
        parts = [r[:, first:last, :].reshape(-1, hd) for r in kv_refs]
        return parts[0] if len(parts) == 1 else jnp.concatenate(parts, axis=0)

    key_low = gathered(at, at + half)
    key_high = gathered(at + half, at + rows)
    both = gathered(at + rows, at + rows + half)
    score_low = dot(key_low, query, ((1,), (1,)))
    score_high = dot(key_high, query, ((1,), (1,)))
    top = jnp.maximum(
        jnp.max(score_low, axis=0, keepdims=True), jnp.max(score_high, axis=0, keepdims=True)
    )
    raised_low = jnp.exp2((score_low - top) * TO_EXP2)
    raised_high = jnp.exp2((score_high - top) * TO_EXP2)
    total = jnp.sum(raised_low, axis=0, keepdims=True) + jnp.sum(raised_high, axis=0, keepdims=True)
    summed = dot(both[:, :outs], raised_low.astype(BF), ((0,), (0,)))
    summed = summed + dot(both[:, outs:], raised_high.astype(BF), ((0,), (0,)))
    sum_ref[...] = summed
    stat_ref[0:1, :] = top
    stat_ref[1:2, :] = total


def frame_attention(own, pieces, rows, at, outs):
    tokens = own.shape[0] * rows
    flops = 2 * tokens * tokens * (HEAD_DIM + outs)
    return pl.pallas_call(
        functools.partial(frame_kernel, rows, at),
        in_specs=[VMEM] * (1 + len(pieces)),
        out_specs=[VMEM, VMEM],
        out_shape=[
            jax.ShapeDtypeStruct((outs, tokens), F32),
            jax.ShapeDtypeStruct((2, tokens), F32),
        ],
        cost_estimate=pl.CostEstimate(
            flops=flops, transcendentals=tokens * tokens, bytes_accessed=1 << 20
        ),
        name="frame",
    )(own, *pieces)


def guide_kernel(rows, count, guide_ref, own_ref, bias_ref, term_ref, *refs):
    sum_refs, stat_refs, out_ref = refs[:count], refs[count : 2 * count], refs[-1]
    sets, _, hd = own_ref.shape
    half = rows // 2
    query = own_ref[:, 0:rows, :].reshape(sets * rows, hd)
    shift = dot(bias_ref[...], query, ((1,), (1,)))
    tops = jnp.concatenate([r[0:1, :] for r in stat_refs], axis=0)
    totals = jnp.concatenate([r[1:2, :] for r in stat_refs], axis=0)
    parts = []
    for b in range(4):
        height = (tops + shift[b * count : (b + 1) * count]) * TO_EXP2
        factor = jnp.exp2(height - jnp.max(height, axis=0, keepdims=True))
        total = jnp.sum(factor * totals, axis=0, keepdims=True)
        parts.append(factor * (guide_ref[b] / total))
    mix = (parts[0] + parts[1]) + (parts[2] + parts[3])
    loads = jnp.concatenate(
        [(parts[0] + parts[2]) * totals, (parts[0] + parts[1]) * totals], axis=0
    )
    result = dot(term_ref[...], loads, ((0,), (0,)), precision=lax.Precision.HIGHEST)
    for j in range(count):
        result = result + mix[j : j + 1, :] * sum_refs[j][...]
    by_token = jnp.transpose(result).reshape(sets, rows, -1)
    out_ref[...] = jnp.concatenate([by_token[:, :half], by_token[:, half:]], axis=2).astype(BF)


def guide(guidance, own, bias, term, sums, stats, rows, outs):
    sets = own.shape[0]
    count = len(sums)
    return pl.pallas_call(
        functools.partial(guide_kernel, rows, count),
        in_specs=[SMEM] + [VMEM] * (3 + 2 * count),
        out_specs=VMEM,
        out_shape=jax.ShapeDtypeStruct((sets, rows // 2, 2 * outs), BF),
        name="guide",
    )(guidance, own, bias, term, *sums, *stats)


def decode_kernel(index_ref, before_ref, mine_ref, after_ref, conv_in_ref, gain_ref, conv_out_ref, out_ref):
    outs = before_ref.shape[1] // 2
    lat = outs // 4
    tokens = before_ref.shape[0] * 2
    left, right = [], []
    for ref in (before_ref, mine_ref, after_ref):
        both = ref[...].astype(F32)
        block = jnp.concatenate([both[:, :outs], both[:, outs:]], axis=0)
        edge = jnp.zeros_like(block[:1])
        earlier = jnp.concatenate([edge, block[:-1]], axis=0)
        later = jnp.concatenate([block[1:], edge], axis=0)
        for dy in range(2):
            at = 2 * lat * dy
            here = block[:, at : at + 2 * lat]
            left.append(jnp.concatenate([earlier[:, at + lat : at + 2 * lat], here], axis=1))
            right.append(jnp.concatenate([here, later[:, at : at + lat]], axis=1))
    height = 4 * tokens
    row = lax.broadcasted_iota(jnp.int32, (height, 1), 0) // tokens
    first, last = index_ref[0] == 0, index_ref[0] == index_ref[1] - 1
    keep = jnp.where((row == 0) & first | (row == 3) & last, 0.0, 1.0)
    taps = []
    for windows in (left, right):
        stack = jnp.concatenate(windows, axis=0).astype(BF)
        features = dot(stack[:height], conv_in_ref[0], ((1,), (0,)))
        for a in range(1, 3):
            part = stack[a * tokens : a * tokens + height]
            features = features + dot(part, conv_in_ref[a], ((1,), (0,)))
        power = jnp.mean(features * features, axis=1, keepdims=True)
        scaled = features * lax.rsqrt(power + norm_eps) * gain_ref[...]
        normed = scaled / (1.0 + jnp.exp(-scaled)) * keep
        taps.append(dot(conv_out_ref[...], normed.astype(BF), ((1,), (1,))))
    even, odd = taps
    step = even.shape[0] // 3
    lane = lax.broadcasted_iota(jnp.int32, (step, height), 1) % tokens
    before = jnp.where(lane == 0, 0.0, pltpu.roll(odd[:step], 1, 1))
    after = jnp.where(lane == tokens - 1, 0.0, pltpu.roll(even[2 * step :], height - 1, 1))
    columns = [
        before + even[step : 2 * step] + odd[2 * step :],
        even[:step] + odd[step : 2 * step] + after,
    ]
    source = lax.broadcasted_iota(jnp.int32, (height, height), 0)
    target = lax.broadcasted_iota(jnp.int32, (height, height), 1)
    colours = None
    for dx, column in enumerate(columns):
        moved = column[0:3]
        for a in range(1, 3):
            moved = moved + pltpu.roll(column[3 * a : 3 * a + 3], height - a * tokens, 1)
        chosen = jnp.where(target == 2 * source + dx, 1.0, 0.0)
        placed = dot(moved, chosen, ((1,), (0,)), precision=lax.Precision.HIGHEST)
        colours = placed if colours is None else colours + placed
    out_ref[:, 0, :] = colours[:, : 2 * tokens]
    out_ref[:, 1, :] = colours[:, 2 * tokens :]


def decode(index, before, mine, after, conv_in, gain, conv_out):
    tokens = before.shape[0] * 2
    return pl.pallas_call(
        decode_kernel,
        in_specs=[SMEM] + [VMEM] * 6,
        out_specs=VMEM,
        out_shape=jax.ShapeDtypeStruct((3, 2, 2 * tokens), F32),
        name="decode",
    )(index, before, mine, after, conv_in, gain, conv_out)


def shifted(value, axis, count, steps):
    return lax.ppermute(value, axis, [(i, (i + steps) % count) for i in range(count)])


def shards(
    queries,
    keys,
    values,
    keyboard,
    mouse,
    key_table,
    mouse_table,
    guidance,
    out_weight,
    latent,
    conv_in,
    gain,
    conv_out,
):
    rounds = lax.axis_size("x")
    sets = lax.axis_size("z")
    x = lax.axis_index("x")
    z = lax.axis_index("z")
    core = lax.axis_index("branch")
    rows = queries.shape[0]
    outs = out_weight.shape[1]
    frames = keyboard.shape[0]
    assert frames == rounds and rounds % 4 == 0
    weight_t = out_weight.T
    packed = pack(core, queries, keys, values, weight_t, sets)
    own = lax.all_to_all(packed, "z", 0, 0, tiled=True)

    near = rounds // 4
    cut = sets // 2
    moving = own[:, rows:, :]
    low, high, offsets = {}, {}, [0]
    for step in range(1, near + 1):
        low[step] = shifted(moving, "x", rounds, step)
        high[step] = shifted(moving, "x", rounds, -step)
        offsets += [-step, step]
    for step in range(near + 1, 2 * near):
        offsets += [-step, step]
    offsets.append(2 * near)
    bias, term = action_terms(
        tuple(offsets), x, core * sets + z, keyboard, mouse, key_table, mouse_table, weight_t
    )

    def attention(*pieces):
        return frame_attention(own, pieces, rows, 0, outs)

    results = [frame_attention(own, [own], rows, rows, outs)]
    for step in range(1, near):
        results += [attention(low[step]), attention(high[step])]
    far_low, far_high, results, bias, term = lax.optimization_barrier(
        (low[near], high[near], results, bias, term)
    )
    for step in range(near + 1, 2 * near):
        low[step] = shifted(far_low, "x", rounds, step - near)
        high[step] = shifted(far_high, "x", rounds, near - step)
    half_low = shifted(far_low[:cut], "x", rounds, near)
    half_high = shifted(far_high[cut:], "x", rounds, -near)
    results += [attention(far_low), attention(far_high)]
    for step in range(near + 1, 2 * near):
        results += [attention(low[step]), attention(high[step])]
    results.append(attention(half_low, half_high))
    sums, stats = zip(*results)
    part = guide(guidance, own, bias, term, sums, stats, rows, outs)
    returned = lax.all_to_all(part, "z", 0, 0, tiled=True)
    mine = jnp.sum(returned.astype(F32), axis=0)
    other = lax.ppermute(mine, "branch", [(0, 1), (1, 0)])
    both = mine + other
    velocity = jnp.concatenate([both[:, :outs], both[:, outs:]], axis=0)

    half = rows // 2
    noisy = jnp.concatenate([latent[:half], latent[half:]], axis=1)
    stepped = (noisy - step_size * both).astype(BF)
    count = rounds * sets
    index = jnp.stack([x * sets + z, jnp.int32(count)])
    before = lax.ppermute(stepped, ("x", "z"), [(i, i + 1) for i in range(count - 1)])
    after = lax.ppermute(stepped, ("x", "z"), [(i + 1, i) for i in range(count - 1)])
    taps_in = conv_in.reshape(conv_in.shape[0], -1, conv_in.shape[3])
    taps_out = conv_out.transpose(1, 0, 3, 2).reshape(3, -1, conv_out.shape[2])
    taps_out = jnp.pad(taps_out, ((0, 0), (0, 16 - taps_out.shape[1]), (0, 0)))
    taps_out = taps_out.reshape(-1, conv_out.shape[2])
    colours = decode(index, before, stepped, after, taps_in, gain[None], taps_out)
    return (velocity, colours)


def solution(mesh):
    cores = mesh.shape["branch"]
    tok = mesh.shape["tok"]

    def run(*arrays):
        sets = min(arrays[0].shape[1] // (HEAD_DIM * cores), tok)
        fine = Mesh(
            mesh.devices.reshape(mesh.shape["groups"], cores, tok // sets, sets),
            ("groups", "branch", "x", "z"),
        )
        tokens = P(("groups", "x", "z"), None)
        placed = (
            tokens,
            tokens,
            tokens,
            P("groups"),
            P("groups"),
            P(),
            P(),
            P(),
            P(),
            tokens,
            P(),
            P(),
            P(),
        )
        return jax.shard_map(
            shards,
            mesh=fine,
            in_specs=placed,
            out_specs=(tokens, P(None, ("groups", "x", "z"), None)),
            check_vma=False,
        )(*arrays)

    return run
```

time: 176 us -> 165 us (0.938)
  the two profiles are of different devices: /device:TPU:72 before, /device:TPU:70 now
where the time goes in v2:
time: 165 us; the launch traced here: 164 us
  blocking collectives  64.5 us (39%)
  starting transfers between devices  43.9 us (27%)
  Pallas kernels  28.9 us (18%)
  waiting for transfers between devices  18.9 us (11%)
  local copies, waits for them, and re-layouts  5.94 us (4%)
    all_to_all x1, blocking collectives, shards(): own = lax.all_to_all(packed, 'z', 0, 0, tiled=True)  64.5 us
    ppermute x8, starting transfers between devices, shifted(): lax.ppermute(value, axis, [(i, (i + steps) % count) for i in range(count)])  28.7 us
    pallas_call x8, Pallas kernels, frame_attention(): pl.pallas_call(functools.partial(frame_kernel, rows, at), in_specs=[VMEM]...  18.9 us
    all_to_all x1, waiting for transfers between devices, shards(): returned = lax.all_to_all(part, 'z', 0, 0, tiled=True)  12.6 us
    all_to_all x1, starting transfers between devices, shards(): returned = lax.all_to_all(part, 'z', 0, 0, tiled=True)  6.39 us
    ppermute x1, starting transfers between devices, shards(): lax.ppermute(stepped, ('x', 'z'), [(i + 1, i) for i in range(count - 1)])  4.99 us
    ppermute x1, waiting for transfers between devices, shards(): lax.ppermute(stepped, ('x', 'z'), [(i, i + 1) for i in range(count - 1)])  4.99 us
    unnamed x31, local copies, waits for them, and re-layouts  4.67 us
  transfers between devices with their start and end apart: 12, of which 3 were waited for; matrix products, arithmetic and copies ran while one was open for 2% of the time, Pallas kernels for 11%

profile of v2, /device:TPU:70, one launch (start us, length us, event | category | flops | bytes accessed | tf_op | source)
XLA Modules:
  0.0 164.4 jit_solution(4131069856123621972)
XLA Ops:
  0.6 2.2 %pack.1 = bf16[16,80,128]{2,1,0:T(8,128)(2,1)} custom-call(s32[1]{0:T(128)} %bitcast.core_ref, bf16[32,4096]{1,0:T(8,128)(2,1)} %q_ref.1, bf16[32,4096]{1,0:T(8,128)(2,1)} %k_ref.1, bf16[32,4096]{1,0:T(8,128)(2,1)} %v_ref.1, bf16[64,4096]{1,0:T(8,128)(2,1)} %bitcast.9), custom_call_target="tpu_custom_call" | custom-call | tf_op jit(solution)/shard_map/pack/pallas_call | solution.py:44
  2.8 64.5 %all_to_all.10.own_ref.refs_0_ = bf16[16,80,128]{2,1,0:T(8,128)(2,1)S(1)} all-to-all(bf16[16,80,128]{2,1,0:T(8,128)(2,1)} %pack.1), channel_id=1, replica_groups=mesh['groups'=2,'branch'=2,'x'=8,'z'=16] {'z'}, dimensions={0} | all-to-all | bytes 655360 | tf_op jit(solution)/shard_map/all_to_all | solution.py:273
  67.3 4.8 %collective-permute-start.2 = (bf16[16,48,128]{2,1,0:T(8,128)(2,1)S(1)}, bf16[16,48,128]{2,1,0:T(8,128)(2,1)S(1)}, u32[]{:S(2)}, u32[]{:S(2)}) collective-permute-start(bf16[16,48,128]{2,1,0:T(8,128)(2,1)S(1)} %slice.28), channel_id=1, source_target_pairs={{0,16},{16,32},{32,48},{48,64},{64,80},{80,96},{96,112},{112,0},{1... | collective-permute-start | bytes 589832 | tf_op jit(solution)/shard_map/ppermute | solution.py:244
  72.1 2.0 %collective-permute-start.3 = (bf16[16,48,128]{2,1,0:T(8,128)(2,1)S(1)}, bf16[16,48,128]{2,1,0:T(8,128)(2,1)S(1)}, u32[]{:S(2)}, u32[]{:S(2)}) collective-permute-start(bf16[16,48,128]{2,1,0:T(8,128)(2,1)S(1)} %slice.28), channel_id=1, source_target_pairs={{0,112},{16,0},{32,16},{48,32},{64,48},{80,64},{96,80},{112,96},{1... | collective-permute-start | bytes 589832 | tf_op jit(solution)/shard_map/ppermute | solution.py:244
  74.1 4.1 %collective-permute-start = (bf16[16,48,128]{2,1,0:T(8,128)(2,1)S(1)}, bf16[16,48,128]{2,1,0:T(8,128)(2,1)S(1)}, u32[]{:S(2)}, u32[]{:S(2)}) collective-permute-start(bf16[16,48,128]{2,1,0:T(8,128)(2,1)S(1)} %slice.28), channel_id=1, source_target_pairs={{0,32},{16,48},{32,64},{48,80},{64,96},{80,112},{96,0},{112,16},{1... | collective-permute-start | bytes 589832 | tf_op jit(solution)/shard_map/ppermute | solution.py:244
  78.2 2.7 %collective-permute-start.1 = (bf16[16,48,128]{2,1,0:T(8,128)(2,1)S(1)}, bf16[16,48,128]{2,1,0:T(8,128)(2,1)S(1)}, u32[]{:S(2)}, u32[]{:S(2)}) collective-permute-start(bf16[16,48,128]{2,1,0:T(8,128)(2,1)S(1)} %slice.28), channel_id=1, source_target_pairs={{0,96},{16,112},{32,0},{48,16},{64,32},{80,48},{96,64},{112,80},{1... | collective-permute-start | bytes 589832 | tf_op jit(solution)/shard_map/ppermute | solution.py:244
  80.9 2.2 %terms.1 = (bf16[32,128]{1,0:T(8,128)(2,1)}, f32[16,64]{1,0:T(8,128)}) custom-call(s32[8]{0:T(128)} %kb_ref.1, s32[8]{0:T(128)} %ms_ref.1, s32[1]{0:T(128)} %bitcast.2.x_ref, s32[1]{0:T(128)} %bitcast.3.head_ref, bf16[16,2,4096]{2,1,0:T(2,128)(2,1)} %key_ref.1, bf16[32,2,4096]{2,1,0:T(2,128)(2,1)} %mouse_ref.1, bf16[64,4096]{1,0:T(8,128)(2,1)} %bitcast.10), custom_call_target="tpu_custom_call" | custom-call | tf_op jit(solution)/shard_map/terms/pallas_call | solution.py:74
  83.1 2.4 %frame.8 = (f32[64,512]{1,0:T(8,128)}, f32[2,512]{1,0:T(2,128)}) custom-call(bf16[16,80,128]{2,1,0:T(8,128)(2,1)} %copy-done, bf16[16,80,128]{2,1,0:T(8,128)(2,1)} %copy-done), custom_call_target="tpu_custom_call" | custom-call | flops 100663296 | bytes 1048576 | tf_op jit(solution)/shard_map/frame/pallas_call | solution.py:126
  85.5 0.0 collective-permute-done.2.refs_0_
  85.5 0.7 copy-done.5
  86.2 2.4 %frame.9 = (f32[64,512]{1,0:T(8,128)}, f32[2,512]{1,0:T(2,128)}) custom-call(bf16[16,80,128]{2,1,0:T(8,128)(2,1)} %copy-done, bf16[16,48,128]{2,1,0:T(8,128)(2,1)} %copy-done.5), custom_call_target="tpu_custom_call" | custom-call | flops 100663296 | bytes 1048576 | tf_op jit(solution)/shard_map/frame/pallas_call | solution.py:126
  88.5 0.0 collective-permute-done.3.refs_0_
  88.5 0.7 copy-done.3
  89.2 2.4 %frame.10 = (f32[64,512]{1,0:T(8,128)}, f32[2,512]{1,0:T(2,128)}) custom-call(bf16[16,80,128]{2,1,0:T(8,128)(2,1)} %copy-done, bf16[16,48,128]{2,1,0:T(8,128)(2,1)} %copy-done.3), custom_call_target="tpu_custom_call" | custom-call | flops 100663296 | bytes 1048576 | tf_op jit(solution)/shard_map/frame/pallas_call | solution.py:126
  91.6 0.0 collective-permute-done.refs_0_
  91.6 0.0 collective-permute-done.1.refs_0_
  91.6 3.7 %collective-permute-start.5 = (bf16[16,48,128]{2,1,0:T(8,128)(2,1)S(1)}, bf16[16,48,128]{2,1,0:T(8,128)(2,1)S(1)}, u32[]{:S(2)}, u32[]{:S(2)}) collective-permute-start(bf16[16,48,128]{2,1,0:T(8,128)(2,1)S(1)} %collective-permute-done.1.refs_0_), channel_id=1, source_target_pairs={{0,112},{16,0},{32,16},{48,32},{64,48},{80,64},{96,80},{112,96},{1... | collective-permute-start | bytes 589832 | tf_op jit(solution)/shard_map/ppermute | solution.py:244
  95.3 4.6 %collective-permute-start.4 = (bf16[16,48,128]{2,1,0:T(8,128)(2,1)S(1)}, bf16[16,48,128]{2,1,0:T(8,128)(2,1)S(1)}, u32[]{:S(2)}, u32[]{:S(2)}) collective-permute-start(bf16[16,48,128]{2,1,0:T(8,128)(2,1)S(1)} %collective-permute-done.refs_0_), channel_id=1, source_target_pairs={{0,16},{16,32},{32,48},{48,64},{64,80},{80,96},{96,112},{112,0},{1... | collective-permute-start | bytes 589832 | tf_op jit(solution)/shard_map/ppermute | solution.py:244
  100.0 3.4 %collective-permute-start.6 = (bf16[8,48,128]{2,1,0:T(8,128)(2,1)S(1)}, bf16[8,48,128]{2,1,0:T(8,128)(2,1)S(1)}, u32[]{:S(2)}, u32[]{:S(2)}) collective-permute-start(bf16[8,48,128]{2,1,0:T(8,128)(2,1)S(1)} %slice.22), channel_id=1, source_target_pairs={{0,32},{16,48},{32,64},{48,80},{64,96},{80,112},{96,0},{112,16},{1... | collective-permute-start | bytes 294920 | tf_op jit(solution)/shard_map/ppermute | solution.py:244
  103.4 3.4 %collective-permute-start.7 = (bf16[8,48,128]{2,1,0:T(8,128)(2,1)S(1)}, bf16[8,48,128]{2,1,0:T(8,128)(2,1)S(1)}, u32[]{:S(2)}, u32[]{:S(2)}) collective-permute-start(bf16[8,48,128]{2,1,0:T(8,128)(2,1)S(1)} %slice.23), channel_id=1, source_target_pairs={{0,96},{16,112},{32,0},{48,16},{64,32},{80,48},{96,64},{112,80},{1... | collective-permute-start | bytes 294920 | tf_op jit(solution)/shard_map/ppermute | solution.py:244
  106.8 2.4 %frame.12 = (f32[64,512]{1,0:T(8,128)}, f32[2,512]{1,0:T(2,128)}) custom-call(bf16[16,80,128]{2,1,0:T(8,128)(2,1)} %copy-done, bf16[16,48,128]{2,1,0:T(8,128)(2,1)} %copy-done.2), custom_call_target="tpu_custom_call" | custom-call | flops 100663296 | bytes 1048576 | tf_op jit(solution)/shard_map/frame/pallas_call | solution.py:126
  109.1 2.4 %frame.11 = (f32[64,512]{1,0:T(8,128)}, f32[2,512]{1,0:T(2,128)}) custom-call(bf16[16,80,128]{2,1,0:T(8,128)(2,1)} %copy-done, bf16[16,48,128]{2,1,0:T(8,128)(2,1)} %copy-done.1), custom_call_target="tpu_custom_call" | custom-call | flops 100663296 | bytes 1048576 | tf_op jit(solution)/shard_map/frame/pallas_call | solution.py:126
  111.5 1.4 collective-permute-done.7.refs_1_
  112.9 0.6 copy-done.8
  113.5 2.4 %frame.15 = (f32[64,512]{1,0:T(8,128)}, f32[2,512]{1,0:T(2,128)}) custom-call(bf16[16,80,128]{2,1,0:T(8,128)(2,1)} %copy-done, bf16[8,48,128]{2,1,0:T(8,128)(2,1)} %copy-done.7, bf16[8,48,128]{2,1,0:T(8,128)(2,1)} %copy-done.8), custom_call_target="tpu_custom_call" | custom-call | flops 100663296 | bytes 1048576 | tf_op jit(solution)/shard_map/frame/pallas_call | solution.py:126
  115.9 0.7 copy-done.6
  116.6 2.4 %frame.14 = (f32[64,512]{1,0:T(8,128)}, f32[2,512]{1,0:T(2,128)}) custom-call(bf16[16,80,128]{2,1,0:T(8,128)(2,1)} %copy-done, bf16[16,48,128]{2,1,0:T(8,128)(2,1)} %copy-done.6), custom_call_target="tpu_custom_call" | custom-call | flops 100663296 | bytes 1048576 | tf_op jit(solution)/shard_map/frame/pallas_call | solution.py:126
  118.9 0.0 collective-permute-done.4.refs_0_
  118.9 0.7 copy-done.4
  119.6 2.3 %frame.13 = (f32[64,512]{1,0:T(8,128)}, f32[2,512]{1,0:T(2,128)}) custom-call(bf16[16,80,128]{2,1,0:T(8,128)(2,1)} %copy-done, bf16[16,48,128]{2,1,0:T(8,128)(2,1)} %copy-done.4), custom_call_target="tpu_custom_call" | custom-call | flops 100663296 | bytes 1048576 | tf_op jit(solution)/shard_map/frame/pallas_call | solution.py:126
  122.0 2.7 %guide.1 = bf16[16,16,128]{2,1,0:T(8,128)(2,1)} custom-call(f32[4]{0:T(128)} %guide_ref.1, bf16[16,80,128]{2,1,0:T(8,128)(2,1)} %copy-done, bf16[32,128]{1,0:T(8,128)(2,1)} %get-tuple-element.38.bias_ref, f32[16,64]{1,0:T(8,128)} %get-tuple-element.39.term_ref, f32[64,512]{1,0:T(8,128)} %get-tuple-element.40.refs_0_, f32[64,512]{1,0:T(8,128)} %get-tuple-element.41.refs_1_, ...), custom_call_target="tpu_custom_call" | custom-call | tf_op jit(solution)/shard_map/guide/pallas_call | solution.py:169
  124.7 6.4 %all-to-all-start.1 = ((bf16[16,16,128]{2,1,0:T(8,128)(2,1)}), bf16[16,16,128]{2,1,0:T(8,128)(2,1)S(1)}, u32[]{:S(2)}, u32[]{:S(2)}) async-start(bf16[16,16,128]{2,1,0:T(8,128)(2,1)} %guide.1), calls=%async_computation.1 | async-start | bytes 131072 | tf_op jit(solution)/shard_map/all_to_all | solution.py:310
  131.1 0.0 copy-start.9
  131.1 12.6 %all-to-all-done.1 = bf16[16,16,128]{2,1,0:T(8,128)(2,1)S(1)} async-done(((bf16[16,16,128]{2,1,0:T(8,128)(2,1)}), bf16[16,16,128]{2,1,0:T(8,128)(2,1)S(1)}, u32[]{:S(2)}, u32[]{:S(2)}) %all-to-all-start.1) | async-done | bytes 65568 | tf_op jit(solution)/shard_map/all_to_all | solution.py:310
  143.7 2.0 %collective-permute-start.8 = (f32[16,128]{1,0:T(8,128)S(1)}, f32[16,128]{1,0:T(8,128)S(1)}, u32[]{:S(2)}, u32[]{:S(2)}) collective-permute-start(f32[16,128]{1,0:T(8,128)S(1)} %convert_reduce_fusion), channel_id=1, source_target_pairs={{0,128},{128,0},{1,129},{129,1},{2,130},{130,2},{3,131},{131,3},{4... | collective-permute-start | bytes 24584 | tf_op jit(solution)/shard_map/ppermute | solution.py:312
  145.7 0.6 pad_add_fusion.index_ref
  146.3 0.0 copy-start.14
  146.3 0.7 copy-done.14
  147.0 0.5 broadcast_in_dim.15.gain_ref
  147.5 0.6 pad.4.clone
  148.1 0.1 fusion
  148.2 5.0 %collective-permute-start.10 = (bf16[16,128]{1,0:T(8,128)(2,1)S(1)}, bf16[16,128]{1,0:T(8,128)(2,1)S(1)}, u32[]{:S(2)}, u32[]{:S(2)}) collective-permute-start(bf16[16,128]{1,0:T(8,128)(2,1)S(1)} %get-tuple-element.58.mine_ref), channel_id=1, source_target_pairs={{1,0},{2,1},{3,2},{4,3},{5,4},{6,5},{7,6},{8,7},{9,8},{10,9},{11,1... | collective-permute-start | bytes 12296 | tf_op jit(solution)/shard_map/ppermute | solution.py:322
  153.2 2.0 %collective-permute-start.9 = (bf16[16,128]{1,0:T(8,128)(2,1)S(1)}, bf16[16,128]{1,0:T(8,128)(2,1)S(1)}, u32[]{:S(2)}, u32[]{:S(2)}) collective-permute-start(bf16[16,128]{1,0:T(8,128)(2,1)S(1)} %get-tuple-element.58.mine_ref), channel_id=1, source_target_pairs={{0,1},{1,2},{2,3},{3,4},{4,5},{5,6},{6,7},{7,8},{8,9},{9,10},{10,1... | collective-permute-start | bytes 12296 | tf_op jit(solution)/shard_map/ppermute | solution.py:321
  155.2 0.1 fusion.2
  155.2 0.6 pad_maximum_fusion
  155.9 5.0 %collective-permute-done.9.before_ref = bf16[16,128]{1,0:T(8,128)(2,1)S(1)} collective-permute-done((bf16[16,128]{1,0:T(8,128)(2,1)S(1)}, bf16[16,128]{1,0:T(8,128)(2,1)S(1)}, u32[]{:S(2)}, u32[]{:S(2)}) %collective-permute-start.9) | collective-permute-done | bytes 4128 | tf_op jit(solution)/shard_map/ppermute | solution.py:321
  160.8 0.6 copy-done.13
  161.4 2.9 %decode.1 = f32[3,2,64]{2,1,0:T(2,128)} custom-call(s32[2]{0:T(128)} %pad_add_fusion.index_ref, bf16[16,128]{1,0:T(8,128)(2,1)} %copy-done.13, bf16[16,128]{1,0:T(8,128)(2,1)} %copy-done.11, bf16[16,128]{1,0:T(8,128)(2,1)} %copy-done.12, bf16[3,48,384]{2,1,0:T(8,128)(2,1)} %bitcast.12, f32[1,384]{1,0:T(1,128)} %broadcast_in_dim.15.gain_ref, ...), custom_call_target="tpu_custom_call" | custom-call | tf_op jit(solution)/shard_map/decode/pallas_call | solution.py:234
  (32 shorter events, 0.1 us)
Async XLA Ops:
  67.3 15.8 %copy-start = (bf16[16,80,128]{2,1,0:T(8,128)(2,1)}, bf16[16,80,128]{2,1,0:T(8,128)(2,1)S(1)}, u32[]{:S(2)}) copy-start(bf16[16,80,128]{2,1,0:T(8,128)(2,1)S(1)} %all_to_all.10.own_ref.refs_0_) | copy-start | bytes 983044
  67.3 18.2 %collective-permute-start.2 = (bf16[16,48,128]{2,1,0:T(8,128)(2,1)S(1)}, bf16[16,48,128]{2,1,0:T(8,128)(2,1)S(1)}, u32[]{:S(2)}, u32[]{:S(2)}) collective-permute-start(bf16[16,48,128]{2,1,0:T(8,128)(2,1)S(1)} %slice.28), channel_id=1, source_target_pairs={{0,16},{16,32},{32,48},{48,64},{64,80},{80,96},{96,112},{112,0},{1... | collective-permute-start | bytes 589832 | tf_op jit(solution)/shard_map/ppermute | solution.py:244
  72.1 16.4 %collective-permute-start.3 = (bf16[16,48,128]{2,1,0:T(8,128)(2,1)S(1)}, bf16[16,48,128]{2,1,0:T(8,128)(2,1)S(1)}, u32[]{:S(2)}, u32[]{:S(2)}) collective-permute-start(bf16[16,48,128]{2,1,0:T(8,128)(2,1)S(1)} %slice.28), channel_id=1, source_target_pairs={{0,112},{16,0},{32,16},{48,32},{64,48},{80,64},{96,80},{112,96},{1... | collective-permute-start | bytes 589832 | tf_op jit(solution)/shard_map/ppermute | solution.py:244
  74.1 17.5 %collective-permute-start = (bf16[16,48,128]{2,1,0:T(8,128)(2,1)S(1)}, bf16[16,48,128]{2,1,0:T(8,128)(2,1)S(1)}, u32[]{:S(2)}, u32[]{:S(2)}) collective-permute-start(bf16[16,48,128]{2,1,0:T(8,128)(2,1)S(1)} %slice.28), channel_id=1, source_target_pairs={{0,32},{16,48},{32,64},{48,80},{64,96},{80,112},{96,0},{112,16},{1... | collective-permute-start | bytes 589832 | tf_op jit(solution)/shard_map/ppermute | solution.py:244
  78.2 13.4 %collective-permute-start.1 = (bf16[16,48,128]{2,1,0:T(8,128)(2,1)S(1)}, bf16[16,48,128]{2,1,0:T(8,128)(2,1)S(1)}, u32[]{:S(2)}, u32[]{:S(2)}) collective-permute-start(bf16[16,48,128]{2,1,0:T(8,128)(2,1)S(1)} %slice.28), channel_id=1, source_target_pairs={{0,96},{16,112},{32,0},{48,16},{64,32},{80,48},{96,64},{112,80},{1... | collective-permute-start | bytes 589832 | tf_op jit(solution)/shard_map/ppermute | solution.py:244
  85.5 0.7 copy-start.5
  88.5 0.7 copy-start.3
  91.6 8.4 %copy-start.1 = (bf16[16,48,128]{2,1,0:T(8,128)(2,1)}, bf16[16,48,128]{2,1,0:T(8,128)(2,1)S(1)}, u32[]{:S(2)}) copy-start(bf16[16,48,128]{2,1,0:T(8,128)(2,1)S(1)} %collective-permute-done.refs_0_) | copy-start | bytes 589828
  91.6 8.4 %copy-start.2 = (bf16[16,48,128]{2,1,0:T(8,128)(2,1)}, bf16[16,48,128]{2,1,0:T(8,128)(2,1)S(1)}, u32[]{:S(2)}) copy-start(bf16[16,48,128]{2,1,0:T(8,128)(2,1)S(1)} %collective-permute-done.1.refs_0_) | copy-start | bytes 589828
  91.6 24.3 %collective-permute-start.5 = (bf16[16,48,128]{2,1,0:T(8,128)(2,1)S(1)}, bf16[16,48,128]{2,1,0:T(8,128)(2,1)S(1)}, u32[]{:S(2)}, u32[]{:S(2)}) collective-permute-start(bf16[16,48,128]{2,1,0:T(8,128)(2,1)S(1)} %collective-permute-done.1.refs_0_), channel_id=1, source_target_pairs={{0,112},{16,0},{32,16},{48,32},{64,48},{80,64},{96,80},{112,96},{1... | collective-permute-start | bytes 589832 | tf_op jit(solution)/shard_map/ppermute | solution.py:244
  95.3 23.6 %collective-permute-start.4 = (bf16[16,48,128]{2,1,0:T(8,128)(2,1)S(1)}, bf16[16,48,128]{2,1,0:T(8,128)(2,1)S(1)}, u32[]{:S(2)}, u32[]{:S(2)}) collective-permute-start(bf16[16,48,128]{2,1,0:T(8,128)(2,1)S(1)} %collective-permute-done.refs_0_), channel_id=1, source_target_pairs={{0,16},{16,32},{32,48},{48,64},{64,80},{80,96},{96,112},{112,0},{1... | collective-permute-start | bytes 589832 | tf_op jit(solution)/shard_map/ppermute | solution.py:244
  100.0 11.5 %collective-permute-start.6 = (bf16[8,48,128]{2,1,0:T(8,128)(2,1)S(1)}, bf16[8,48,128]{2,1,0:T(8,128)(2,1)S(1)}, u32[]{:S(2)}, u32[]{:S(2)}) collective-permute-start(bf16[8,48,128]{2,1,0:T(8,128)(2,1)S(1)} %slice.22), channel_id=1, source_target_pairs={{0,32},{16,48},{32,64},{48,80},{64,96},{80,112},{96,0},{112,16},{1... | collective-permute-start | bytes 294920 | tf_op jit(solution)/shard_map/ppermute | solution.py:244
  103.4 9.5 %collective-permute-start.7 = (bf16[8,48,128]{2,1,0:T(8,128)(2,1)S(1)}, bf16[8,48,128]{2,1,0:T(8,128)(2,1)S(1)}, u32[]{:S(2)}, u32[]{:S(2)}) collective-permute-start(bf16[8,48,128]{2,1,0:T(8,128)(2,1)S(1)} %slice.23), channel_id=1, source_target_pairs={{0,96},{16,112},{32,0},{48,16},{64,32},{80,48},{96,64},{112,80},{1... | collective-permute-start | bytes 294920 | tf_op jit(solution)/shard_map/ppermute | solution.py:244
  111.5 1.4 copy-start.7
  112.9 0.6 copy-start.8
  115.9 0.7 copy-start.6
  118.9 0.7 copy-start.4
  124.6 6.4 %copy-start.10 = (f32[32,64]{1,0:T(8,128)S(1)}, f32[32,64]{1,0:T(8,128)}, u32[]{:S(2)}) copy-start(f32[32,64]{1,0:T(8,128)} %param.22) | copy-start | bytes 24580
  124.7 19.0 %all-to-all-start.1 = ((bf16[16,16,128]{2,1,0:T(8,128)(2,1)}), bf16[16,16,128]{2,1,0:T(8,128)(2,1)S(1)}, u32[]{:S(2)}, u32[]{:S(2)}) async-start(bf16[16,16,128]{2,1,0:T(8,128)(2,1)} %guide.1), calls=%async_computation.1 | async-start | bytes 131072 | tf_op jit(solution)/shard_map/all_to_all | solution.py:310
  131.1 15.2 %copy-start.9 = (bf16[3,3,384,3]{2,3,1,0:T(4,128)(2,1)S(1)}, bf16[3,3,384,3]{2,3,1,0:T(4,128)(2,1)}, u32[]{:S(2)}) copy-start(bf16[3,3,384,3]{2,3,1,0:T(4,128)(2,1)} %param.25) | copy-start | bytes 62212
  143.7 4.4 %collective-permute-start.8 = (f32[16,128]{1,0:T(8,128)S(1)}, f32[16,128]{1,0:T(8,128)S(1)}, u32[]{:S(2)}, u32[]{:S(2)}) collective-permute-start(f32[16,128]{1,0:T(8,128)S(1)} %convert_reduce_fusion), channel_id=1, source_target_pairs={{0,128},{128,0},{1,129},{129,1},{2,130},{130,2},{3,131},{131,3},{4... | collective-permute-start | bytes 24584 | tf_op jit(solution)/shard_map/ppermute | solution.py:312
  146.3 0.7 copy-start.14
  148.2 7.0 %copy-start.11 = (bf16[16,128]{1,0:T(8,128)(2,1)}, bf16[16,128]{1,0:T(8,128)(2,1)S(1)}, u32[]{:S(2)}) copy-start(bf16[16,128]{1,0:T(8,128)(2,1)S(1)} %get-tuple-element.58.mine_ref) | copy-start | bytes 12292
  148.2 7.7 %collective-permute-start.10 = (bf16[16,128]{1,0:T(8,128)(2,1)S(1)}, bf16[16,128]{1,0:T(8,128)(2,1)S(1)}, u32[]{:S(2)}, u32[]{:S(2)}) collective-permute-start(bf16[16,128]{1,0:T(8,128)(2,1)S(1)} %get-tuple-element.58.mine_ref), channel_id=1, source_target_pairs={{1,0},{2,1},{3,2},{4,3},{5,4},{6,5},{7,6},{8,7},{9,8},{10,9},{11,1... | collective-permute-start | bytes 12296 | tf_op jit(solution)/shard_map/ppermute | solution.py:322
  153.2 7.6 %collective-permute-start.9 = (bf16[16,128]{1,0:T(8,128)(2,1)S(1)}, bf16[16,128]{1,0:T(8,128)(2,1)S(1)}, u32[]{:S(2)}, u32[]{:S(2)}) collective-permute-start(bf16[16,128]{1,0:T(8,128)(2,1)S(1)} %get-tuple-element.58.mine_ref), channel_id=1, source_target_pairs={{0,1},{1,2},{2,3},{3,4},{4,5},{5,6},{6,7},{7,8},{8,9},{9,10},{10,1... | collective-permute-start | bytes 12296 | tf_op jit(solution)/shard_map/ppermute | solution.py:321
  155.9 5.0 %copy-start.12 = (bf16[16,128]{1,0:T(8,128)(2,1)}, bf16[16,128]{1,0:T(8,128)(2,1)S(1)}, u32[]{:S(2)}) copy-start(bf16[16,128]{1,0:T(8,128)(2,1)S(1)} %collective-permute-done.10.after_ref) | copy-start | bytes 12292
  160.8 0.6 copy-start.13

commit v3 on v2

--- a/solution.py
+++ b/solution.py
@@ -18,40 +18,65 @@
 F32 = jnp.float32
 VMEM = pl.BlockSpec(memory_space=pltpu.VMEM)
 SMEM = pl.BlockSpec(memory_space=pltpu.SMEM)
+GRANT = pltpu.CompilerParams(vmem_limit_bytes=12 << 20)
+
+
+def in_hbm(array):
+    return pltpu.with_memory_space_constraint(array, pltpu.HBM)
 
 
 def dot(a, b, dims, **kw):
     return lax.dot_general(a, b, (dims, ((), ())), preferred_element_type=F32, **kw)
 
 
-def pack_kernel(core_ref, q_ref, k_ref, v_ref, w_ref, out_ref):
+def pack_kernel(core_ref, q_ref, k_ref, v_ref, w_ref, out_ref, v_tmp, w_tmp, sems):
     sets, _, hd = out_ref.shape
     rows = q_ref.shape[0]
     half = rows // 2
+    first = pl.multiple_of(core_ref[0] * (sets * hd), hd)
+    mine = pl.ds(first, sets * hd)
+    copies = [
+        pltpu.make_async_copy(w_ref.at[:, mine], w_tmp, sems.at[0]),
+        pltpu.make_async_copy(v_ref.at[:, mine], v_tmp, sems.at[1]),
+    ]
+    for n, source in enumerate((q_ref, k_ref)):
+        for z in range(sets):
+            copies.append(
+                pltpu.make_async_copy(
+                    source.at[:, pl.ds(pl.multiple_of(first + z * hd, hd), hd)],
+                    out_ref.at[z, pl.ds(n * rows, rows), :],
+                    sems.at[len(copies)],
+                )
+            )
+    for copy in copies:
+        copy.start()
+    for copy in copies[:2]:
+        copy.wait()
     for z in range(sets):
         cols = slice(z * hd, (z + 1) * hd)
-        out_ref[z, 0:rows, :] = q_ref[:, cols]
-        out_ref[z, rows : 2 * rows, :] = k_ref[:, cols]
-        projected = dot(v_ref[:, cols], w_ref[:, cols], ((1,), (1,))).astype(BF)
+        projected = dot(v_tmp[:, cols], w_tmp[:, cols], ((1,), (1,))).astype(BF)
         out_ref[z, 2 * rows :, :] = jnp.concatenate([projected[:half], projected[half:]], axis=1)
+    for copy in copies[2:]:
+        copy.wait()
 
 
 def pack(core, queries, keys, values, weight_t, sets):
     rows = queries.shape[0]
     cols = sets * HEAD_DIM
-    outs = weight_t.shape[0]
-    block = pl.BlockSpec((rows, cols), lambda i, c: (0, c[0]))
+    hbm = pl.BlockSpec(memory_space=pltpu.HBM)
     return pl.pallas_call(
         pack_kernel,
-        grid_spec=pltpu.PrefetchScalarGridSpec(
-            num_scalar_prefetch=1,
-            grid=(1,),
-            in_specs=[block, block, block, pl.BlockSpec((outs, cols), lambda i, c: (0, c[0]))],
-            out_specs=VMEM,
-        ),
+        in_specs=[SMEM, hbm, hbm, hbm, hbm],
+        out_specs=VMEM,
         out_shape=jax.ShapeDtypeStruct((sets, 2 * rows + rows // 2, HEAD_DIM), BF),
+        scratch_shapes=[
+            pltpu.VMEM((rows, cols), BF),
+            pltpu.VMEM((weight_t.shape[0], cols), BF),
+            pltpu.SemaphoreType.DMA((2 + 2 * sets,)),
+        ],
         name="pack",
-    )(core[None], queries, keys, values, weight_t)
+        compiler_params=GRANT,
+    )(core[None], *(in_hbm(a) for a in (queries, keys, values, weight_t)))
 
 
 def terms_kernel(offsets, kb_ref, ms_ref, x_ref, head_ref, key_ref, mouse_ref, w_ref, bias_ref, term_ref):
@@ -88,6 +113,7 @@
             jax.ShapeDtypeStruct((2 * frames, outs), F32),
         ],
         name="terms",
+        compiler_params=GRANT,
     )(keyboard, mouse, x[None], head[None], key_table, mouse_table, weight_t)
 
 
@@ -135,6 +161,7 @@
             flops=flops, transcendentals=tokens * tokens, bytes_accessed=1 << 20
         ),
         name="frame",
+        compiler_params=GRANT,
     )(own, *pieces)
 
 
@@ -172,6 +199,7 @@
         out_specs=VMEM,
         out_shape=jax.ShapeDtypeStruct((sets, rows // 2, 2 * outs), BF),
         name="guide",
+        compiler_params=GRANT,
     )(guidance, own, bias, term, *sums, *stats)
 
 
@@ -237,6 +265,7 @@
         out_specs=VMEM,
         out_shape=jax.ShapeDtypeStruct((3, 2, 2 * tokens), F32),
         name="decode",
+        compiler_params=GRANT,
     )(index, before, mine, after, conv_in, gain, conv_out)
 
 

time: 165 us -> 152 us (0.921)
  the two profiles are of different devices: /device:TPU:70 before, /device:TPU:68 now
where the time goes in v3:
time: 152 us
  blocking collectives  64.4 us (42%)
  starting transfers between devices  43.5 us (29%)
  waiting for transfers between devices  27.9 us (18%)
  Pallas kernels  12.1 us (8%)
  local copies, waits for them, and re-layouts  2.11 us (1%)
    all_to_all x1, blocking collectives, shards(): own = lax.all_to_all(packed, 'z', 0, 0, tiled=True)  64.4 us
    ppermute x8, starting transfers between devices, shifted(): lax.ppermute(value, axis, [(i, (i + steps) % count) for i in range(count)])  27.6 us
    all_to_all x1, waiting for transfers between devices, shards(): returned = lax.all_to_all(part, 'z', 0, 0, tiled=True)  12.6 us
    ppermute x8, waiting for transfers between devices, shifted(): lax.ppermute(value, axis, [(i, (i + steps) % count) for i in range(count)])  10.6 us
    all_to_all x1, starting transfers between devices, shards(): returned = lax.all_to_all(part, 'z', 0, 0, tiled=True)  8.02 us
    pallas_call x8, Pallas kernels, frame_attention(): pl.pallas_call(functools.partial(frame_kernel, rows, at), in_specs=[VMEM]...  5.28 us
    ppermute x1, waiting for transfers between devices, shards(): lax.ppermute(stepped, ('x', 'z'), [(i, i + 1) for i in range(count - 1)])  4.29 us
    ppermute x1, starting transfers between devices, shards(): lax.ppermute(stepped, ('x', 'z'), [(i + 1, i) for i in range(count - 1)])  3.24 us
  transfers between devices with their start and end apart: 12, of which 6 were waited for; matrix products, arithmetic and copies ran while one was open for 1% of the time, Pallas kernels for 4%

profile of v3, /device:TPU:68, one launch (start us, length us, event | category | flops | bytes accessed | tf_op | source)
XLA Modules:
  0.0 151.7 jit_solution(3193402188551736563)
XLA Ops:
  0.6 1.7 %pack.1 = bf16[16,80,128]{2,1,0:T(8,128)(2,1)S(1)} custom-call(s32[1]{0:T(128)} %bitcast.core_ref, bf16[32,4096]{1,0:T(8,128)(2,1)} %q_ref.1, bf16[32,4096]{1,0:T(8,128)(2,1)} %k_ref.1, bf16[32,4096]{1,0:T(8,128)(2,1)} %v_ref.1, bf16[64,4096]{1,0:T(8,128)(2,1)} %bitcast.9), custom_call_target="tpu_custom_call" | custom-call | tf_op jit(solution)/shard_map/pack/pallas_call | solution.py:67
  2.4 0.0 copy-start
  2.4 0.0 copy-start.1
  2.4 64.4 %all_to_all.10.own_ref.refs_0_ = bf16[16,80,128]{2,1,0:T(8,128)(2,1)S(1)} all-to-all(bf16[16,80,128]{2,1,0:T(8,128)(2,1)S(1)} %pack.1), channel_id=1, replica_groups=mesh['groups'=2,'branch'=2,'x'=8,'z'=16] {'z'}, dimensions={0} | all-to-all | bytes 655360 | tf_op jit(solution)/shard_map/all_to_all | solution.py:302
  66.8 3.6 %collective-permute-start.2 = (bf16[16,48,128]{2,1,0:T(8,128)(2,1)S(1)}, bf16[16,48,128]{2,1,0:T(8,128)(2,1)S(1)}, u32[]{:S(2)}, u32[]{:S(2)}) collective-permute-start(bf16[16,48,128]{2,1,0:T(8,128)(2,1)S(1)} %slice.28), channel_id=1, source_target_pairs={{0,16},{16,32},{32,48},{48,64},{64,80},{80,96},{96,112},{112,0},{1... | collective-permute-start | bytes 589832 | tf_op jit(solution)/shard_map/ppermute | solution.py:273
  70.4 2.3 %collective-permute-start.3 = (bf16[16,48,128]{2,1,0:T(8,128)(2,1)S(1)}, bf16[16,48,128]{2,1,0:T(8,128)(2,1)S(1)}, u32[]{:S(2)}, u32[]{:S(2)}) collective-permute-start(bf16[16,48,128]{2,1,0:T(8,128)(2,1)S(1)} %slice.28), channel_id=1, source_target_pairs={{0,112},{16,0},{32,16},{48,32},{64,48},{80,64},{96,80},{112,96},{1... | collective-permute-start | bytes 589832 | tf_op jit(solution)/shard_map/ppermute | solution.py:273
  72.7 7.0 %collective-permute-start = (bf16[16,48,128]{2,1,0:T(8,128)(2,1)S(1)}, bf16[16,48,128]{2,1,0:T(8,128)(2,1)S(1)}, u32[]{:S(2)}, u32[]{:S(2)}) collective-permute-start(bf16[16,48,128]{2,1,0:T(8,128)(2,1)S(1)} %slice.28), channel_id=1, source_target_pairs={{0,32},{16,48},{32,64},{48,80},{64,96},{80,112},{96,0},{112,16},{1... | collective-permute-start | bytes 589832 | tf_op jit(solution)/shard_map/ppermute | solution.py:273
  79.8 2.0 %collective-permute-start.1 = (bf16[16,48,128]{2,1,0:T(8,128)(2,1)S(1)}, bf16[16,48,128]{2,1,0:T(8,128)(2,1)S(1)}, u32[]{:S(2)}, u32[]{:S(2)}) collective-permute-start(bf16[16,48,128]{2,1,0:T(8,128)(2,1)S(1)} %slice.28), channel_id=1, source_target_pairs={{0,96},{16,112},{32,0},{48,16},{64,32},{80,48},{96,64},{112,80},{1... | collective-permute-start | bytes 589832 | tf_op jit(solution)/shard_map/ppermute | solution.py:273
  81.7 0.0 copy-start.4
  81.8 0.0 copy-start.5
  81.8 0.6 copy-done.4
  82.4 0.0 copy-done.5
  82.4 0.7 terms.1
  83.1 0.7 frame.8
  83.8 0.0 collective-permute-done.2.refs_0_
  83.8 0.7 frame.9
  84.5 0.7 frame.10
  85.2 5.3 %collective-permute-done.1.refs_0_ = bf16[16,48,128]{2,1,0:T(8,128)(2,1)S(1)} collective-permute-done((bf16[16,48,128]{2,1,0:T(8,128)(2,1)S(1)}, bf16[16,48,128]{2,1,0:T(8,128)(2,1)S(1)}, u32[]{:S(2)}, u32[]{:S(2)}) %collective-permute-start.1) | collective-permute-done | bytes 196640 | tf_op jit(solution)/shard_map/ppermute | solution.py:273
  90.5 1.9 %collective-permute-start.5 = (bf16[16,48,128]{2,1,0:T(8,128)(2,1)S(1)}, bf16[16,48,128]{2,1,0:T(8,128)(2,1)S(1)}, u32[]{:S(2)}, u32[]{:S(2)}) collective-permute-start(bf16[16,48,128]{2,1,0:T(8,128)(2,1)S(1)} %collective-permute-done.1.refs_0_), channel_id=1, source_target_pairs={{0,112},{16,0},{32,16},{48,32},{64,48},{80,64},{96,80},{112,96},{1... | collective-permute-start | bytes 589832 | tf_op jit(solution)/shard_map/ppermute | solution.py:273
  92.4 4.0 %collective-permute-start.4 = (bf16[16,48,128]{2,1,0:T(8,128)(2,1)S(1)}, bf16[16,48,128]{2,1,0:T(8,128)(2,1)S(1)}, u32[]{:S(2)}, u32[]{:S(2)}) collective-permute-start(bf16[16,48,128]{2,1,0:T(8,128)(2,1)S(1)} %collective-permute-done.refs_0_), channel_id=1, source_target_pairs={{0,16},{16,32},{32,48},{48,64},{64,80},{80,96},{96,112},{112,0},{1... | collective-permute-start | bytes 589832 | tf_op jit(solution)/shard_map/ppermute | solution.py:273
  96.4 3.8 %collective-permute-start.6 = (bf16[8,48,128]{2,1,0:T(8,128)(2,1)S(1)}, bf16[8,48,128]{2,1,0:T(8,128)(2,1)S(1)}, u32[]{:S(2)}, u32[]{:S(2)}) collective-permute-start(bf16[8,48,128]{2,1,0:T(8,128)(2,1)S(1)} %slice.22), channel_id=1, source_target_pairs={{0,32},{16,48},{32,64},{48,80},{64,96},{80,112},{96,0},{112,16},{1... | collective-permute-start | bytes 294920 | tf_op jit(solution)/shard_map/ppermute | solution.py:273
  100.2 3.0 %collective-permute-start.7 = (bf16[8,48,128]{2,1,0:T(8,128)(2,1)S(1)}, bf16[8,48,128]{2,1,0:T(8,128)(2,1)S(1)}, u32[]{:S(2)}, u32[]{:S(2)}) collective-permute-start(bf16[8,48,128]{2,1,0:T(8,128)(2,1)S(1)} %slice.23), channel_id=1, source_target_pairs={{0,96},{16,112},{32,0},{48,16},{64,32},{80,48},{96,64},{112,80},{1... | collective-permute-start | bytes 294920 | tf_op jit(solution)/shard_map/ppermute | solution.py:273
  103.2 0.7 frame.12
  103.9 0.7 frame.11
  104.5 0.2 collective-permute-done.6.refs_0_
  104.7 5.1 %collective-permute-done.7.refs_1_ = bf16[8,48,128]{2,1,0:T(8,128)(2,1)S(1)} collective-permute-done((bf16[8,48,128]{2,1,0:T(8,128)(2,1)S(1)}, bf16[8,48,128]{2,1,0:T(8,128)(2,1)S(1)}, u32[]{:S(2)}, u32[]{:S(2)}) %collective-permute-start.7) | collective-permute-done | bytes 98336 | tf_op jit(solution)/shard_map/ppermute | solution.py:273
  109.9 0.7 frame.15
  110.5 0.7 frame.14
  111.2 0.7 frame.13
  111.9 0.0 copy-start.6
  111.9 0.6 copy-done.6
  112.6 1.8 %guide.1 = bf16[16,16,128]{2,1,0:T(8,128)(2,1)} custom-call(f32[4]{0:T(128)S(1)} %copy-done.6, bf16[16,80,128]{2,1,0:T(8,128)(2,1)S(1)} %all_to_all.10.own_ref.refs_0_, bf16[32,128]{1,0:T(8,128)(2,1)S(1)} %get-tuple-element.38.bias_ref, f32[16,64]{1,0:T(8,128)S(1)} %get-tuple-element.39.term_ref, f32[64,512]{1,0:T(8,128)S(1)} %get-tuple-element.40.refs_0_, ...), custom_call_target="tpu_custom_call" | custom-call | tf_op jit(solution)/shard_map/guide/pallas_call | solution.py:196
  114.4 8.0 %all-to-all-start.1 = ((bf16[16,16,128]{2,1,0:T(8,128)(2,1)}), bf16[16,16,128]{2,1,0:T(8,128)(2,1)S(1)}, u32[]{:S(2)}, u32[]{:S(2)}) async-start(bf16[16,16,128]{2,1,0:T(8,128)(2,1)} %guide.1), calls=%async_computation.1 | async-start | bytes 131072 | tf_op jit(solution)/shard_map/all_to_all | solution.py:339
  122.4 0.0 copy-start.7
  122.4 12.6 %all-to-all-done.1 = bf16[16,16,128]{2,1,0:T(8,128)(2,1)S(1)} async-done(((bf16[16,16,128]{2,1,0:T(8,128)(2,1)}), bf16[16,16,128]{2,1,0:T(8,128)(2,1)S(1)}, u32[]{:S(2)}, u32[]{:S(2)}) %all-to-all-start.1) | async-done | bytes 65568 | tf_op jit(solution)/shard_map/all_to_all | solution.py:339
  135.1 2.0 %collective-permute-start.8 = (f32[16,128]{1,0:T(8,128)S(1)}, f32[16,128]{1,0:T(8,128)S(1)}, u32[]{:S(2)}, u32[]{:S(2)}) collective-permute-start(f32[16,128]{1,0:T(8,128)S(1)} %convert_reduce_fusion), channel_id=1, source_target_pairs={{0,128},{128,0},{1,129},{129,1},{2,130},{130,2},{3,131},{131,3},{4... | collective-permute-start | bytes 24584 | tf_op jit(solution)/shard_map/ppermute | solution.py:341
  137.1 0.1 pad_add_fusion.index_ref
  137.2 0.0 copy-start.9
  137.2 0.7 copy-done.9
  137.9 0.3 collective-permute-done.8
  138.2 0.1 fusion
  138.3 3.2 %collective-permute-start.10 = (bf16[16,128]{1,0:T(8,128)(2,1)S(1)}, bf16[16,128]{1,0:T(8,128)(2,1)S(1)}, u32[]{:S(2)}, u32[]{:S(2)}) collective-permute-start(bf16[16,128]{1,0:T(8,128)(2,1)S(1)} %get-tuple-element.58.mine_ref), channel_id=1, source_target_pairs={{1,0},{2,1},{3,2},{4,3},{5,4},{6,5},{7,6},{8,7},{9,8},{10,9},{11,1... | collective-permute-start | bytes 12296 | tf_op jit(solution)/shard_map/ppermute | solution.py:351
  141.5 2.6 %collective-permute-start.9 = (bf16[16,128]{1,0:T(8,128)(2,1)S(1)}, bf16[16,128]{1,0:T(8,128)(2,1)S(1)}, u32[]{:S(2)}, u32[]{:S(2)}) collective-permute-start(bf16[16,128]{1,0:T(8,128)(2,1)S(1)} %get-tuple-element.58.mine_ref), channel_id=1, source_target_pairs={{0,1},{1,2},{2,3},{3,4},{4,5},{5,6},{6,7},{7,8},{8,9},{9,10},{10,1... | collective-permute-start | bytes 12296 | tf_op jit(solution)/shard_map/ppermute | solution.py:350
  144.2 0.1 fusion.2
  144.3 0.6 pad_maximum_fusion
  144.9 0.0 collective-permute-done.10.after_ref
  144.9 4.3 %collective-permute-done.9.before_ref = bf16[16,128]{1,0:T(8,128)(2,1)S(1)} collective-permute-done((bf16[16,128]{1,0:T(8,128)(2,1)S(1)}, bf16[16,128]{1,0:T(8,128)(2,1)S(1)}, u32[]{:S(2)}, u32[]{:S(2)}) %collective-permute-start.9) | collective-permute-done | bytes 4128 | tf_op jit(solution)/shard_map/ppermute | solution.py:350
  149.2 2.6 %decode.1 = f32[3,2,64]{2,1,0:T(2,128)} custom-call(s32[2]{0:T(128)S(1)} %pad_add_fusion.index_ref, bf16[16,128]{1,0:T(8,128)(2,1)S(1)} %collective-permute-done.9.before_ref, bf16[16,128]{1,0:T(8,128)(2,1)S(1)} %get-tuple-element.58.mine_ref, bf16[16,128]{1,0:T(8,128)(2,1)S(1)} %collective-permute-done.10.after_ref, bf16[3,48,384]{2,1,0:T(8,128)(2,1)S(1)} %bitcast.12, ...), custom_call_target="tpu_custom_call" | custom-call | tf_op jit(solution)/shard_map/decode/pallas_call | solution.py:262
  (22 shorter events, 0.1 us)
Async XLA Ops:
  0.6 81.1 %copy-start.2 = (bf16[16,2,4096]{2,1,0:T(2,128)(2,1)S(1)}, bf16[16,2,4096]{2,1,0:T(2,128)(2,1)}, u32[]{:S(2)}) copy-start(bf16[16,2,4096]{2,1,0:T(2,128)(2,1)} %key_ref.1) | copy-start | bytes 786436
  2.4 79.4 %copy-start = (bf16[4096,64]{0,1:T(8,128)(2,1)S(1)}, bf16[4096,64]{0,1:T(8,128)(2,1)}, u32[]{:S(2)}) copy-start(bf16[4096,64]{0,1:T(8,128)(2,1)} %param.21) | copy-start | bytes 1572868
  2.4 79.4 %copy-start.1 = (bf16[32,2,4096]{2,1,0:T(2,128)(2,1)S(1)}, bf16[32,2,4096]{2,1,0:T(2,128)(2,1)}, u32[]{:S(2)}) copy-start(bf16[32,2,4096]{2,1,0:T(2,128)(2,1)} %mouse_ref.1) | copy-start | bytes 1572868
  66.8 17.0 %collective-permute-start.2 = (bf16[16,48,128]{2,1,0:T(8,128)(2,1)S(1)}, bf16[16,48,128]{2,1,0:T(8,128)(2,1)S(1)}, u32[]{:S(2)}, u32[]{:S(2)}) collective-permute-start(bf16[16,48,128]{2,1,0:T(8,128)(2,1)S(1)} %slice.28), channel_id=1, source_target_pairs={{0,16},{16,32},{32,48},{48,64},{64,80},{80,96},{96,112},{112,0},{1... | collective-permute-start | bytes 589832 | tf_op jit(solution)/shard_map/ppermute | solution.py:273
  70.4 14.1 %collective-permute-start.3 = (bf16[16,48,128]{2,1,0:T(8,128)(2,1)S(1)}, bf16[16,48,128]{2,1,0:T(8,128)(2,1)S(1)}, u32[]{:S(2)}, u32[]{:S(2)}) collective-permute-start(bf16[16,48,128]{2,1,0:T(8,128)(2,1)S(1)} %slice.28), channel_id=1, source_target_pairs={{0,112},{16,0},{32,16},{48,32},{64,48},{80,64},{96,80},{112,96},{1... | collective-permute-start | bytes 589832 | tf_op jit(solution)/shard_map/ppermute | solution.py:273
  72.7 12.4 %collective-permute-start = (bf16[16,48,128]{2,1,0:T(8,128)(2,1)S(1)}, bf16[16,48,128]{2,1,0:T(8,128)(2,1)S(1)}, u32[]{:S(2)}, u32[]{:S(2)}) collective-permute-start(bf16[16,48,128]{2,1,0:T(8,128)(2,1)S(1)} %slice.28), channel_id=1, source_target_pairs={{0,32},{16,48},{32,64},{48,80},{64,96},{80,112},{96,0},{112,16},{1... | collective-permute-start | bytes 589832 | tf_op jit(solution)/shard_map/ppermute | solution.py:273
  79.8 10.7 %collective-permute-start.1 = (bf16[16,48,128]{2,1,0:T(8,128)(2,1)S(1)}, bf16[16,48,128]{2,1,0:T(8,128)(2,1)S(1)}, u32[]{:S(2)}, u32[]{:S(2)}) collective-permute-start(bf16[16,48,128]{2,1,0:T(8,128)(2,1)S(1)} %slice.28), channel_id=1, source_target_pairs={{0,96},{16,112},{32,0},{48,16},{64,32},{80,48},{96,64},{112,80},{1... | collective-permute-start | bytes 589832 | tf_op jit(solution)/shard_map/ppermute | solution.py:273
  81.7 0.7 copy-start.4
  81.8 0.7 copy-start.5
  90.5 20.1 %collective-permute-start.5 = (bf16[16,48,128]{2,1,0:T(8,128)(2,1)S(1)}, bf16[16,48,128]{2,1,0:T(8,128)(2,1)S(1)}, u32[]{:S(2)}, u32[]{:S(2)}) collective-permute-start(bf16[16,48,128]{2,1,0:T(8,128)(2,1)S(1)} %collective-permute-done.1.refs_0_), channel_id=1, source_target_pairs={{0,112},{16,0},{32,16},{48,32},{64,48},{80,64},{96,80},{112,96},{1... | collective-permute-start | bytes 589832 | tf_op jit(solution)/shard_map/ppermute | solution.py:273
  92.4 18.8 %collective-permute-start.4 = (bf16[16,48,128]{2,1,0:T(8,128)(2,1)S(1)}, bf16[16,48,128]{2,1,0:T(8,128)(2,1)S(1)}, u32[]{:S(2)}, u32[]{:S(2)}) collective-permute-start(bf16[16,48,128]{2,1,0:T(8,128)(2,1)S(1)} %collective-permute-done.refs_0_), channel_id=1, source_target_pairs={{0,16},{16,32},{32,48},{48,64},{64,80},{80,96},{96,112},{112,0},{1... | collective-permute-start | bytes 589832 | tf_op jit(solution)/shard_map/ppermute | solution.py:273
  96.4 8.3 %collective-permute-start.6 = (bf16[8,48,128]{2,1,0:T(8,128)(2,1)S(1)}, bf16[8,48,128]{2,1,0:T(8,128)(2,1)S(1)}, u32[]{:S(2)}, u32[]{:S(2)}) collective-permute-start(bf16[8,48,128]{2,1,0:T(8,128)(2,1)S(1)} %slice.22), channel_id=1, source_target_pairs={{0,32},{16,48},{32,64},{48,80},{64,96},{80,112},{96,0},{112,16},{1... | collective-permute-start | bytes 294920 | tf_op jit(solution)/shard_map/ppermute | solution.py:273
  100.2 9.7 %collective-permute-start.7 = (bf16[8,48,128]{2,1,0:T(8,128)(2,1)S(1)}, bf16[8,48,128]{2,1,0:T(8,128)(2,1)S(1)}, u32[]{:S(2)}, u32[]{:S(2)}) collective-permute-start(bf16[8,48,128]{2,1,0:T(8,128)(2,1)S(1)} %slice.23), channel_id=1, source_target_pairs={{0,96},{16,112},{32,0},{48,16},{64,32},{80,48},{96,64},{112,80},{1... | collective-permute-start | bytes 294920 | tf_op jit(solution)/shard_map/ppermute | solution.py:273
  111.9 0.7 copy-start.6
  114.4 8.0 %copy-start.8 = (f32[32,64]{1,0:T(8,128)S(1)}, f32[32,64]{1,0:T(8,128)}, u32[]{:S(2)}) copy-start(f32[32,64]{1,0:T(8,128)} %param.22) | copy-start | bytes 24580
  114.4 20.7 %all-to-all-start.1 = ((bf16[16,16,128]{2,1,0:T(8,128)(2,1)}), bf16[16,16,128]{2,1,0:T(8,128)(2,1)S(1)}, u32[]{:S(2)}, u32[]{:S(2)}) async-start(bf16[16,16,128]{2,1,0:T(8,128)(2,1)} %guide.1), calls=%async_computation.1 | async-start | bytes 131072 | tf_op jit(solution)/shard_map/all_to_all | solution.py:339
  122.4 14.7 %copy-start.7 = (bf16[3,3,384,3]{2,3,1,0:T(4,128)(2,1)S(1)}, bf16[3,3,384,3]{2,3,1,0:T(4,128)(2,1)}, u32[]{:S(2)}) copy-start(bf16[3,3,384,3]{2,3,1,0:T(4,128)(2,1)} %param.25) | copy-start | bytes 62212
  135.1 3.1 %collective-permute-start.8 = (f32[16,128]{1,0:T(8,128)S(1)}, f32[16,128]{1,0:T(8,128)S(1)}, u32[]{:S(2)}, u32[]{:S(2)}) collective-permute-start(f32[16,128]{1,0:T(8,128)S(1)} %convert_reduce_fusion), channel_id=1, source_target_pairs={{0,128},{128,0},{1,129},{129,1},{2,130},{130,2},{3,131},{131,3},{4... | collective-permute-start | bytes 24584 | tf_op jit(solution)/shard_map/ppermute | solution.py:341
  137.2 0.7 copy-start.9
  137.8 11.3 %copy-start.3 = (bf16[3,3,16,384]{3,2,1,0:T(8,128)(2,1)S(1)}, bf16[3,3,16,384]{3,2,1,0:T(8,128)(2,1)}, u32[]{:S(2)}) copy-start(bf16[3,3,16,384]{3,2,1,0:T(8,128)(2,1)} %param.23) | copy-start | bytes 331780
  138.3 6.6 %collective-permute-start.10 = (bf16[16,128]{1,0:T(8,128)(2,1)S(1)}, bf16[16,128]{1,0:T(8,128)(2,1)S(1)}, u32[]{:S(2)}, u32[]{:S(2)}) collective-permute-start(bf16[16,128]{1,0:T(8,128)(2,1)S(1)} %get-tuple-element.58.mine_ref), channel_id=1, source_target_pairs={{1,0},{2,1},{3,2},{4,3},{5,4},{6,5},{7,6},{8,7},{9,8},{10,9},{11,1... | collective-permute-start | bytes 12296 | tf_op jit(solution)/shard_map/ppermute | solution.py:351
  141.5 7.6 %collective-permute-start.9 = (bf16[16,128]{1,0:T(8,128)(2,1)S(1)}, bf16[16,128]{1,0:T(8,128)(2,1)S(1)}, u32[]{:S(2)}, u32[]{:S(2)}) collective-permute-start(bf16[16,128]{1,0:T(8,128)(2,1)S(1)} %get-tuple-element.58.mine_ref), channel_id=1, source_target_pairs={{0,1},{1,2},{2,3},{3,4},{4,5},{5,6},{6,7},{7,8},{8,9},{9,10},{10,1... | collective-permute-start | bytes 12296 | tf_op jit(solution)/shard_map/ppermute | solution.py:350

commit v4 on v3

v4 whole, which is shorter than its diff:
```python
import functools
import math

import jax
import jax.numpy as jnp
from jax import lax
from jax.experimental import pallas as pl
from jax.experimental.pallas import tpu as pltpu
from jax.sharding import Mesh
from jax.sharding import PartitionSpec as P

HEAD_DIM = 128

step_size = 0.25
norm_eps = 1e-06
TO_EXP2 = HEAD_DIM ** (-0.5) / math.log(2.0)
BF = jnp.bfloat16
F32 = jnp.float32
VMEM = pl.BlockSpec(memory_space=pltpu.VMEM)
SMEM = pl.BlockSpec(memory_space=pltpu.SMEM)
GRANT = pltpu.CompilerParams(vmem_limit_bytes=12 << 20)


def in_hbm(array):
    return pltpu.with_memory_space_constraint(array, pltpu.HBM)


def dot(a, b, dims, **kw):
    return lax.dot_general(a, b, (dims, ((), ())), preferred_element_type=F32, **kw)


def pack_kernel(core_ref, q_ref, k_ref, v_ref, w_ref, out_ref, q_tmp, k_tmp, v_tmp, w_tmp, sems):
    heads, _, hd = out_ref.shape
    rows = q_tmp.shape[0]
    half = rows // 2
    mine = pl.ds(pl.multiple_of(core_ref[0] * rows, rows), rows)
    copies = [
        pltpu.make_async_copy(w_ref, w_tmp, sems.at[0]),
        pltpu.make_async_copy(v_ref.at[mine, :], v_tmp, sems.at[1]),
        pltpu.make_async_copy(q_ref.at[mine, :], q_tmp, sems.at[2]),
        pltpu.make_async_copy(k_ref.at[mine, :], k_tmp, sems.at[3]),
    ]
    for copy in copies:
        copy.start()
    for copy in copies:
        copy.wait()
    for h in range(heads):
        cols = slice(h * hd, (h + 1) * hd)
        out_ref[h, 0:rows, :] = q_tmp[:, cols]
        out_ref[h, rows : 2 * rows, :] = k_tmp[:, cols]
        projected = dot(v_tmp[:, cols], w_tmp[:, cols], ((1,), (1,)))
        projected = jnp.concatenate([projected[:half], projected[half:]], axis=1)
        out_ref[h, 2 * rows :, :] = projected.astype(BF)


def pack(core, queries, keys, values, weight_t, rows):
    width = queries.shape[1]
    heads = width // HEAD_DIM
    hbm = pl.BlockSpec(memory_space=pltpu.HBM)
    return pl.pallas_call(
        pack_kernel,
        in_specs=[SMEM, hbm, hbm, hbm, hbm],
        out_specs=VMEM,
        out_shape=jax.ShapeDtypeStruct((heads, 2 * rows + rows // 2, HEAD_DIM), BF),
        scratch_shapes=[pltpu.VMEM((rows, width), BF)] * 3
        + [pltpu.VMEM(weight_t.shape, BF), pltpu.SemaphoreType.DMA((4,))],
        name="pack",
        compiler_params=GRANT,
    )(core[None], *(in_hbm(a) for a in (queries, keys, values, weight_t)))


def terms_kernel(order, kb_ref, ms_ref, head_ref, key_ref, mouse_ref, w_ref, bias_ref, term_ref):
    rows_key = jnp.concatenate([key_ref[pl.ds(kb_ref[f], 1)] for f in order], axis=0)
    rows_mouse = jnp.concatenate([mouse_ref[pl.ds(ms_ref[f], 1)] for f in order], axis=0)
    rows_key = rows_key.astype(F32)
    rows_mouse = rows_mouse.astype(F32)
    bias_key, bias_mouse = rows_key[:, 0, :], rows_mouse[:, 0, :]
    bias = [bias_key + bias_mouse, bias_mouse, bias_key, jnp.zeros_like(bias_key)]
    bias_ref[...] = jnp.concatenate(bias, axis=0).astype(BF)
    terms = jnp.concatenate([rows_key[:, 1, :], rows_mouse[:, 1, :]], axis=0).astype(BF)
    term_ref[...] = dot(terms, w_ref[...], ((1,), (1,)))


def action_terms(order, head, keyboard, mouse, key_table, mouse_table, weight_t):
    frames = len(order)
    outs = weight_t.shape[0]
    return pl.pallas_call(
        functools.partial(terms_kernel, order),
        grid_spec=pltpu.PrefetchScalarGridSpec(
            num_scalar_prefetch=3,
            grid=(1,),
            in_specs=[
                pl.BlockSpec(key_table.shape[:2] + (HEAD_DIM,), lambda i, a, b, h: (0, 0, h[0])),
                pl.BlockSpec(mouse_table.shape[:2] + (HEAD_DIM,), lambda i, a, b, h: (0, 0, h[0])),
                pl.BlockSpec((outs, HEAD_DIM), lambda i, a, b, h: (0, h[0])),
            ],
            out_specs=[VMEM, VMEM],
        ),
        out_shape=[
            jax.ShapeDtypeStruct((4 * frames, HEAD_DIM), BF),
            jax.ShapeDtypeStruct((2 * frames, outs), F32),
        ],
        name="terms",
        compiler_params=GRANT,
    )(keyboard, mouse, head[None], key_table, mouse_table, weight_t)


def share_kernel(rows, sets, own_ref, share_ref, sum_ref, top_ref, total_ref):
    heads, _, hd = own_ref.shape
    half = rows // 2
    outs = sum_ref.shape[1]
    query = own_ref[:, 0:rows, :].reshape(heads * rows, hd)
    gathered, per_gather = share_ref.shape[0], heads // sets
    for at in range(gathered):
        for part in range(per_gather):
            frame = at * per_gather + part
            place = slice(part * sets, (part + 1) * sets)
            keys = share_ref[at, place, 0:rows, :].reshape(sets * rows, hd)
            values = share_ref[at, place, rows:, :].reshape(sets * half, hd)
            scores = dot(keys, query, ((1,), (1,)))
            top = jnp.max(scores, axis=0, keepdims=True)
            raised = jnp.exp2((scores - top) * TO_EXP2)
            top_ref[frame : frame + 1, :] = top
            total_ref[frame : frame + 1, :] = jnp.sum(raised, axis=0, keepdims=True)
            raised = raised.reshape(sets, 2, half, -1)
            low = raised[:, 0].reshape(sets * half, -1).astype(BF)
            high = raised[:, 1].reshape(sets * half, -1).astype(BF)
            summed = dot(values[:, :outs], low, ((0,), (0,)))
            sum_ref[frame] = summed + dot(values[:, outs:], high, ((0,), (0,)))


def share_attention(own, share, rows, sets, outs):
    heads = own.shape[0]
    tokens = heads * rows
    frames = share.shape[0] * heads // sets
    keys = frames * sets * rows
    return pl.pallas_call(
        functools.partial(share_kernel, rows, sets),
        in_specs=[VMEM, VMEM],
        out_specs=[VMEM, VMEM, VMEM],
        out_shape=[
            jax.ShapeDtypeStruct((frames, outs, tokens), F32),
            jax.ShapeDtypeStruct((frames, tokens), F32),
            jax.ShapeDtypeStruct((frames, tokens), F32),
        ],
        cost_estimate=pl.CostEstimate(
            flops=2 * tokens * keys * (HEAD_DIM + outs),
            transcendentals=tokens * keys,
            bytes_accessed=1 << 20,
        ),
        name="share",
        compiler_params=GRANT,
    )(own, share)


def guide_kernel(rows, guide_ref, own_ref, bias_ref, term_ref, *refs):
    shares, out_ref = refs[:-1], refs[-1]
    sum_refs, top_refs, total_refs = shares[0::3], shares[1::3], shares[2::3]
    heads, _, hd = own_ref.shape
    half = rows // 2
    count = top_refs[0].shape[0]
    query = own_ref[:, 0:rows, :].reshape(heads * rows, hd)
    shift = dot(bias_ref[...], query, ((1,), (1,)))
    tops = [r[...] for r in top_refs]
    totals = [r[...] for r in total_refs]
    mixes = [None] * len(tops)
    by_key, by_mouse = None, None
    for b in range(4):
        heights = [(top + shift[b * count : (b + 1) * count]) * TO_EXP2 for top in tops]
        peak = functools.reduce(jnp.maximum, heights)
        peak = jnp.max(peak, axis=0, keepdims=True)
        factors = [jnp.exp2(height - peak) for height in heights]
        loads = functools.reduce(jnp.add, [f * t for f, t in zip(factors, totals)])
        scale = guide_ref[b] / jnp.sum(loads, axis=0, keepdims=True)
        parts = [f * scale for f in factors]
        mixes = [p if m is None else m + p for m, p in zip(mixes, parts)]
        loads = loads * scale
        if b % 2 == 0:
            by_key = loads if by_key is None else by_key + loads
        if b < 2:
            by_mouse = loads if by_mouse is None else by_mouse + loads
    loads = jnp.concatenate([by_key, by_mouse], axis=0)
    result = dot(term_ref[...], loads, ((0,), (0,)), precision=lax.Precision.HIGHEST)
    for mix, sum_ref in zip(mixes, sum_refs):
        for frame in range(count):
            result = result + mix[frame : frame + 1, :] * sum_ref[frame]
    by_token = jnp.transpose(result).reshape(heads, 2, half, -1)
    packed = jnp.concatenate([by_token[:, 0], by_token[:, 1]], axis=2)
    out_ref[...] = packed.astype(BF)


def guide(guidance, own, bias, term, shares, rows, outs):
    heads = own.shape[0]
    arrays = [array for share in shares for array in share]
    return pl.pallas_call(
        functools.partial(guide_kernel, rows),
        in_specs=[SMEM] + [VMEM] * (3 + len(arrays)),
        out_specs=VMEM,
        out_shape=jax.ShapeDtypeStruct((heads, rows // 2, 2 * outs), BF),
        name="guide",
        compiler_params=GRANT,
    )(guidance, own, bias, term, *arrays)


def decode_kernel(index_ref, before_ref, mine_ref, after_ref, conv_in_ref, gain_ref, conv_out_ref, out_ref):
    outs = before_ref.shape[1] // 2
    lat = outs // 4
    tokens = before_ref.shape[0] * 2
    left, right = [], []
    for ref in (before_ref, mine_ref, after_ref):
        both = ref[...].astype(F32)
        quarter = tokens // 4
        parts = [both[:quarter], both[quarter:]]
        parts = [p[:, side] for p in parts for side in (slice(0, outs), slice(outs, None))]
        block = jnp.concatenate(parts, axis=0)
        edge = jnp.zeros_like(block[:1])
        earlier = jnp.concatenate([edge, block[:-1]], axis=0)
        later = jnp.concatenate([block[1:], edge], axis=0)
        for dy in range(2):
            at = 2 * lat * dy
            here = block[:, at : at + 2 * lat]
            left.append(jnp.concatenate([earlier[:, at + lat : at + 2 * lat], here], axis=1))
            right.append(jnp.concatenate([here, later[:, at : at + lat]], axis=1))
    height = 4 * tokens
    row = lax.broadcasted_iota(jnp.int32, (height, 1), 0) // tokens
    first, last = index_ref[0] == 0, index_ref[0] == index_ref[1] - 1
    keep = jnp.where((row == 0) & first | (row == 3) & last, 0.0, 1.0)
    taps = []
    for windows in (left, right):
        stack = jnp.concatenate(windows, axis=0).astype(BF)
        features = dot(stack[:height], conv_in_ref[0], ((1,), (0,)))
        for a in range(1, 3):
            part = stack[a * tokens : a * tokens + height]
            features = features + dot(part, conv_in_ref[a], ((1,), (0,)))
        power = jnp.mean(features * features, axis=1, keepdims=True)
        scaled = features * lax.rsqrt(power + norm_eps) * gain_ref[...]
        normed = scaled / (1.0 + jnp.exp(-scaled)) * keep
        taps.append(dot(conv_out_ref[...], normed.astype(BF), ((1,), (1,))))
    even, odd = taps
    step = even.shape[0] // 3
    lane = lax.broadcasted_iota(jnp.int32, (step, height), 1) % tokens
    before = jnp.where(lane == 0, 0.0, pltpu.roll(odd[:step], 1, 1))
    after = jnp.where(lane == tokens - 1, 0.0, pltpu.roll(even[2 * step :], height - 1, 1))
    columns = [
        before + even[step : 2 * step] + odd[2 * step :],
        even[:step] + odd[step : 2 * step] + after,
    ]
    source = lax.broadcasted_iota(jnp.int32, (height, height), 0)
    target = lax.broadcasted_iota(jnp.int32, (height, height), 1)
    colours = None
    for dx, column in enumerate(columns):
        moved = column[0:3]
        for a in range(1, 3):
            moved = moved + pltpu.roll(column[3 * a : 3 * a + 3], height - a * tokens, 1)
        chosen = jnp.where(target == 2 * source + dx, 1.0, 0.0)
        placed = dot(moved, chosen, ((1,), (0,)), precision=lax.Precision.HIGHEST)
        colours = placed if colours is None else colours + placed
    out_ref[:, 0, :] = colours[:, : 2 * tokens]
    out_ref[:, 1, :] = colours[:, 2 * tokens :]


def decode(index, before, mine, after, conv_in, gain, conv_out):
    tokens = before.shape[0] * 2
    return pl.pallas_call(
        decode_kernel,
        in_specs=[SMEM] + [VMEM] * 6,
        out_specs=VMEM,
        out_shape=jax.ShapeDtypeStruct((3, 2, 2 * tokens), F32),
        name="decode",
        compiler_params=GRANT,
    )(index, before, mine, after, conv_in, gain, conv_out)


def shards(
    queries,
    keys,
    values,
    keyboard,
    mouse,
    key_table,
    mouse_table,
    guidance,
    out_weight,
    latent,
    conv_in,
    gain,
    conv_out,
):
    wide, narrow, sets = lax.axis_size("xh"), lax.axis_size("xl"), lax.axis_size("z")
    xh, xl, z = lax.axis_index("xh"), lax.axis_index("xl"), lax.axis_index("z")
    cores = lax.axis_size("branch")
    core = lax.axis_index("branch")
    outs = out_weight.shape[1]
    frames = keyboard.shape[0]
    assert frames == wide * narrow and cores == 2
    rows = queries.shape[0] // cores
    swap = [(0, 1), (1, 0)]

    weight_t = out_weight.T
    packed = pack(core, queries, keys, values, weight_t, rows)
    own = lax.all_to_all(packed, ("xh", "z"), 0, 0, tiled=True)
    share = lax.all_gather(own[:, rows:, :], "xl")
    other_share = lax.ppermute(share, "branch", swap)
    order = tuple(part * narrow + at for at in range(narrow) for part in range(wide))
    bias, term = action_terms(
        order, xh * sets + z, keyboard, mouse, key_table, mouse_table, weight_t
    )
    shares = [share_attention(own, s, rows, sets, outs) for s in (share, other_share)]
    part = guide(guidance, own, bias, term, shares, rows, outs)
    returned = lax.all_to_all(part, ("xh", "z"), 0, 0, tiled=True)
    mine = jnp.sum(returned.astype(F32), axis=0)
    other = lax.ppermute(mine, "branch", swap)
    both = jnp.where(core == 0, jnp.stack([mine, other]), jnp.stack([other, mine]))

    def laid(tokens):
        return tokens.reshape(2, 2, -1, outs).transpose(0, 2, 1, 3).reshape(-1, 2 * outs)

    velocity = both.reshape(2, -1, 2, outs).transpose(0, 2, 1, 3).reshape(-1, outs)
    stepped = (laid(latent) - step_size * both.reshape(-1, 2 * outs)).astype(BF)
    places = ("xh", "xl", "z")
    count = wide * narrow * sets
    index = jnp.stack([(xh * narrow + xl) * sets + z, jnp.int32(count)])
    before = lax.ppermute(stepped, places, [(i, i + 1) for i in range(count - 1)])
    after = lax.ppermute(stepped, places, [(i + 1, i) for i in range(count - 1)])
    taps_in = conv_in.reshape(conv_in.shape[0], -1, conv_in.shape[3])
    taps_out = conv_out.transpose(1, 0, 3, 2).reshape(3, -1, conv_out.shape[2])
    taps_out = jnp.pad(taps_out, ((0, 0), (0, 16 - taps_out.shape[1]), (0, 0)))
    taps_out = taps_out.reshape(-1, conv_out.shape[2])
    colours = decode(index, before, stepped, after, taps_in, gain[None], taps_out)
    return (velocity, colours)


def solution(mesh):
    cores = mesh.shape["branch"]
    tok = mesh.shape["tok"]

    def run(*arrays):
        heads = arrays[0].shape[1] // HEAD_DIM
        sets = heads // cores
        fine = Mesh(
            mesh.devices.reshape(mesh.shape["groups"], cores, cores, tok // heads, sets),
            ("groups", "branch", "xh", "xl", "z"),
        )
        tokens = P(("groups", "xh", "xl", "z"), None)
        placed = (
            tokens,
            tokens,
            tokens,
            P("groups"),
            P("groups"),
            P(),
            P(),
            P(),
            P(),
            tokens,
            P(),
            P(),
            P(),
        )
        return jax.shard_map(
            shards,
            mesh=fine,
            in_specs=placed,
            out_specs=(tokens, P(None, ("groups", "xh", "xl", "z"), None)),
            check_vma=False,
        )(*arrays)

    return run
```

time: 152 us -> 148 us (0.974)
  the two profiles are of different devices: /device:TPU:68 before, /device:TPU:80 now
where the time goes in v4:
time: 148 us; the launch traced here: 147 us
  blocking collectives  95.3 us (64%)
  waiting for transfers between devices  22 us (15%)
  Pallas kernels  12.9 us (9%)
  starting transfers between devices  12.7 us (9%)
  local copies, waits for them, and re-layouts  2.92 us (2%)
    all_to_all x1, blocking collectives, shards(): own = lax.all_to_all(packed, ('xh', 'z'), 0, 0, tiled=True)  77.9 us
    all_to_all x1, waiting for transfers between devices, shards(): returned = lax.all_to_all(part, ('xh', 'z'), 0, 0, tiled=True)  18.4 us
    all_gather x1, blocking collectives, shards(): share = lax.all_gather(own[:, rows:, :], 'xl')  17.5 us
    pallas_call x2, Pallas kernels, share_attention(): pl.pallas_call(functools.partial(share_kernel, rows, sets), in_specs=[VME...  6.05 us
    all_to_all x1, starting transfers between devices, shards(): returned = lax.all_to_all(part, ('xh', 'z'), 0, 0, tiled=True)  4.76 us
    ppermute x1, waiting for transfers between devices, shards(): lax.ppermute(stepped, places, [(i + 1, i) for i in range(count - 1)])  3.52 us
  transfers between devices with their start and end apart: 5, of which 2 were waited for; matrix products, arithmetic and copies ran while one was open for 1% of the time, Pallas kernels for 3%

profile of v4, /device:TPU:80, one launch (start us, length us, event | category | flops | bytes accessed | tf_op | source)
XLA Modules:
  0.0 147.4 jit_solution(7488960709061658448)
XLA Ops:
  0.6 1.7 %pack.1 = bf16[32,40,128]{2,1,0:T(8,128)(2,1)S(1)} custom-call(s32[1]{0:T(128)} %bitcast.core_ref, bf16[32,4096]{1,0:T(8,128)(2,1)} %q_ref.1, bf16[32,4096]{1,0:T(8,128)(2,1)} %k_ref.1, bf16[32,4096]{1,0:T(8,128)(2,1)} %v_ref.1, bf16[64,4096]{1,0:T(8,128)(2,1)} %bitcast.24), custom_call_target="tpu_custom_call" | custom-call | tf_op jit(solution)/shard_map/pack/pallas_call | solution.py:60
  2.3 77.9 %all_to_all.10.own_ref = bf16[32,40,128]{2,1,0:T(8,128)(2,1)S(1)} all-to-all(bf16[32,40,128]{2,1,0:T(8,128)(2,1)S(1)} %pack.1), channel_id=1, replica_groups=mesh['groups'=2,'branch'=2,'xh'=2,'xl'=4,'z'=16] {'xh','z'}, dimensions={0} | all-to-all | bytes 655360 | tf_op jit(solution)/shard_map/all_to_all | solution.py:301
  80.2 0.0 copy-start.1
  80.2 0.0 copy-start
  80.2 0.0 copy-start.2
  80.3 17.5 %all-gather = bf16[128,24,128]{2,1,0:T(8,128)(2,1)S(1)} all-gather(bf16[32,24,128]{2,1,0:T(8,128)(2,1)S(1)} %slice.4), channel_id=2, replica_groups=mesh['groups'=2,'branch'=2,'xh'=2,'xl'=4,'z'=16] {'xl'}, dimensions={0}, use_global_device_ids=true | all-gather | bytes 983040 | tf_op jit(solution)/shard_map/all_gather | solution.py:302
  97.7 1.9 %collective-permute-start = (bf16[4,32,24,128]{3,2,1,0:T(8,128)(2,1)S(1)}, bf16[4,32,24,128]{3,2,1,0:T(8,128)(2,1)S(1)}, u32[]{:S(2)}, u32[]{:S(2)}) collective-permute-start(bf16[4,32,24,128]{3,2,1,0:T(8,128)(2,1)S(1)} %bitcast.26), channel_id=1, source_target_pairs={{0,128},{128,0},{1,129},{129,1},{2,130},{130,2},{3,131},{131,3},{4... | collective-permute-start | bytes 2359304 | tf_op jit(solution)/shard_map/ppermute | solution.py:303
  99.7 0.0 copy-start.4
  99.7 0.0 copy-start.5
  99.7 0.0 copy-done.1
  99.7 0.0 copy-done
  99.7 0.0 copy-done.2
  99.7 0.6 copy-done.4
  100.3 0.0 copy-done.5
  100.3 0.7 terms.1
  101.1 3.0 %share.2 = (f32[8,64,512]{2,1,0:T(8,128)S(1)}, f32[8,512]{1,0:T(8,128)S(1)}, f32[8,512]{1,0:T(8,128)S(1)}) custom-call(bf16[32,40,128]{2,1,0:T(8,128)(2,1)S(1)} %all_to_all.10.own_ref, bf16[4,32,24,128]{3,2,1,0:T(8,128)(2,1)S(1)} %bitcast.27), custom_call_target="tpu_custom_call" | custom-call | flops 402653184 | bytes 1048576 | tf_op jit(solution)/shard_map/share/pallas_call | solution.py:137
  104.1 0.0 collective-permute-done.share_ref
  104.1 3.0 %share.3 = (f32[8,64,512]{2,1,0:T(8,128)S(1)}, f32[8,512]{1,0:T(8,128)S(1)}, f32[8,512]{1,0:T(8,128)S(1)}) custom-call(bf16[32,40,128]{2,1,0:T(8,128)(2,1)S(1)} %all_to_all.10.own_ref, bf16[4,32,24,128]{3,2,1,0:T(8,128)(2,1)S(1)} %collective-permute-done.share_ref), custom_call_target="tpu_custom_call" | custom-call | flops 402653184 | bytes 1048576 | tf_op jit(solution)/shard_map/share/pallas_call | solution.py:137
  107.1 0.0 copy-start.6
  107.1 0.6 copy-done.6
  107.8 1.9 %guide.1 = bf16[32,8,128]{2,1,0:T(8,128)(2,1)} custom-call(f32[4]{0:T(128)S(1)} %copy-done.6, bf16[32,40,128]{2,1,0:T(8,128)(2,1)S(1)} %all_to_all.10.own_ref, bf16[32,128]{1,0:T(8,128)(2,1)S(1)} %get-tuple-element.10.bias_ref, f32[16,64]{1,0:T(8,128)S(1)} %get-tuple-element.11.term_ref, f32[8,64,512]{2,1,0:T(8,128)S(1)} %get-tuple-element.12.refs_0_, ...), custom_call_target="tpu_custom_call" | custom-call | tf_op jit(solution)/shard_map/guide/pallas_call | solution.py:195
  109.7 4.8 %all-to-all-start.1 = ((bf16[32,8,128]{2,1,0:T(8,128)(2,1)}), bf16[32,8,128]{2,1,0:T(8,128)(2,1)S(1)}, u32[]{:S(2)}, u32[]{:S(2)}) async-start(bf16[32,8,128]{2,1,0:T(8,128)(2,1)} %guide.1), calls=%async_computation.1 | async-start | bytes 131072 | tf_op jit(solution)/shard_map/all_to_all | solution.py:310
  114.5 18.4 %all-to-all-done.1 = bf16[32,8,128]{2,1,0:T(8,128)(2,1)S(1)} async-done(((bf16[32,8,128]{2,1,0:T(8,128)(2,1)}), bf16[32,8,128]{2,1,0:T(8,128)(2,1)S(1)}, u32[]{:S(2)}, u32[]{:S(2)}) %all-to-all-start.1) | async-done | bytes 65568 | tf_op jit(solution)/shard_map/all_to_all | solution.py:310
  132.9 0.0 copy-start.8
  132.9 1.9 %collective-permute-start.1 = (f32[8,128]{1,0:T(8,128)S(1)}, f32[8,128]{1,0:T(8,128)S(1)}, u32[]{:S(2)}, u32[]{:S(2)}) collective-permute-start(f32[8,128]{1,0:T(8,128)S(1)} %convert_reduce_fusion), channel_id=1, source_target_pairs={{0,128},{128,0},{1,129},{129,1},{2,130},{130,2},{3,131},{131,3},{4... | collective-permute-start | bytes 12296 | tf_op jit(solution)/shard_map/ppermute | solution.py:312
  134.9 0.1 pad_add_fusion.index_ref
  135.0 0.0 copy-done.8
  135.0 0.0 copy-start.7
  135.0 0.1 reshape.40
  135.1 0.6 copy-done.7
  135.7 0.0 copy-start.9
  135.8 0.7 copy-done.9
  136.4 0.0 copy-start.3
  136.4 0.1 stack.28
  136.5 0.0 collective-permute-done.1
  136.5 2.7 %collective-permute-start.2 = (bf16[16,128]{1,0:T(8,128)(2,1)S(1)}, bf16[16,128]{1,0:T(8,128)(2,1)S(1)}, u32[]{:S(2)}, u32[]{:S(2)}) collective-permute-start(bf16[16,128]{1,0:T(8,128)(2,1)S(1)} %fusion.3.mine_ref), channel_id=1, source_target_pairs={{0,1},{1,2},{2,3},{3,4},{4,5},{5,6},{6,7},{7,8},{8,9},{9,10},{10,1... | collective-permute-start | bytes 12296 | tf_op jit(solution)/shard_map/ppermute | solution.py:323
  139.3 1.3 collective-permute-start.3
  140.6 0.1 stack.29
  140.7 0.6 maximum_select_fusion
  141.3 0.0 collective-permute-done.2.before_ref
  141.3 3.5 %collective-permute-done.3.after_ref = bf16[16,128]{1,0:T(8,128)(2,1)S(1)} collective-permute-done((bf16[16,128]{1,0:T(8,128)(2,1)S(1)}, bf16[16,128]{1,0:T(8,128)(2,1)S(1)}, u32[]{:S(2)}, u32[]{:S(2)}) %collective-permute-start.3) | collective-permute-done | bytes 4128 | tf_op jit(solution)/shard_map/ppermute | solution.py:324
  144.8 0.0 copy-done.3
  144.8 2.6 %decode.1 = f32[3,2,64]{2,1,0:T(2,128)} custom-call(s32[2]{0:T(128)S(1)} %pad_add_fusion.index_ref, bf16[16,128]{1,0:T(8,128)(2,1)S(1)} %collective-permute-done.2.before_ref, bf16[16,128]{1,0:T(8,128)(2,1)S(1)} %fusion.3.mine_ref, bf16[16,128]{1,0:T(8,128)(2,1)S(1)} %collective-permute-done.3.after_ref, bf16[3,48,384]{2,1,0:T(8,128)(2,1)S(1)} %bitcast.29, ...), custom_call_target="tpu_custom_call" | custom-call | tf_op jit(solution)/shard_map/decode/pallas_call | solution.py:264
  (10 shorter events, 0.1 us)
Async XLA Ops:
  80.2 19.5 %copy-start.1 = (bf16[32,2,4096]{2,1,0:T(2,128)(2,1)S(1)}, bf16[32,2,4096]{2,1,0:T(2,128)(2,1)}, u32[]{:S(2)}) copy-start(bf16[32,2,4096]{2,1,0:T(2,128)(2,1)} %mouse_ref.1) | copy-start | bytes 1572868
  80.2 19.5 %copy-start = (bf16[4096,64]{0,1:T(8,128)(2,1)S(1)}, bf16[4096,64]{0,1:T(8,128)(2,1)}, u32[]{:S(2)}) copy-start(bf16[4096,64]{0,1:T(8,128)(2,1)} %param.21) | copy-start | bytes 1572868
  80.2 19.5 %copy-start.2 = (bf16[16,2,4096]{2,1,0:T(2,128)(2,1)S(1)}, bf16[16,2,4096]{2,1,0:T(2,128)(2,1)}, u32[]{:S(2)}) copy-start(bf16[16,2,4096]{2,1,0:T(2,128)(2,1)} %key_ref.1) | copy-start | bytes 786436
  97.7 6.4 %collective-permute-start = (bf16[4,32,24,128]{3,2,1,0:T(8,128)(2,1)S(1)}, bf16[4,32,24,128]{3,2,1,0:T(8,128)(2,1)S(1)}, u32[]{:S(2)}, u32[]{:S(2)}) collective-permute-start(bf16[4,32,24,128]{3,2,1,0:T(8,128)(2,1)S(1)} %bitcast.26), channel_id=1, source_target_pairs={{0,128},{128,0},{1,129},{129,1},{2,130},{130,2},{3,131},{131,3},{4... | collective-permute-start | bytes 2359304 | tf_op jit(solution)/shard_map/ppermute | solution.py:303
  99.7 0.7 copy-start.4
  99.7 0.7 copy-start.5
  107.1 0.7 copy-start.6
  109.7 23.2 %all-to-all-start.1 = ((bf16[32,8,128]{2,1,0:T(8,128)(2,1)}), bf16[32,8,128]{2,1,0:T(8,128)(2,1)S(1)}, u32[]{:S(2)}, u32[]{:S(2)}) async-start(bf16[32,8,128]{2,1,0:T(8,128)(2,1)} %guide.1), calls=%async_computation.1 | async-start | bytes 131072 | tf_op jit(solution)/shard_map/all_to_all | solution.py:310
  132.9 2.1 %copy-start.8 = (f32[32,64]{1,0:T(8,128)S(1)}, f32[32,64]{1,0:T(8,128)}, u32[]{:S(2)}) copy-start(f32[32,64]{1,0:T(8,128)} %param.22) | copy-start | bytes 24580
  132.9 3.6 %collective-permute-start.1 = (f32[8,128]{1,0:T(8,128)S(1)}, f32[8,128]{1,0:T(8,128)S(1)}, u32[]{:S(2)}, u32[]{:S(2)}) collective-permute-start(f32[8,128]{1,0:T(8,128)S(1)} %convert_reduce_fusion), channel_id=1, source_target_pairs={{0,128},{128,0},{1,129},{129,1},{2,130},{130,2},{3,131},{131,3},{4... | collective-permute-start | bytes 12296 | tf_op jit(solution)/shard_map/ppermute | solution.py:312
  135.0 0.7 copy-start.7
  135.7 0.7 copy-start.9
  136.4 8.4 %copy-start.3 = (bf16[3,3,16,384]{3,2,1,0:T(8,128)(2,1)S(1)}, bf16[3,3,16,384]{3,2,1,0:T(8,128)(2,1)}, u32[]{:S(2)}) copy-start(bf16[3,3,16,384]{3,2,1,0:T(8,128)(2,1)} %param.23) | copy-start | bytes 331780
  136.5 4.8 %collective-permute-start.2 = (bf16[16,128]{1,0:T(8,128)(2,1)S(1)}, bf16[16,128]{1,0:T(8,128)(2,1)S(1)}, u32[]{:S(2)}, u32[]{:S(2)}) collective-permute-start(bf16[16,128]{1,0:T(8,128)(2,1)S(1)} %fusion.3.mine_ref), channel_id=1, source_target_pairs={{0,1},{1,2},{2,3},{3,4},{4,5},{5,6},{6,7},{7,8},{8,9},{9,10},{10,1... | collective-permute-start | bytes 12296 | tf_op jit(solution)/shard_map/ppermute | solution.py:323
  139.3 5.5 %collective-permute-start.3 = (bf16[16,128]{1,0:T(8,128)(2,1)S(1)}, bf16[16,128]{1,0:T(8,128)(2,1)S(1)}, u32[]{:S(2)}, u32[]{:S(2)}) collective-permute-start(bf16[16,128]{1,0:T(8,128)(2,1)S(1)} %fusion.3.mine_ref), channel_id=1, source_target_pairs={{1,0},{2,1},{3,2},{4,3},{5,4},{6,5},{7,6},{8,7},{9,8},{10,9},{11,1... | collective-permute-start | bytes 12296 | tf_op jit(solution)/shard_map/ppermute | solution.py:324

commit v5 on v4

--- a/solution.py
+++ b/solution.py
@@ -301,7 +301,7 @@
     own = lax.all_to_all(packed, ("xh", "z"), 0, 0, tiled=True)
     share = lax.all_gather(own[:, rows:, :], "xl")
     other_share = lax.ppermute(share, "branch", swap)
-    order = tuple(part * narrow + at for at in range(narrow) for part in range(wide))
+    order = tuple(range(frames))
     bias, term = action_terms(
         order, xh * sets + z, keyboard, mouse, key_table, mouse_table, weight_t
     )
@@ -317,9 +317,9 @@
 
     velocity = both.reshape(2, -1, 2, outs).transpose(0, 2, 1, 3).reshape(-1, outs)
     stepped = (laid(latent) - step_size * both.reshape(-1, 2 * outs)).astype(BF)
-    places = ("xh", "xl", "z")
+    places = ("xl", "xh", "z")
     count = wide * narrow * sets
-    index = jnp.stack([(xh * narrow + xl) * sets + z, jnp.int32(count)])
+    index = jnp.stack([(xl * wide + xh) * sets + z, jnp.int32(count)])
     before = lax.ppermute(stepped, places, [(i, i + 1) for i in range(count - 1)])
     after = lax.ppermute(stepped, places, [(i + 1, i) for i in range(count - 1)])
     taps_in = conv_in.reshape(conv_in.shape[0], -1, conv_in.shape[3])
@@ -338,10 +338,10 @@
         heads = arrays[0].shape[1] // HEAD_DIM
         sets = heads // cores
         fine = Mesh(
-            mesh.devices.reshape(mesh.shape["groups"], cores, cores, tok // heads, sets),
-            ("groups", "branch", "xh", "xl", "z"),
+            mesh.devices.reshape(mesh.shape["groups"], cores, tok // heads, cores, sets),
+            ("groups", "branch", "xl", "xh", "z"),
         )
-        tokens = P(("groups", "xh", "xl", "z"), None)
+        tokens = P(("groups", "xl", "xh", "z"), None)
         placed = (
             tokens,
             tokens,
@@ -361,7 +361,7 @@
             shards,
             mesh=fine,
             in_specs=placed,
-            out_specs=(tokens, P(None, ("groups", "xh", "xl", "z"), None)),
+            out_specs=(tokens, P(None, ("groups", "xl", "xh", "z"), None)),
             check_vma=False,
         )(*arrays)
 

time: 148 us -> 139 us (0.939)
  blocking collectives: 95.3 us -> 90.2 us
  waiting for transfers between devices: 22 us -> 18 us
    all_to_all x1, blocking collectives: 77.9 us -> 69.6 us  [shards(): own = lax.all_to_all(packed, ('xh', 'z'), 0, 0, tiled=True)]
    all_to_all x1, waiting for transfers between devices: 18.4 us -> 14.5 us  [shards(): returned = lax.all_to_all(part, ('xh', 'z'), 0, 0, tiled=True)]
    all_gather x1, blocking collectives: 17.5 us -> 20.6 us  [shards(): share = lax.all_gather(own[:, rows:, :], 'xl')]
where the time goes in v5:
time: 139 us; the launch traced here: 138 us
  blocking collectives  90.2 us (65%)
  waiting for transfers between devices  18 us (13%)
  Pallas kernels  12.9 us (9%)
  starting transfers between devices  12.7 us (9%)
  local copies, waits for them, and re-layouts  2.92 us (2%)
    all_to_all x1, blocking collectives, shards(): own = lax.all_to_all(packed, ('xh', 'z'), 0, 0, tiled=True)  69.6 us
    all_gather x1, blocking collectives, shards(): share = lax.all_gather(own[:, rows:, :], 'xl')  20.6 us
    all_to_all x1, waiting for transfers between devices, shards(): returned = lax.all_to_all(part, ('xh', 'z'), 0, 0, tiled=True)  14.5 us
    pallas_call x2, Pallas kernels, share_attention(): pl.pallas_call(functools.partial(share_kernel, rows, sets), in_specs=[VME...  6.05 us
    all_to_all x1, starting transfers between devices, shards(): returned = lax.all_to_all(part, ('xh', 'z'), 0, 0, tiled=True)  4.86 us
    ppermute x1, waiting for transfers between devices, shards(): lax.ppermute(stepped, places, [(i + 1, i) for i in range(count - 1)])  3.52 us
  transfers between devices with their start and end apart: 5, of which 2 were waited for; matrix products, arithmetic and copies ran while one was open for 1% of the time, Pallas kernels for 3%

profile of v5, /device:TPU:80, one launch (start us, length us, event | category | flops | bytes accessed | tf_op | source)
XLA Modules:
  0.0 138.3 jit_solution(11984703306558882295)
XLA Ops:
  0.6 1.7 %pack.1 = bf16[32,40,128]{2,1,0:T(8,128)(2,1)S(1)} custom-call(s32[1]{0:T(128)} %bitcast.core_ref, bf16[32,4096]{1,0:T(8,128)(2,1)} %q_ref.1, bf16[32,4096]{1,0:T(8,128)(2,1)} %k_ref.1, bf16[32,4096]{1,0:T(8,128)(2,1)} %v_ref.1, bf16[64,4096]{1,0:T(8,128)(2,1)} %bitcast.24), custom_call_target="tpu_custom_call" | custom-call | tf_op jit(solution)/shard_map/pack/pallas_call | solution.py:60
  2.3 69.6 %all_to_all.10.own_ref = bf16[32,40,128]{2,1,0:T(8,128)(2,1)S(1)} all-to-all(bf16[32,40,128]{2,1,0:T(8,128)(2,1)S(1)} %pack.1), channel_id=1, replica_groups=mesh['groups'=2,'branch'=2,'xl'=4,'xh'=2,'z'=16] {'xh','z'}, dimensions={0} | all-to-all | bytes 655360 | tf_op jit(solution)/shard_map/all_to_all | solution.py:301
  71.9 0.0 copy-start.1
  71.9 0.0 copy-start
  71.9 0.0 copy-start.2
  71.9 20.6 %all-gather = bf16[128,24,128]{2,1,0:T(8,128)(2,1)S(1)} all-gather(bf16[32,24,128]{2,1,0:T(8,128)(2,1)S(1)} %slice.4), channel_id=2, replica_groups=mesh['groups'=2,'branch'=2,'xl'=4,'xh'=2,'z'=16] {'xl'}, dimensions={0}, use_global_device_ids=true | all-gather | bytes 983040 | tf_op jit(solution)/shard_map/all_gather | solution.py:302
  92.6 1.9 %collective-permute-start = (bf16[4,32,24,128]{3,2,1,0:T(8,128)(2,1)S(1)}, bf16[4,32,24,128]{3,2,1,0:T(8,128)(2,1)S(1)}, u32[]{:S(2)}, u32[]{:S(2)}) collective-permute-start(bf16[4,32,24,128]{3,2,1,0:T(8,128)(2,1)S(1)} %bitcast.26), channel_id=1, source_target_pairs={{0,128},{128,0},{1,129},{129,1},{2,130},{130,2},{3,131},{131,3},{4... | collective-permute-start | bytes 2359304 | tf_op jit(solution)/shard_map/ppermute | solution.py:303
  94.5 0.0 copy-start.4
  94.6 0.0 copy-start.5
  94.6 0.0 copy-done.1
  94.6 0.0 copy-done
  94.6 0.0 copy-done.2
  94.6 0.6 copy-done.4
  95.2 0.0 copy-done.5
  95.2 0.7 terms.1
  95.9 3.0 %share.2 = (f32[8,64,512]{2,1,0:T(8,128)S(1)}, f32[8,512]{1,0:T(8,128)S(1)}, f32[8,512]{1,0:T(8,128)S(1)}) custom-call(bf16[32,40,128]{2,1,0:T(8,128)(2,1)S(1)} %all_to_all.10.own_ref, bf16[4,32,24,128]{3,2,1,0:T(8,128)(2,1)S(1)} %bitcast.27), custom_call_target="tpu_custom_call" | custom-call | flops 402653184 | bytes 1048576 | tf_op jit(solution)/shard_map/share/pallas_call | solution.py:137
  99.0 0.0 collective-permute-done.share_ref
  99.0 3.0 %share.3 = (f32[8,64,512]{2,1,0:T(8,128)S(1)}, f32[8,512]{1,0:T(8,128)S(1)}, f32[8,512]{1,0:T(8,128)S(1)}) custom-call(bf16[32,40,128]{2,1,0:T(8,128)(2,1)S(1)} %all_to_all.10.own_ref, bf16[4,32,24,128]{3,2,1,0:T(8,128)(2,1)S(1)} %collective-permute-done.share_ref), custom_call_target="tpu_custom_call" | custom-call | flops 402653184 | bytes 1048576 | tf_op jit(solution)/shard_map/share/pallas_call | solution.py:137
  102.0 0.0 copy-start.6
  102.0 0.6 copy-done.6
  102.7 1.9 %guide.1 = bf16[32,8,128]{2,1,0:T(8,128)(2,1)} custom-call(f32[4]{0:T(128)S(1)} %copy-done.6, bf16[32,40,128]{2,1,0:T(8,128)(2,1)S(1)} %all_to_all.10.own_ref, bf16[32,128]{1,0:T(8,128)(2,1)S(1)} %get-tuple-element.10.bias_ref, f32[16,64]{1,0:T(8,128)S(1)} %get-tuple-element.11.term_ref, f32[8,64,512]{2,1,0:T(8,128)S(1)} %get-tuple-element.12.refs_0_, ...), custom_call_target="tpu_custom_call" | custom-call | tf_op jit(solution)/shard_map/guide/pallas_call | solution.py:195
  104.6 4.9 %all-to-all-start.1 = ((bf16[32,8,128]{2,1,0:T(8,128)(2,1)}), bf16[32,8,128]{2,1,0:T(8,128)(2,1)S(1)}, u32[]{:S(2)}, u32[]{:S(2)}) async-start(bf16[32,8,128]{2,1,0:T(8,128)(2,1)} %guide.1), calls=%async_computation.1 | async-start | bytes 131072 | tf_op jit(solution)/shard_map/all_to_all | solution.py:310
  109.5 14.5 %all-to-all-done.1 = bf16[32,8,128]{2,1,0:T(8,128)(2,1)S(1)} async-done(((bf16[32,8,128]{2,1,0:T(8,128)(2,1)}), bf16[32,8,128]{2,1,0:T(8,128)(2,1)S(1)}, u32[]{:S(2)}, u32[]{:S(2)}) %all-to-all-start.1) | async-done | bytes 65568 | tf_op jit(solution)/shard_map/all_to_all | solution.py:310
  123.9 0.0 copy-start.8
  123.9 1.9 %collective-permute-start.1 = (f32[8,128]{1,0:T(8,128)S(1)}, f32[8,128]{1,0:T(8,128)S(1)}, u32[]{:S(2)}, u32[]{:S(2)}) collective-permute-start(f32[8,128]{1,0:T(8,128)S(1)} %convert_reduce_fusion), channel_id=1, source_target_pairs={{0,128},{128,0},{1,129},{129,1},{2,130},{130,2},{3,131},{131,3},{4... | collective-permute-start | bytes 12296 | tf_op jit(solution)/shard_map/ppermute | solution.py:312
  125.9 0.1 pad_add_fusion.index_ref
  126.0 0.0 copy-done.8
  126.0 0.0 copy-start.7
  126.0 0.1 reshape.40
  126.1 0.6 copy-done.7
  126.7 0.0 copy-start.9
  126.8 0.7 copy-done.9
  127.4 0.0 copy-start.3
  127.4 0.1 stack.28
  127.5 0.0 collective-permute-done.1
  127.5 2.7 %collective-permute-start.2 = (bf16[16,128]{1,0:T(8,128)(2,1)S(1)}, bf16[16,128]{1,0:T(8,128)(2,1)S(1)}, u32[]{:S(2)}, u32[]{:S(2)}) collective-permute-start(bf16[16,128]{1,0:T(8,128)(2,1)S(1)} %fusion.3.mine_ref), channel_id=1, source_target_pairs={{0,1},{1,2},{2,3},{3,4},{4,5},{5,6},{6,7},{7,8},{8,9},{9,10},{10,1... | collective-permute-start | bytes 12296 | tf_op jit(solution)/shard_map/ppermute | solution.py:323
  130.2 1.3 collective-permute-start.3
  131.6 0.1 stack.29
  131.6 0.6 maximum_select_fusion
  132.2 0.0 collective-permute-done.2.before_ref
  132.3 3.5 %collective-permute-done.3.after_ref = bf16[16,128]{1,0:T(8,128)(2,1)S(1)} collective-permute-done((bf16[16,128]{1,0:T(8,128)(2,1)S(1)}, bf16[16,128]{1,0:T(8,128)(2,1)S(1)}, u32[]{:S(2)}, u32[]{:S(2)}) %collective-permute-start.3) | collective-permute-done | bytes 4128 | tf_op jit(solution)/shard_map/ppermute | solution.py:324
  135.8 0.0 copy-done.3
  135.8 2.6 %decode.1 = f32[3,2,64]{2,1,0:T(2,128)} custom-call(s32[2]{0:T(128)S(1)} %pad_add_fusion.index_ref, bf16[16,128]{1,0:T(8,128)(2,1)S(1)} %collective-permute-done.2.before_ref, bf16[16,128]{1,0:T(8,128)(2,1)S(1)} %fusion.3.mine_ref, bf16[16,128]{1,0:T(8,128)(2,1)S(1)} %collective-permute-done.3.after_ref, bf16[3,48,384]{2,1,0:T(8,128)(2,1)S(1)} %bitcast.29, ...), custom_call_target="tpu_custom_call" | custom-call | tf_op jit(solution)/shard_map/decode/pallas_call | solution.py:264
  (10 shorter events, 0.1 us)
Async XLA Ops:
  71.9 22.7 %copy-start.1 = (bf16[32,2,4096]{2,1,0:T(2,128)(2,1)S(1)}, bf16[32,2,4096]{2,1,0:T(2,128)(2,1)}, u32[]{:S(2)}) copy-start(bf16[32,2,4096]{2,1,0:T(2,128)(2,1)} %mouse_ref.1) | copy-start | bytes 1572868
  71.9 22.7 %copy-start = (bf16[4096,64]{0,1:T(8,128)(2,1)S(1)}, bf16[4096,64]{0,1:T(8,128)(2,1)}, u32[]{:S(2)}) copy-start(bf16[4096,64]{0,1:T(8,128)(2,1)} %param.21) | copy-start | bytes 1572868
  71.9 22.7 %copy-start.2 = (bf16[16,2,4096]{2,1,0:T(2,128)(2,1)S(1)}, bf16[16,2,4096]{2,1,0:T(2,128)(2,1)}, u32[]{:S(2)}) copy-start(bf16[16,2,4096]{2,1,0:T(2,128)(2,1)} %key_ref.1) | copy-start | bytes 786436
  92.6 6.4 %collective-permute-start = (bf16[4,32,24,128]{3,2,1,0:T(8,128)(2,1)S(1)}, bf16[4,32,24,128]{3,2,1,0:T(8,128)(2,1)S(1)}, u32[]{:S(2)}, u32[]{:S(2)}) collective-permute-start(bf16[4,32,24,128]{3,2,1,0:T(8,128)(2,1)S(1)} %bitcast.26), channel_id=1, source_target_pairs={{0,128},{128,0},{1,129},{129,1},{2,130},{130,2},{3,131},{131,3},{4... | collective-permute-start | bytes 2359304 | tf_op jit(solution)/shard_map/ppermute | solution.py:303
  94.5 0.7 copy-start.4
  94.6 0.7 copy-start.5
  102.0 0.7 copy-start.6
  104.6 19.3 %all-to-all-start.1 = ((bf16[32,8,128]{2,1,0:T(8,128)(2,1)}), bf16[32,8,128]{2,1,0:T(8,128)(2,1)S(1)}, u32[]{:S(2)}, u32[]{:S(2)}) async-start(bf16[32,8,128]{2,1,0:T(8,128)(2,1)} %guide.1), calls=%async_computation.1 | async-start | bytes 131072 | tf_op jit(solution)/shard_map/all_to_all | solution.py:310
  123.9 2.1 %copy-start.8 = (f32[32,64]{1,0:T(8,128)S(1)}, f32[32,64]{1,0:T(8,128)}, u32[]{:S(2)}) copy-start(f32[32,64]{1,0:T(8,128)} %param.22) | copy-start | bytes 24580
  123.9 3.6 %collective-permute-start.1 = (f32[8,128]{1,0:T(8,128)S(1)}, f32[8,128]{1,0:T(8,128)S(1)}, u32[]{:S(2)}, u32[]{:S(2)}) collective-permute-start(f32[8,128]{1,0:T(8,128)S(1)} %convert_reduce_fusion), channel_id=1, source_target_pairs={{0,128},{128,0},{1,129},{129,1},{2,130},{130,2},{3,131},{131,3},{4... | collective-permute-start | bytes 12296 | tf_op jit(solution)/shard_map/ppermute | solution.py:312
  126.0 0.7 copy-start.7
  126.7 0.7 copy-start.9
  127.4 8.3 %copy-start.3 = (bf16[3,3,16,384]{3,2,1,0:T(8,128)(2,1)S(1)}, bf16[3,3,16,384]{3,2,1,0:T(8,128)(2,1)}, u32[]{:S(2)}) copy-start(bf16[3,3,16,384]{3,2,1,0:T(8,128)(2,1)} %param.23) | copy-start | bytes 331780
  127.5 4.7 %collective-permute-start.2 = (bf16[16,128]{1,0:T(8,128)(2,1)S(1)}, bf16[16,128]{1,0:T(8,128)(2,1)S(1)}, u32[]{:S(2)}, u32[]{:S(2)}) collective-permute-start(bf16[16,128]{1,0:T(8,128)(2,1)S(1)} %fusion.3.mine_ref), channel_id=1, source_target_pairs={{0,1},{1,2},{2,3},{3,4},{4,5},{5,6},{6,7},{7,8},{8,9},{9,10},{10,1... | collective-permute-start | bytes 12296 | tf_op jit(solution)/shard_map/ppermute | solution.py:323
  130.2 5.5 %collective-permute-start.3 = (bf16[16,128]{1,0:T(8,128)(2,1)S(1)}, bf16[16,128]{1,0:T(8,128)(2,1)S(1)}, u32[]{:S(2)}, u32[]{:S(2)}) collective-permute-start(bf16[16,128]{1,0:T(8,128)(2,1)S(1)} %fusion.3.mine_ref), channel_id=1, source_target_pairs={{1,0},{2,1},{3,2},{4,3},{5,4},{6,5},{7,6},{8,7},{9,8},{10,9},{11,1... | collective-permute-start | bytes 12296 | tf_op jit(solution)/shard_map/ppermute | solution.py:324

commit v6 on v5

--- a/solution.py
+++ b/solution.py
@@ -29,18 +29,40 @@
     return lax.dot_general(a, b, (dims, ((), ())), preferred_element_type=F32, **kw)
 
 
-def pack_kernel(core_ref, q_ref, k_ref, v_ref, w_ref, out_ref, q_tmp, k_tmp, v_tmp, w_tmp, sems):
+def pack_kernel(
+    core_ref, head_ref, q_ref, k_ref, v_ref, w_ref, kb_ref, ms_ref, key_ref, mouse_ref, guide_ref,
+    out_ref, bias_ref, term_ref, line_ref,
+    q_tmp, k_tmp, v_tmp, w_tmp, kb_tmp, ms_tmp, key_tmp, mouse_tmp, guide_tmp, sems,
+):
     heads, _, hd = out_ref.shape
     rows = q_tmp.shape[0]
     half = rows // 2
+    frames = kb_tmp.shape[0]
     mine = pl.ds(pl.multiple_of(core_ref[0] * rows, rows), rows)
+    head = pl.ds(pl.multiple_of(head_ref[0] * hd, hd), hd)
+    ids = [
+        pltpu.make_async_copy(kb_ref, kb_tmp, sems.at[4]),
+        pltpu.make_async_copy(ms_ref, ms_tmp, sems.at[5]),
+        pltpu.make_async_copy(guide_ref, guide_tmp, sems.at[6]),
+    ]
     copies = [
         pltpu.make_async_copy(w_ref, w_tmp, sems.at[0]),
         pltpu.make_async_copy(v_ref.at[mine, :], v_tmp, sems.at[1]),
         pltpu.make_async_copy(q_ref.at[mine, :], q_tmp, sems.at[2]),
         pltpu.make_async_copy(k_ref.at[mine, :], k_tmp, sems.at[3]),
     ]
-    for copy in copies:
+    for copy in ids + copies:
+        copy.start()
+    for copy in ids:
+        copy.wait()
+    picks = []
+    for f in range(frames):
+        at = 7 + 2 * f
+        picks += [
+            pltpu.make_async_copy(key_ref.at[kb_tmp[f], :, head], key_tmp.at[f], sems.at[at]),
+            pltpu.make_async_copy(mouse_ref.at[ms_tmp[f], :, head], mouse_tmp.at[f], sems.at[at + 1]),
+        ]
+    for copy in picks:
         copy.start()
     for copy in copies:
         copy.wait()
@@ -51,58 +73,46 @@
         projected = dot(v_tmp[:, cols], w_tmp[:, cols], ((1,), (1,)))
         projected = jnp.concatenate([projected[:half], projected[half:]], axis=1)
         out_ref[h, 2 * rows :, :] = projected.astype(BF)
-
-
-def pack(core, queries, keys, values, weight_t, rows):
-    width = queries.shape[1]
-    heads = width // HEAD_DIM
-    hbm = pl.BlockSpec(memory_space=pltpu.HBM)
-    return pl.pallas_call(
-        pack_kernel,
-        in_specs=[SMEM, hbm, hbm, hbm, hbm],
-        out_specs=VMEM,
-        out_shape=jax.ShapeDtypeStruct((heads, 2 * rows + rows // 2, HEAD_DIM), BF),
-        scratch_shapes=[pltpu.VMEM((rows, width), BF)] * 3
-        + [pltpu.VMEM(weight_t.shape, BF), pltpu.SemaphoreType.DMA((4,))],
-        name="pack",
-        compiler_params=GRANT,
-    )(core[None], *(in_hbm(a) for a in (queries, keys, values, weight_t)))
-
-
-def terms_kernel(order, kb_ref, ms_ref, head_ref, key_ref, mouse_ref, w_ref, bias_ref, term_ref):
-    rows_key = jnp.concatenate([key_ref[pl.ds(kb_ref[f], 1)] for f in order], axis=0)
-    rows_mouse = jnp.concatenate([mouse_ref[pl.ds(ms_ref[f], 1)] for f in order], axis=0)
-    rows_key = rows_key.astype(F32)
-    rows_mouse = rows_mouse.astype(F32)
+    for copy in picks:
+        copy.wait()
+    rows_key = key_tmp[...].astype(F32)
+    rows_mouse = mouse_tmp[...].astype(F32)
     bias_key, bias_mouse = rows_key[:, 0, :], rows_mouse[:, 0, :]
     bias = [bias_key + bias_mouse, bias_mouse, bias_key, jnp.zeros_like(bias_key)]
     bias_ref[...] = jnp.concatenate(bias, axis=0).astype(BF)
     terms = jnp.concatenate([rows_key[:, 1, :], rows_mouse[:, 1, :]], axis=0).astype(BF)
-    term_ref[...] = dot(terms, w_ref[...], ((1,), (1,)))
-
-
-def action_terms(order, head, keyboard, mouse, key_table, mouse_table, weight_t):
-    frames = len(order)
+    term_ref[...] = dot(terms, w_tmp[:, head], ((1,), (1,)))
+    for b in range(line_ref.shape[0]):
+        line_ref[b : b + 1, :] = jnp.full((1, hd), guide_tmp[b], F32)
+
+
+def pack(
+    core, head, queries, keys, values, weight_t, keyboard, mouse, key_table, mouse_table, guidance, rows
+):
+    width = queries.shape[1]
+    heads = width // HEAD_DIM
+    frames = keyboard.shape[0]
     outs = weight_t.shape[0]
+    arrays = (queries, keys, values, weight_t, keyboard, mouse, key_table, mouse_table, guidance)
     return pl.pallas_call(
-        functools.partial(terms_kernel, order),
-        grid_spec=pltpu.PrefetchScalarGridSpec(
-            num_scalar_prefetch=3,
-            grid=(1,),
-            in_specs=[
-                pl.BlockSpec(key_table.shape[:2] + (HEAD_DIM,), lambda i, a, b, h: (0, 0, h[0])),
-                pl.BlockSpec(mouse_table.shape[:2] + (HEAD_DIM,), lambda i, a, b, h: (0, 0, h[0])),
-                pl.BlockSpec((outs, HEAD_DIM), lambda i, a, b, h: (0, h[0])),
-            ],
-            out_specs=[VMEM, VMEM],
-        ),
+        pack_kernel,
+        in_specs=[SMEM, SMEM] + [pl.BlockSpec(memory_space=pltpu.HBM)] * len(arrays),
+        out_specs=[VMEM] * 4,
         out_shape=[
+            jax.ShapeDtypeStruct((heads, 2 * rows + rows // 2, HEAD_DIM), BF),
             jax.ShapeDtypeStruct((4 * frames, HEAD_DIM), BF),
             jax.ShapeDtypeStruct((2 * frames, outs), F32),
+            jax.ShapeDtypeStruct((guidance.shape[0], HEAD_DIM), F32),
         ],
-        name="terms",
+        scratch_shapes=[pltpu.VMEM((rows, width), BF)] * 3
+        + [pltpu.VMEM(weight_t.shape, BF)]
+        + [pltpu.SMEM((frames,), jnp.int32)] * 2
+        + [pltpu.VMEM((frames, 2, HEAD_DIM), BF)] * 2
+        + [pltpu.SMEM(guidance.shape, F32)]
+        + [pltpu.SemaphoreType.DMA((7 + 2 * frames,))],
+        name="pack",
         compiler_params=GRANT,
-    )(keyboard, mouse, head[None], key_table, mouse_table, weight_t)
+    )(core[None], head[None], *(in_hbm(a) for a in arrays))
 
 
 def share_kernel(rows, sets, own_ref, share_ref, sum_ref, top_ref, total_ref):
@@ -110,23 +120,31 @@
     half = rows // 2
     outs = sum_ref.shape[1]
     query = own_ref[:, 0:rows, :].reshape(heads * rows, hd)
-    gathered, per_gather = share_ref.shape[0], heads // sets
-    for at in range(gathered):
-        for part in range(per_gather):
-            frame = at * per_gather + part
-            place = slice(part * sets, (part + 1) * sets)
-            keys = share_ref[at, place, 0:rows, :].reshape(sets * rows, hd)
-            values = share_ref[at, place, rows:, :].reshape(sets * half, hd)
-            scores = dot(keys, query, ((1,), (1,)))
-            top = jnp.max(scores, axis=0, keepdims=True)
-            raised = jnp.exp2((scores - top) * TO_EXP2)
-            top_ref[frame : frame + 1, :] = top
-            total_ref[frame : frame + 1, :] = jnp.sum(raised, axis=0, keepdims=True)
-            raised = raised.reshape(sets, 2, half, -1)
-            low = raised[:, 0].reshape(sets * half, -1).astype(BF)
-            high = raised[:, 1].reshape(sets * half, -1).astype(BF)
-            summed = dot(values[:, :outs], low, ((0,), (0,)))
-            sum_ref[frame] = summed + dot(values[:, outs:], high, ((0,), (0,)))
+    per_gather = heads // sets
+    frames = share_ref.shape[0] * per_gather
+
+    def scores_of(frame):
+        at, part = frame // per_gather, frame % per_gather
+        keys = share_ref[at, part * sets : (part + 1) * sets, 0:rows, :]
+        return dot(keys.reshape(sets * rows, hd), query, ((1,), (1,)))
+
+    coming = scores_of(0)
+    for frame in range(frames):
+        scores = coming
+        if frame + 1 < frames:
+            coming = scores_of(frame + 1)
+        at, part = frame // per_gather, frame % per_gather
+        values = share_ref[at, part * sets : (part + 1) * sets, rows:, :].reshape(sets * half, hd)
+        values = jnp.concatenate([values[:, :outs], values[:, outs:]], axis=0)
+        top = jnp.max(scores, axis=0, keepdims=True)
+        raised = jnp.exp2((scores - top) * TO_EXP2)
+        top_ref[frame : frame + 1, :] = top
+        total_ref[frame : frame + 1, :] = jnp.sum(raised, axis=0, keepdims=True)
+        raised = raised.reshape(sets, 2, half, -1)
+        low = raised[:, 0].reshape(sets * half, -1)
+        high = raised[:, 1].reshape(sets * half, -1)
+        raised = jnp.concatenate([low, high], axis=0).astype(BF)
+        sum_ref[frame] = dot(values, raised, ((0,), (0,)))
 
 
 def share_attention(own, share, rows, sets, outs):
@@ -171,7 +189,7 @@
         peak = jnp.max(peak, axis=0, keepdims=True)
         factors = [jnp.exp2(height - peak) for height in heights]
         loads = functools.reduce(jnp.add, [f * t for f, t in zip(factors, totals)])
-        scale = guide_ref[b] / jnp.sum(loads, axis=0, keepdims=True)
+        scale = guide_ref[b : b + 1, 0:1] / jnp.sum(loads, axis=0, keepdims=True)
         parts = [f * scale for f in factors]
         mixes = [p if m is None else m + p for m, p in zip(mixes, parts)]
         loads = loads * scale
@@ -194,7 +212,7 @@
     arrays = [array for share in shares for array in share]
     return pl.pallas_call(
         functools.partial(guide_kernel, rows),
-        in_specs=[SMEM] + [VMEM] * (3 + len(arrays)),
+        in_specs=[VMEM] * (4 + len(arrays)),
         out_specs=VMEM,
         out_shape=jax.ShapeDtypeStruct((heads, rows // 2, 2 * outs), BF),
         name="guide",
@@ -291,42 +309,45 @@
     cores = lax.axis_size("branch")
     core = lax.axis_index("branch")
     outs = out_weight.shape[1]
-    frames = keyboard.shape[0]
-    assert frames == wide * narrow and cores == 2
+    assert keyboard.shape[0] == wide * narrow and cores == 2
     rows = queries.shape[0] // cores
     swap = [(0, 1), (1, 0)]
 
     weight_t = out_weight.T
-    packed = pack(core, queries, keys, values, weight_t, rows)
+    packed, bias, term, lines = pack(
+        core, xh * sets + z, queries, keys, values, weight_t,
+        keyboard, mouse, key_table, mouse_table, guidance, rows,
+    )
     own = lax.all_to_all(packed, ("xh", "z"), 0, 0, tiled=True)
     share = lax.all_gather(own[:, rows:, :], "xl")
     other_share = lax.ppermute(share, "branch", swap)
-    order = tuple(range(frames))
-    bias, term = action_terms(
-        order, xh * sets + z, keyboard, mouse, key_table, mouse_table, weight_t
-    )
     shares = [share_attention(own, s, rows, sets, outs) for s in (share, other_share)]
-    part = guide(guidance, own, bias, term, shares, rows, outs)
+    part = guide(lines, own, bias, term, shares, rows, outs)
+    part, latent, conv_out, gain = lax.optimization_barrier((part, latent, conv_out, gain))
     returned = lax.all_to_all(part, ("xh", "z"), 0, 0, tiled=True)
-    mine = jnp.sum(returned.astype(F32), axis=0)
-    other = lax.ppermute(mine, "branch", swap)
-    both = jnp.where(core == 0, jnp.stack([mine, other]), jnp.stack([other, mine]))
 
     def laid(tokens):
         return tokens.reshape(2, 2, -1, outs).transpose(0, 2, 1, 3).reshape(-1, 2 * outs)
 
-    velocity = both.reshape(2, -1, 2, outs).transpose(0, 2, 1, 3).reshape(-1, outs)
-    stepped = (laid(latent) - step_size * both.reshape(-1, 2 * outs)).astype(BF)
-    places = ("xl", "xh", "z")
     count = wide * narrow * sets
     index = jnp.stack([(xl * wide + xh) * sets + z, jnp.int32(count)])
-    before = lax.ppermute(stepped, places, [(i, i + 1) for i in range(count - 1)])
-    after = lax.ppermute(stepped, places, [(i + 1, i) for i in range(count - 1)])
     taps_in = conv_in.reshape(conv_in.shape[0], -1, conv_in.shape[3])
     taps_out = conv_out.transpose(1, 0, 3, 2).reshape(3, -1, conv_out.shape[2])
     taps_out = jnp.pad(taps_out, ((0, 0), (0, 16 - taps_out.shape[1]), (0, 0)))
     taps_out = taps_out.reshape(-1, conv_out.shape[2])
-    colours = decode(index, before, stepped, after, taps_in, gain[None], taps_out)
+    noisy = laid(latent)
+    mine = jnp.sum(returned.astype(F32), axis=0)
+    mine, noisy, taps_out, gain, index = lax.optimization_barrier(
+        (mine, noisy, taps_out, gain[None], index)
+    )
+    other = lax.ppermute(mine, "branch", swap)
+    both = jnp.where(core == 0, jnp.stack([mine, other]), jnp.stack([other, mine]))
+    velocity = both.reshape(2, -1, 2, outs).transpose(0, 2, 1, 3).reshape(-1, outs)
+    stepped = (noisy - step_size * both.reshape(-1, 2 * outs)).astype(BF)
+    places = ("xl", "xh", "z")
+    before = lax.ppermute(stepped, places, [(i, i + 1) for i in range(count - 1)])
+    after = lax.ppermute(stepped, places, [(i + 1, i) for i in range(count - 1)])
+    colours = decode(index, before, stepped, after, taps_in, gain, taps_out)
     return (velocity, colours)
 
 

time: 139 us -> 135 us (0.971); the launches traced: 138 us -> 132 us
  waiting for transfers between devices: 18 us -> 14.7 us
  Pallas kernels: 12.9 us -> 9.62 us
  starting transfers between devices: 12.7 us -> 14.8 us
    ppermute x1, waiting for transfers between devices: 3.52 us -> 0.01 us  [shards(): lax.ppermute(stepped, places, [(i + 1, i) for i in range(count - 1)])]
    pallas_call x2, Pallas kernels: 6.05 us -> 3.65 us  [share_attention(): pl.pallas_call(functools.partial(share_kernel, rows, sets), in_specs=[VME...]
    ppermute x1, starting transfers between devices: 2.69 us -> 4.59 us  [shards(): lax.ppermute(stepped, places, [(i, i + 1) for i in range(count - 1)])]
    all_to_all x1, waiting for transfers between devices: 14.5 us -> 12.6 us  [shards(): returned = lax.all_to_all(part, ('xh', 'z'), 0, 0, tiled=True)]
    pallas_call x3 -> x2, Pallas kernels: 4.3 us -> 3.4 us  [the longest x1 2.02 us: pack(): pl.pallas_call(pack_kernel, in_specs=[SMEM, SMEM] + [pl.BlockSpec(memory_...]
  transfers between devices with their start and end apart: 5 -> 5, of which waited for: 2 -> 4; matrix products, arithmetic and copies ran while one was open for 1% -> 1% of each run, Pallas kernels for 3% -> 1%
where the time goes in v6:
time: 135 us; the launch traced here: 132 us
  blocking collectives  90.1 us (67%)
  starting transfers between devices  14.8 us (11%)
  waiting for transfers between devices  14.7 us (11%)
  Pallas kernels  9.62 us (7%)
  local copies, waits for them, and re-layouts  1.59 us (1%)
    all_to_all x1, blocking collectives, shards(): own = lax.all_to_all(packed, ('xh', 'z'), 0, 0, tiled=True)  69.6 us
    all_gather x1, blocking collectives, shards(): share = lax.all_gather(own[:, rows:, :], 'xl')  20.5 us
    all_to_all x1, waiting for transfers between devices, shards(): returned = lax.all_to_all(part, ('xh', 'z'), 0, 0, tiled=True)  12.6 us
    all_to_all x1, starting transfers between devices, shards(): returned = lax.all_to_all(part, ('xh', 'z'), 0, 0, tiled=True)  4.98 us
    ppermute x1, starting transfers between devices, shards(): lax.ppermute(stepped, places, [(i, i + 1) for i in range(count - 1)])  4.59 us
    pallas_call x2, Pallas kernels, share_attention(): pl.pallas_call(functools.partial(share_kernel, rows, sets), in_specs=[VME...  3.65 us
  transfers between devices with their start and end apart: 5, of which 4 were waited for; matrix products, arithmetic and copies ran while one was open for 1% of the time, Pallas kernels for 1%

profile of v6, /device:TPU:80, one launch (start us, length us, event | category | flops | bytes accessed | tf_op | source)
XLA Modules:
  0.0 132.2 jit_solution(4830762001330812977)
XLA Ops:
  0.6 2.0 %pack.1 = (bf16[32,40,128]{2,1,0:T(8,128)(2,1)S(1)}, bf16[32,128]{1,0:T(8,128)(2,1)S(1)}, f32[16,64]{1,0:T(8,128)S(1)}, f32[4,128]{1,0:T(4,128)S(1)}) custom-call(s32[1]{0:T(128)} %bitcast.core_ref, s32[1]{0:T(128)} %bitcast.1.head_ref, bf16[32,4096]{1,0:T(8,128)(2,1)} %q_ref.1, bf16[32,4096]{1,0:T(8,128)(2,1)} %k_ref.1, bf16[32,4096]{1,0:T(8,128)(2,1)} %v_ref.1, ...), custom_call_target="tpu_custom_call" | custom-call | tf_op jit(solution)/shard_map/pack/pallas_call | solution.py:97
  2.7 69.6 %all_to_all.10.own_ref = bf16[32,40,128]{2,1,0:T(8,128)(2,1)S(1)} all-to-all(bf16[32,40,128]{2,1,0:T(8,128)(2,1)S(1)} %get-tuple-element.22), channel_id=1, replica_groups=mesh['groups'=2,'branch'=2,'xl'=4,'xh'=2,'z'=16] {'xh','z'}, dimensions={0} | all-to-all | bytes 655360 | tf_op jit(solution)/shard_map/all_to_all | solution.py:321
  72.3 20.5 %all-gather = bf16[128,24,128]{2,1,0:T(8,128)(2,1)S(1)} all-gather(bf16[32,24,128]{2,1,0:T(8,128)(2,1)S(1)} %slice.4), channel_id=2, replica_groups=mesh['groups'=2,'branch'=2,'xl'=4,'xh'=2,'z'=16] {'xl'}, dimensions={0}, use_global_device_ids=true | all-gather | bytes 983040 | tf_op jit(solution)/shard_map/all_gather | solution.py:322
  92.8 1.9 %collective-permute-start = (bf16[4,32,24,128]{3,2,1,0:T(8,128)(2,1)S(1)}, bf16[4,32,24,128]{3,2,1,0:T(8,128)(2,1)S(1)}, u32[]{:S(2)}, u32[]{:S(2)}) collective-permute-start(bf16[4,32,24,128]{3,2,1,0:T(8,128)(2,1)S(1)} %bitcast.24), channel_id=1, source_target_pairs={{0,128},{128,0},{1,129},{129,1},{2,130},{130,2},{3,131},{131,3},{4... | collective-permute-start | bytes 2359304 | tf_op jit(solution)/shard_map/ppermute | solution.py:323
  94.7 1.8 %share.2 = (f32[8,64,512]{2,1,0:T(8,128)S(1)}, f32[8,512]{1,0:T(8,128)S(1)}, f32[8,512]{1,0:T(8,128)S(1)}) custom-call(bf16[32,40,128]{2,1,0:T(8,128)(2,1)S(1)} %all_to_all.10.own_ref, bf16[4,32,24,128]{3,2,1,0:T(8,128)(2,1)S(1)} %bitcast.25), custom_call_target="tpu_custom_call" | custom-call | flops 402653184 | bytes 1048576 | tf_op jit(solution)/shard_map/share/pallas_call | solution.py:155
  96.6 0.4 collective-permute-done.share_ref
  97.0 1.8 %share.3 = (f32[8,64,512]{2,1,0:T(8,128)S(1)}, f32[8,512]{1,0:T(8,128)S(1)}, f32[8,512]{1,0:T(8,128)S(1)}) custom-call(bf16[32,40,128]{2,1,0:T(8,128)(2,1)S(1)} %all_to_all.10.own_ref, bf16[4,32,24,128]{3,2,1,0:T(8,128)(2,1)S(1)} %collective-permute-done.share_ref), custom_call_target="tpu_custom_call" | custom-call | flops 402653184 | bytes 1048576 | tf_op jit(solution)/shard_map/share/pallas_call | solution.py:155
  98.8 1.4 %guide.1 = bf16[32,8,128]{2,1,0:T(8,128)(2,1)} custom-call(f32[4,128]{1,0:T(4,128)S(1)} %get-tuple-element.21.guide_ref, bf16[32,40,128]{2,1,0:T(8,128)(2,1)S(1)} %all_to_all.10.own_ref, bf16[32,128]{1,0:T(8,128)(2,1)S(1)} %get-tuple-element.23.bias_ref, f32[16,64]{1,0:T(8,128)S(1)} %get-tuple-element.24.term_ref, ...), custom_call_target="tpu_custom_call" | custom-call | tf_op jit(solution)/shard_map/guide/pallas_call | solution.py:213
  100.2 0.0 copy-start.3
  100.2 5.0 %all-to-all-start.1 = ((bf16[32,8,128]{2,1,0:T(8,128)(2,1)}), bf16[32,8,128]{2,1,0:T(8,128)(2,1)S(1)}, u32[]{:S(2)}, u32[]{:S(2)}) async-start(bf16[32,8,128]{2,1,0:T(8,128)(2,1)} %guide.1), calls=%async_computation.1 | async-start | bytes 131072 | tf_op jit(solution)/shard_map/all_to_all | solution.py:327
  105.2 0.0 copy-start.2
  105.2 0.1 pad_add_fusion.index_ref
  105.3 0.0 copy-done.3
  105.3 0.6 copy-done.2
  105.9 0.0 copy-start.1
  105.9 0.1 reshape.39
  106.0 0.6 copy-done.1
  106.7 0.0 copy-start
  106.7 12.6 %all-to-all-done.1 = bf16[32,8,128]{2,1,0:T(8,128)(2,1)S(1)} async-done(((bf16[32,8,128]{2,1,0:T(8,128)(2,1)}), bf16[32,8,128]{2,1,0:T(8,128)(2,1)S(1)}, u32[]{:S(2)}, u32[]{:S(2)}) %all-to-all-start.1) | async-done | bytes 65568 | tf_op jit(solution)/shard_map/all_to_all | solution.py:327
  119.4 1.9 %collective-permute-start.1 = (f32[8,128]{1,0:T(8,128)S(1)}, f32[8,128]{1,0:T(8,128)S(1)}, u32[]{:S(2)}, u32[]{:S(2)}) collective-permute-start(f32[8,128]{1,0:T(8,128)S(1)} %convert_reduce_fusion), channel_id=1, source_target_pairs={{0,128},{128,0},{1,129},{129,1},{2,130},{130,2},{3,131},{131,3},{4... | collective-permute-start | bytes 12296 | tf_op jit(solution)/shard_map/ppermute | solution.py:343
  121.3 0.1 stack.30
  121.4 1.0 collective-permute-done.1
  122.5 1.3 collective-permute-start.3
  123.8 4.6 %collective-permute-start.2 = (bf16[16,128]{1,0:T(8,128)(2,1)S(1)}, bf16[16,128]{1,0:T(8,128)(2,1)S(1)}, u32[]{:S(2)}, u32[]{:S(2)}) collective-permute-start(bf16[16,128]{1,0:T(8,128)(2,1)S(1)} %fusion.3.mine_ref), channel_id=1, source_target_pairs={{0,1},{1,2},{2,3},{3,4},{4,5},{5,6},{6,7},{7,8},{8,9},{9,10},{10,1... | collective-permute-start | bytes 12296 | tf_op jit(solution)/shard_map/ppermute | solution.py:348
  128.4 0.1 stack.31
  128.4 0.6 maximum_select_fusion
  129.1 0.0 collective-permute-done.3.after_ref
  129.1 0.6 collective-permute-done.2.before_ref
  129.7 0.0 copy-done
  129.7 2.6 %decode.1 = f32[3,2,64]{2,1,0:T(2,128)} custom-call(s32[2]{0:T(128)S(1)} %pad_add_fusion.index_ref, bf16[16,128]{1,0:T(8,128)(2,1)S(1)} %collective-permute-done.2.before_ref, bf16[16,128]{1,0:T(8,128)(2,1)S(1)} %fusion.3.mine_ref, bf16[16,128]{1,0:T(8,128)(2,1)S(1)} %collective-permute-done.3.after_ref, bf16[3,48,384]{2,1,0:T(8,128)(2,1)S(1)} %bitcast.27, ...), custom_call_target="tpu_custom_call" | custom-call | tf_op jit(solution)/shard_map/decode/pallas_call | solution.py:282
  (10 shorter events, 0.1 us)
Async XLA Ops:
  92.8 4.2 %collective-permute-start = (bf16[4,32,24,128]{3,2,1,0:T(8,128)(2,1)S(1)}, bf16[4,32,24,128]{3,2,1,0:T(8,128)(2,1)S(1)}, u32[]{:S(2)}, u32[]{:S(2)}) collective-permute-start(bf16[4,32,24,128]{3,2,1,0:T(8,128)(2,1)S(1)} %bitcast.24), channel_id=1, source_target_pairs={{0,128},{128,0},{1,129},{129,1},{2,130},{130,2},{3,131},{131,3},{4... | collective-permute-start | bytes 2359304 | tf_op jit(solution)/shard_map/ppermute | solution.py:323
  100.2 5.1 %copy-start.3 = (f32[384]{0:T(512)S(1)}, f32[384]{0:T(512)}, u32[]{:S(2)}) copy-start(f32[384]{0:T(512)} %param.24) | copy-start | bytes 4612
  100.2 19.1 %all-to-all-start.1 = ((bf16[32,8,128]{2,1,0:T(8,128)(2,1)}), bf16[32,8,128]{2,1,0:T(8,128)(2,1)S(1)}, u32[]{:S(2)}, u32[]{:S(2)}) async-start(bf16[32,8,128]{2,1,0:T(8,128)(2,1)} %guide.1), calls=%async_computation.1 | async-start | bytes 131072 | tf_op jit(solution)/shard_map/all_to_all | solution.py:327
  105.2 0.7 copy-start.2
  105.9 0.7 copy-start.1
  106.7 23.0 %copy-start = (bf16[3,3,16,384]{3,2,1,0:T(8,128)(2,1)S(1)}, bf16[3,3,16,384]{3,2,1,0:T(8,128)(2,1)}, u32[]{:S(2)}) copy-start(bf16[3,3,16,384]{3,2,1,0:T(8,128)(2,1)} %param.23) | copy-start | bytes 331780
  119.4 3.1 %collective-permute-start.1 = (f32[8,128]{1,0:T(8,128)S(1)}, f32[8,128]{1,0:T(8,128)S(1)}, u32[]{:S(2)}, u32[]{:S(2)}) collective-permute-start(f32[8,128]{1,0:T(8,128)S(1)} %convert_reduce_fusion), channel_id=1, source_target_pairs={{0,128},{128,0},{1,129},{129,1},{2,130},{130,2},{3,131},{131,3},{4... | collective-permute-start | bytes 12296 | tf_op jit(solution)/shard_map/ppermute | solution.py:343
  122.5 6.6 %collective-permute-start.3 = (bf16[16,128]{1,0:T(8,128)(2,1)S(1)}, bf16[16,128]{1,0:T(8,128)(2,1)S(1)}, u32[]{:S(2)}, u32[]{:S(2)}) collective-permute-start(bf16[16,128]{1,0:T(8,128)(2,1)S(1)} %fusion.3.mine_ref), channel_id=1, source_target_pairs={{1,0},{2,1},{3,2},{4,3},{5,4},{6,5},{7,6},{8,7},{9,8},{10,9},{11,1... | collective-permute-start | bytes 12296 | tf_op jit(solution)/shard_map/ppermute | solution.py:349
  123.8 5.9 %collective-permute-start.2 = (bf16[16,128]{1,0:T(8,128)(2,1)S(1)}, bf16[16,128]{1,0:T(8,128)(2,1)S(1)}, u32[]{:S(2)}, u32[]{:S(2)}) collective-permute-start(bf16[16,128]{1,0:T(8,128)(2,1)S(1)} %fusion.3.mine_ref), channel_id=1, source_target_pairs={{0,1},{1,2},{2,3},{3,4},{4,5},{5,6},{6,7},{7,8},{8,9},{9,10},{10,1... | collective-permute-start | bytes 12296 | tf_op jit(solution)/shard_map/ppermute | solution.py:348

commit v7 on v6

--- a/solution.py
+++ b/solution.py
@@ -115,11 +115,10 @@
     )(core[None], head[None], *(in_hbm(a) for a in arrays))
 
 
-def share_kernel(rows, sets, own_ref, share_ref, sum_ref, top_ref, total_ref):
-    heads, _, hd = own_ref.shape
+def share_body(rows, sets, heads, query, share_ref, sum_ref, top_ref, total_ref):
+    hd = query.shape[1]
     half = rows // 2
     outs = sum_ref.shape[1]
-    query = own_ref[:, 0:rows, :].reshape(heads * rows, hd)
     per_gather = heads // sets
     frames = share_ref.shape[0] * per_gather
 
@@ -147,38 +146,73 @@
         sum_ref[frame] = dot(values, raised, ((0,), (0,)))
 
 
-def share_attention(own, share, rows, sets, outs):
-    heads = own.shape[0]
-    tokens = heads * rows
+def own_share_kernel(rows, sets, at_ref, own_ref, share_ref, query_ref, *out_refs):
+    heads, _, hd = own_ref.shape
+    count = share_ref.shape[0]
+    before, after = lax.rem(at_ref[0] + (count - 1), count), lax.rem(at_ref[0] + 1, count)
+    earlier = share_ref[pl.ds(before, 1), heads + 1, 0:rows, :].reshape(rows, hd)
+    later = share_ref[pl.ds(after, 1), heads, 0:rows, :].reshape(rows, hd)
+    query = own_ref[:, 0:rows, :].reshape(heads * rows, hd)
+    query_ref[0:rows, :] = earlier
+    query_ref[rows : rows + heads * rows, :] = query
+    query_ref[rows + heads * rows :, :] = later
+    share_body(rows, sets, heads, query_ref[...], share_ref, *out_refs)
+
+
+def other_share_kernel(rows, sets, heads, query_ref, share_ref, *out_refs):
+    share_body(rows, sets, heads, query_ref[...], share_ref, *out_refs)
+
+
+def share_shapes(share, heads, rows, sets, outs):
+    tokens = (heads + 2) * rows
     frames = share.shape[0] * heads // sets
+    shapes = [
+        jax.ShapeDtypeStruct((frames, outs, tokens), F32),
+        jax.ShapeDtypeStruct((frames, tokens), F32),
+        jax.ShapeDtypeStruct((frames, tokens), F32),
+    ]
     keys = frames * sets * rows
+    cost = pl.CostEstimate(
+        flops=2 * tokens * keys * (HEAD_DIM + outs),
+        transcendentals=tokens * keys,
+        bytes_accessed=1 << 20,
+    )
+    return tokens, shapes, cost
+
+
+def own_share_attention(place, own, share, rows, sets, outs):
+    tokens, shapes, cost = share_shapes(share, own.shape[0], rows, sets, outs)
     return pl.pallas_call(
-        functools.partial(share_kernel, rows, sets),
+        functools.partial(own_share_kernel, rows, sets),
+        in_specs=[SMEM, VMEM, VMEM],
+        out_specs=[VMEM] * 4,
+        out_shape=[jax.ShapeDtypeStruct((tokens, HEAD_DIM), BF)] + shapes,
+        cost_estimate=cost,
+        name="own_share",
+        compiler_params=GRANT,
+    )(place[None], own, share)
+
+
+def other_share_attention(query, share, heads, rows, sets, outs):
+    _, shapes, cost = share_shapes(share, heads, rows, sets, outs)
+    return pl.pallas_call(
+        functools.partial(other_share_kernel, rows, sets, heads),
         in_specs=[VMEM, VMEM],
-        out_specs=[VMEM, VMEM, VMEM],
-        out_shape=[
-            jax.ShapeDtypeStruct((frames, outs, tokens), F32),
-            jax.ShapeDtypeStruct((frames, tokens), F32),
-            jax.ShapeDtypeStruct((frames, tokens), F32),
-        ],
-        cost_estimate=pl.CostEstimate(
-            flops=2 * tokens * keys * (HEAD_DIM + outs),
-            transcendentals=tokens * keys,
-            bytes_accessed=1 << 20,
-        ),
-        name="share",
+        out_specs=[VMEM] * 3,
+        out_shape=shapes,
+        cost_estimate=cost,
+        name="other_share",
         compiler_params=GRANT,
-    )(own, share)
-
-
-def guide_kernel(rows, guide_ref, own_ref, bias_ref, term_ref, *refs):
+    )(query, share)
+
+
+def guide_kernel(rows, guide_ref, query_ref, bias_ref, term_ref, *refs):
     shares, out_ref = refs[:-1], refs[-1]
     sum_refs, top_refs, total_refs = shares[0::3], shares[1::3], shares[2::3]
-    heads, _, hd = own_ref.shape
+    heads = out_ref.shape[0]
     half = rows // 2
     count = top_refs[0].shape[0]
-    query = own_ref[:, 0:rows, :].reshape(heads * rows, hd)
-    shift = dot(bias_ref[...], query, ((1,), (1,)))
+    shift = dot(bias_ref[...], query_ref[...], ((1,), (1,)))
     tops = [r[...] for r in top_refs]
     totals = [r[...] for r in total_refs]
     mixes = [None] * len(tops)
@@ -202,35 +236,50 @@
     for mix, sum_ref in zip(mixes, sum_refs):
         for frame in range(count):
             result = result + mix[frame : frame + 1, :] * sum_ref[frame]
-    by_token = jnp.transpose(result).reshape(heads, 2, half, -1)
-    packed = jnp.concatenate([by_token[:, 0], by_token[:, 1]], axis=2)
-    out_ref[...] = packed.astype(BF)
-
-
-def guide(guidance, own, bias, term, shares, rows, outs):
-    heads = own.shape[0]
+    by_token = jnp.transpose(result).reshape(heads + 2, 2, half, -1)
+    packed = jnp.concatenate([by_token[:, 0], by_token[:, 1]], axis=2).astype(BF)
+    for side in range(3):
+        out_ref[:, side * half : (side + 1) * half, :] = packed[side : side + heads]
+
+
+def guide(lines, query, bias, term, shares, rows, outs):
+    heads = query.shape[0] // rows - 2
     arrays = [array for share in shares for array in share]
     return pl.pallas_call(
         functools.partial(guide_kernel, rows),
         in_specs=[VMEM] * (4 + len(arrays)),
         out_specs=VMEM,
-        out_shape=jax.ShapeDtypeStruct((heads, rows // 2, 2 * outs), BF),
+        out_shape=jax.ShapeDtypeStruct((heads, 3 * (rows // 2), 2 * outs), BF),
         name="guide",
         compiler_params=GRANT,
-    )(guidance, own, bias, term, *arrays)
-
-
-def decode_kernel(index_ref, before_ref, mine_ref, after_ref, conv_in_ref, gain_ref, conv_out_ref, out_ref):
-    outs = before_ref.shape[1] // 2
+    )(lines, query, bias, term, *arrays)
+
+
+def decode_kernel(
+    index_ref, mine_ref, other_ref, noisy_ref, conv_in_ref, gain_ref, conv_out_ref, velocity_ref, out_ref
+):
+    outs = velocity_ref.shape[1]
     lat = outs // 4
-    tokens = before_ref.shape[0] * 2
+    tokens = velocity_ref.shape[0]
+    quarter = tokens // 4
+    first, last = index_ref[0] == 0, index_ref[0] == index_ref[1] - 1
+    low_core = index_ref[2] == 0
     left, right = [], []
-    for ref in (before_ref, mine_ref, after_ref):
-        both = ref[...].astype(F32)
-        quarter = tokens // 4
-        parts = [both[:quarter], both[quarter:]]
-        parts = [p[:, side] for p in parts for side in (slice(0, outs), slice(outs, None))]
-        block = jnp.concatenate(parts, axis=0)
+    for side in range(3):
+        place = slice(side * quarter, (side + 1) * quarter)
+        here, there = mine_ref[place, :], other_ref[place, :]
+        both = [jnp.where(low_core, here, there), jnp.where(low_core, there, here)]
+        blocks = []
+        for n, velocity in enumerate(both):
+            stepped = noisy_ref[side, n * quarter : (n + 1) * quarter, :] - step_size * velocity
+            blocks += [stepped[:, :outs], stepped[:, outs:]]
+            if side == 1:
+                at = 2 * n * quarter
+                velocity_ref[at : at + quarter, :] = velocity[:, :outs]
+                velocity_ref[at + quarter : at + 2 * quarter, :] = velocity[:, outs:]
+        block = jnp.concatenate(blocks, axis=0).astype(BF).astype(F32)
+        if side != 1:
+            block = jnp.where(first if side == 0 else last, 0.0, block)
         edge = jnp.zeros_like(block[:1])
         earlier = jnp.concatenate([edge, block[:-1]], axis=0)
         later = jnp.concatenate([block[1:], edge], axis=0)
@@ -241,7 +290,6 @@
             right.append(jnp.concatenate([here, later[:, at : at + lat]], axis=1))
     height = 4 * tokens
     row = lax.broadcasted_iota(jnp.int32, (height, 1), 0) // tokens
-    first, last = index_ref[0] == 0, index_ref[0] == index_ref[1] - 1
     keep = jnp.where((row == 0) & first | (row == 3) & last, 0.0, 1.0)
     taps = []
     for windows in (left, right):
@@ -277,16 +325,19 @@
     out_ref[:, 1, :] = colours[:, 2 * tokens :]
 
 
-def decode(index, before, mine, after, conv_in, gain, conv_out):
-    tokens = before.shape[0] * 2
+def decode(index, mine, other, noisy, conv_in, gain, conv_out):
+    tokens, outs = 2 * noisy.shape[1], noisy.shape[2] // 2
     return pl.pallas_call(
         decode_kernel,
         in_specs=[SMEM] + [VMEM] * 6,
-        out_specs=VMEM,
-        out_shape=jax.ShapeDtypeStruct((3, 2, 2 * tokens), F32),
+        out_specs=[VMEM, VMEM],
+        out_shape=[
+            jax.ShapeDtypeStruct((tokens, outs), F32),
+            jax.ShapeDtypeStruct((3, 2, 2 * tokens), F32),
+        ],
         name="decode",
         compiler_params=GRANT,
-    )(index, before, mine, after, conv_in, gain, conv_out)
+    )(index, mine, other, noisy, conv_in, gain, conv_out)
 
 
 def shards(
@@ -319,36 +370,34 @@
         keyboard, mouse, key_table, mouse_table, guidance, rows,
     )
     own = lax.all_to_all(packed, ("xh", "z"), 0, 0, tiled=True)
-    share = lax.all_gather(own[:, rows:, :], "xl")
+    moving = jnp.concatenate(
+        [own[:, rows:], own[:1, : rows + rows // 2], own[-1:, : rows + rows // 2]], axis=0
+    )
+    share = lax.all_gather(moving, "xl")
     other_share = lax.ppermute(share, "branch", swap)
-    shares = [share_attention(own, s, rows, sets, outs) for s in (share, other_share)]
-    part = guide(lines, own, bias, term, shares, rows, outs)
+    query, *first = own_share_attention(xl, own, share, rows, sets, outs)
+    second = other_share_attention(query, other_share, own.shape[0], rows, sets, outs)
+    part = guide(lines, query, bias, term, [first, second], rows, outs)
     part, latent, conv_out, gain = lax.optimization_barrier((part, latent, conv_out, gain))
     returned = lax.all_to_all(part, ("xh", "z"), 0, 0, tiled=True)
 
-    def laid(tokens):
-        return tokens.reshape(2, 2, -1, outs).transpose(0, 2, 1, 3).reshape(-1, 2 * outs)
-
     count = wide * narrow * sets
-    index = jnp.stack([(xl * wide + xh) * sets + z, jnp.int32(count)])
+    places = ("xl", "xh", "z")
+    index = jnp.stack([(xl * wide + xh) * sets + z, jnp.int32(count), core])
     taps_in = conv_in.reshape(conv_in.shape[0], -1, conv_in.shape[3])
     taps_out = conv_out.transpose(1, 0, 3, 2).reshape(3, -1, conv_out.shape[2])
     taps_out = jnp.pad(taps_out, ((0, 0), (0, 16 - taps_out.shape[1]), (0, 0)))
     taps_out = taps_out.reshape(-1, conv_out.shape[2])
-    noisy = laid(latent)
+    noisy = latent.reshape(2, 2, -1, outs).transpose(0, 2, 1, 3).reshape(-1, 2 * outs)
+    before = lax.ppermute(noisy, places, [(i, i + 1) for i in range(count - 1)])
+    after = lax.ppermute(noisy, places, [(i + 1, i) for i in range(count - 1)])
+    noisy = jnp.stack([before, noisy, after])
     mine = jnp.sum(returned.astype(F32), axis=0)
     mine, noisy, taps_out, gain, index = lax.optimization_barrier(
         (mine, noisy, taps_out, gain[None], index)
     )
     other = lax.ppermute(mine, "branch", swap)
-    both = jnp.where(core == 0, jnp.stack([mine, other]), jnp.stack([other, mine]))
-    velocity = both.reshape(2, -1, 2, outs).transpose(0, 2, 1, 3).reshape(-1, outs)
-    stepped = (noisy - step_size * both.reshape(-1, 2 * outs)).astype(BF)
-    places = ("xl", "xh", "z")
-    before = lax.ppermute(stepped, places, [(i, i + 1) for i in range(count - 1)])
-    after = lax.ppermute(stepped, places, [(i + 1, i) for i in range(count - 1)])
-    colours = decode(index, before, stepped, after, taps_in, gain, taps_out)
-    return (velocity, colours)
+    return tuple(decode(index, mine, other, noisy, taps_in, gain, taps_out))
 
 
 def solution(mesh):

time: 135 us -> 133 us (0.985)
    all_to_all x1, waiting for transfers between devices: 12.6 us -> 11 us  [shards(): returned = lax.all_to_all(part, ('xh', 'z'), 0, 0, tiled=True)]
    ppermute x2, waiting for transfers between devices: 0.61 us -> 2.22 us  [the longest x1 2.21 us: shards(): after = lax.ppermute(noisy, places, [(i + 1, i) for i in range(count - 1)])]
  transfers between devices with their start and end apart: 5 -> 5, of which waited for: 4 -> 4; matrix products, arithmetic and copies ran while one was open for 1% -> 0% of each run, Pallas kernels for 1% -> 2%
where the time goes in v7:
time: 133 us; the launch traced here: 131 us
  blocking collectives  90.9 us (68%)
  starting transfers between devices  14.6 us (11%)
  waiting for transfers between devices  14.6 us (11%)
  Pallas kernels  10.2 us (8%)
    all_to_all x1, blocking collectives, shards(): own = lax.all_to_all(packed, ('xh', 'z'), 0, 0, tiled=True)  69.6 us
    all_gather x1, blocking collectives, shards(): share = lax.all_gather(moving, 'xl')  21.3 us
    all_to_all x1, waiting for transfers between devices, shards(): returned = lax.all_to_all(part, ('xh', 'z'), 0, 0, tiled=True)  11 us
    all_to_all x1, starting transfers between devices, shards(): returned = lax.all_to_all(part, ('xh', 'z'), 0, 0, tiled=True)  4.78 us
    ppermute x1, starting transfers between devices, shards(): before = lax.ppermute(noisy, places, [(i, i + 1) for i in range(count - 1)])  4.59 us
  transfers between devices with their start and end apart: 5, of which 4 were waited for; matrix products, arithmetic and copies ran while one was open for 0% of the time, Pallas kernels for 2%

profile of v7, /device:TPU:80, one launch (start us, length us, event | category | flops | bytes accessed | tf_op | source)
XLA Modules:
  0.0 131.5 jit_solution(16498813914228165421)
XLA Ops:
  0.6 2.0 %pack.1 = (bf16[32,40,128]{2,1,0:T(8,128)(2,1)S(1)}, bf16[32,128]{1,0:T(8,128)(2,1)S(1)}, f32[16,64]{1,0:T(8,128)S(1)}, f32[4,128]{1,0:T(4,128)S(1)}) custom-call(s32[1]{0:T(128)} %bitcast.core_ref, s32[1]{0:T(128)} %bitcast.1.head_ref, bf16[32,4096]{1,0:T(8,128)(2,1)} %q_ref.1, bf16[32,4096]{1,0:T(8,128)(2,1)} %k_ref.1, bf16[32,4096]{1,0:T(8,128)(2,1)} %v_ref.1, ...), custom_call_target="tpu_custom_call" | custom-call | tf_op jit(solution)/shard_map/pack/pallas_call | solution.py:97
  2.7 69.6 %all_to_all.10.own_ref = bf16[32,40,128]{2,1,0:T(8,128)(2,1)S(1)} all-to-all(bf16[32,40,128]{2,1,0:T(8,128)(2,1)S(1)} %get-tuple-element.23), channel_id=1, replica_groups=mesh['groups'=2,'branch'=2,'xl'=4,'xh'=2,'z'=16] {'xh','z'}, dimensions={0} | all-to-all | bytes 655360 | tf_op jit(solution)/shard_map/all_to_all | solution.py:372
  72.3 21.3 %all-gather = bf16[136,24,128]{2,1,0:T(8,128)(2,1)S(1)} all-gather(bf16[34,24,128]{2,1,0:T(8,128)(2,1)S(1)} %pad_maximum_fusion), channel_id=2, replica_groups=mesh['groups'=2,'branch'=2,'xl'=4,'xh'=2,'z'=16] {'xl'}, dimensions={0}, use_global_device_ids=true | all-gather | bytes 1044480 | tf_op jit(solution)/shard_map/all_gather | solution.py:376
  93.7 1.9 %collective-permute-start = (bf16[4,34,24,128]{3,2,1,0:T(8,128)(2,1)S(1)}, bf16[4,34,24,128]{3,2,1,0:T(8,128)(2,1)S(1)}, u32[]{:S(2)}, u32[]{:S(2)}) collective-permute-start(bf16[4,34,24,128]{3,2,1,0:T(8,128)(2,1)S(1)} %bitcast.16), channel_id=1, source_target_pairs={{0,128},{128,0},{1,129},{129,1},{2,130},{130,2},{3,131},{131,3},{4... | collective-permute-start | bytes 2506760 | tf_op jit(solution)/shard_map/ppermute | solution.py:377
  95.6 2.0 %own_share.1 = (bf16[544,128]{1,0:T(8,128)(2,1)S(1)}, f32[8,64,544]{2,1,0:T(8,128)S(1)}, f32[8,544]{1,0:T(8,128)S(1)}, f32[8,544]{1,0:T(8,128)S(1)}) custom-call(s32[1]{0:T(128)} %bitcast.3.at_ref, bf16[32,40,128]{2,1,0:T(8,128)(2,1)S(1)} %all_to_all.10.own_ref, bf16[4,34,24,128]{3,2,1,0:T(8,128)(2,1)S(1)} %bitcast.17), custom_call_target="tpu_custom_call" | custom-call | flops 427819008 | bytes 1048576 | tf_op jit(solution)/shard_map/own_share/pallas_call | solution.py:185
  97.6 0.3 collective-permute-done.share_ref
  97.9 2.0 %other_share.1 = (f32[8,64,544]{2,1,0:T(8,128)S(1)}, f32[8,544]{1,0:T(8,128)S(1)}, f32[8,544]{1,0:T(8,128)S(1)}) custom-call(bf16[544,128]{1,0:T(8,128)(2,1)S(1)} %get-tuple-element.24.query_ref, bf16[4,34,24,128]{3,2,1,0:T(8,128)(2,1)S(1)} %collective-permute-done.share_ref), custom_call_target="tpu_custom_call" | custom-call | flops 427819008 | bytes 1048576 | tf_op jit(solution)/shard_map/other_share/pallas_call | solution.py:198
  99.9 0.0 copy-start.2
  100.0 0.0 copy-start.3
  100.0 0.0 copy-start.1
  100.0 0.0 copy-start
  100.0 1.5 %guide.1 = bf16[32,24,128]{2,1,0:T(8,128)(2,1)} custom-call(f32[4,128]{1,0:T(4,128)S(1)} %get-tuple-element.22.guide_ref, bf16[544,128]{1,0:T(8,128)(2,1)S(1)} %get-tuple-element.24.query_ref, bf16[32,128]{1,0:T(8,128)(2,1)S(1)} %get-tuple-element.25.bias_ref, f32[16,64]{1,0:T(8,128)S(1)} %get-tuple-element.26.term_ref, ...), custom_call_target="tpu_custom_call" | custom-call | tf_op jit(solution)/shard_map/guide/pallas_call | solution.py:248
  101.5 4.8 %all-to-all-start.1 = ((bf16[32,24,128]{2,1,0:T(8,128)(2,1)}), bf16[32,24,128]{2,1,0:T(8,128)(2,1)S(1)}, u32[]{:S(2)}, u32[]{:S(2)}) async-start(bf16[32,24,128]{2,1,0:T(8,128)(2,1)} %guide.1), calls=%async_computation.1 | async-start | bytes 393216 | tf_op jit(solution)/shard_map/all_to_all | solution.py:382
  106.3 0.0 copy-done.2
  106.4 0.1 reshape.20
  106.4 1.3 collective-permute-start.2
  107.7 4.6 %collective-permute-start.1 = (f32[16,128]{1,0:T(8,128)S(1)}, f32[16,128]{1,0:T(8,128)S(1)}, u32[]{:S(2)}, u32[]{:S(2)}) collective-permute-start(f32[16,128]{1,0:T(8,128)S(1)} %reshape.20), channel_id=1, source_target_pairs={{0,1},{1,2},{2,3},{3,4},{4,5},{5,6},{6,7},{7,8},{8,9},{9,10},{10,1... | collective-permute-start | bytes 24584 | tf_op jit(solution)/shard_map/ppermute | solution.py:392
  112.3 0.1 pad_add_fusion.index_ref
  112.4 0.1 stack_reshape.3
  112.5 0.0 copy-done.3
  112.5 0.0 copy-done.1
  112.6 2.2 %collective-permute-done.2 = f32[16,128]{1,0:T(8,128)S(1)} collective-permute-done((f32[16,128]{1,0:T(8,128)S(1)}, f32[16,128]{1,0:T(8,128)S(1)}, u32[]{:S(2)}, u32[]{:S(2)}) %collective-permute-start.2) | collective-permute-done | bytes 8224 | tf_op jit(solution)/shard_map/ppermute | solution.py:393
  114.8 0.0 collective-permute-done.1
  114.8 11.0 %all-to-all-done.1 = bf16[32,24,128]{2,1,0:T(8,128)(2,1)S(1)} async-done(((bf16[32,24,128]{2,1,0:T(8,128)(2,1)}), bf16[32,24,128]{2,1,0:T(8,128)(2,1)S(1)}, u32[]{:S(2)}, u32[]{:S(2)}) %all-to-all-start.1) | async-done | bytes 196640 | tf_op jit(solution)/shard_map/all_to_all | solution.py:382
  125.8 2.0 %collective-permute-start.3 = (f32[24,128]{1,0:T(8,128)S(1)}, f32[24,128]{1,0:T(8,128)S(1)}, u32[]{:S(2)}, u32[]{:S(2)}) collective-permute-start(f32[24,128]{1,0:T(8,128)S(1)} %convert_reduce_fusion.mine_ref), channel_id=1, source_target_pairs={{0,128},{128,0},{1,129},{129,1},{2,130},{130,2},{3,131},{131,3},{4... | collective-permute-start | bytes 36872 | tf_op jit(solution)/shard_map/ppermute | solution.py:399
  127.8 1.1 collective-permute-done.3.other_ref
  128.9 0.0 copy-done
  128.9 2.6 %decode.1 = (f32[32,64]{1,0:T(8,128)}, f32[3,2,64]{2,1,0:T(2,128)}) custom-call(s32[3]{0:T(128)S(1)} %pad_add_fusion.index_ref, f32[24,128]{1,0:T(8,128)S(1)} %convert_reduce_fusion.mine_ref, f32[24,128]{1,0:T(8,128)S(1)} %collective-permute-done.3.other_ref, f32[3,16,128]{2,1,0:T(8,128)S(1)} %pad_maximum_fusion.1.noisy_ref, ...), custom_call_target="tpu_custom_call" | custom-call | tf_op jit(solution)/shard_map/decode/pallas_call | solution.py:330
  (10 shorter events, 0.1 us)
Async XLA Ops:
  93.7 4.3 %collective-permute-start = (bf16[4,34,24,128]{3,2,1,0:T(8,128)(2,1)S(1)}, bf16[4,34,24,128]{3,2,1,0:T(8,128)(2,1)S(1)}, u32[]{:S(2)}, u32[]{:S(2)}) collective-permute-start(bf16[4,34,24,128]{3,2,1,0:T(8,128)(2,1)S(1)} %bitcast.16), channel_id=1, source_target_pairs={{0,128},{128,0},{1,129},{129,1},{2,130},{130,2},{3,131},{131,3},{4... | collective-permute-start | bytes 2506760 | tf_op jit(solution)/shard_map/ppermute | solution.py:377
  99.9 6.4 %copy-start.2 = (f32[32,64]{1,0:T(8,128)S(1)}, f32[32,64]{1,0:T(8,128)}, u32[]{:S(2)}) copy-start(f32[32,64]{1,0:T(8,128)} %param.22) | copy-start | bytes 24580
  100.0 12.6 %copy-start.3 = (f32[384]{0:T(512)S(1)}, f32[384]{0:T(512)}, u32[]{:S(2)}) copy-start(f32[384]{0:T(512)} %param.24) | copy-start | bytes 4612
  100.0 12.5 %copy-start.1 = (bf16[3,3,384,3]{2,3,1,0:T(4,128)(2,1)S(1)}, bf16[3,3,384,3]{2,3,1,0:T(4,128)(2,1)}, u32[]{:S(2)}) copy-start(bf16[3,3,384,3]{2,3,1,0:T(4,128)(2,1)} %param.25) | copy-start | bytes 62212
  100.0 28.9 %copy-start = (bf16[3,3,16,384]{3,2,1,0:T(8,128)(2,1)S(1)}, bf16[3,3,16,384]{3,2,1,0:T(8,128)(2,1)}, u32[]{:S(2)}) copy-start(bf16[3,3,16,384]{3,2,1,0:T(8,128)(2,1)} %param.23) | copy-start | bytes 331780
  101.5 24.2 %all-to-all-start.1 = ((bf16[32,24,128]{2,1,0:T(8,128)(2,1)}), bf16[32,24,128]{2,1,0:T(8,128)(2,1)S(1)}, u32[]{:S(2)}, u32[]{:S(2)}) async-start(bf16[32,24,128]{2,1,0:T(8,128)(2,1)} %guide.1), calls=%async_computation.1 | async-start | bytes 393216 | tf_op jit(solution)/shard_map/all_to_all | solution.py:382
  106.4 8.3 %collective-permute-start.2 = (f32[16,128]{1,0:T(8,128)S(1)}, f32[16,128]{1,0:T(8,128)S(1)}, u32[]{:S(2)}, u32[]{:S(2)}) collective-permute-start(f32[16,128]{1,0:T(8,128)S(1)} %reshape.20), channel_id=1, source_target_pairs={{1,0},{2,1},{3,2},{4,3},{5,4},{6,5},{7,6},{8,7},{9,8},{10,9},{11,1... | collective-permute-start | bytes 24584 | tf_op jit(solution)/shard_map/ppermute | solution.py:393
  107.7 7.0 %collective-permute-start.1 = (f32[16,128]{1,0:T(8,128)S(1)}, f32[16,128]{1,0:T(8,128)S(1)}, u32[]{:S(2)}, u32[]{:S(2)}) collective-permute-start(f32[16,128]{1,0:T(8,128)S(1)} %reshape.20), channel_id=1, source_target_pairs={{0,1},{1,2},{2,3},{3,4},{4,5},{5,6},{6,7},{7,8},{8,9},{9,10},{10,1... | collective-permute-start | bytes 24584 | tf_op jit(solution)/shard_map/ppermute | solution.py:392
  125.8 3.1 %collective-permute-start.3 = (f32[24,128]{1,0:T(8,128)S(1)}, f32[24,128]{1,0:T(8,128)S(1)}, u32[]{:S(2)}, u32[]{:S(2)}) collective-permute-start(f32[24,128]{1,0:T(8,128)S(1)} %convert_reduce_fusion.mine_ref), channel_id=1, source_target_pairs={{0,128},{128,0},{1,129},{129,1},{2,130},{130,2},{3,131},{131,3},{4... | collective-permute-start | bytes 36872 | tf_op jit(solution)/shard_map/ppermute | solution.py:399

commit v8 on v7

--- a/solution.py
+++ b/solution.py
@@ -45,11 +45,14 @@
         pltpu.make_async_copy(ms_ref, ms_tmp, sems.at[5]),
         pltpu.make_async_copy(guide_ref, guide_tmp, sems.at[6]),
     ]
+    width = w_tmp.shape[1]
+    cuts = [slice(n * width // 2, (n + 1) * width // 2) for n in range(2)]
     copies = [
-        pltpu.make_async_copy(w_ref, w_tmp, sems.at[0]),
-        pltpu.make_async_copy(v_ref.at[mine, :], v_tmp, sems.at[1]),
-        pltpu.make_async_copy(q_ref.at[mine, :], q_tmp, sems.at[2]),
-        pltpu.make_async_copy(k_ref.at[mine, :], k_tmp, sems.at[3]),
+        pltpu.make_async_copy(q_ref.at[mine, :], q_tmp, sems.at[0]),
+        pltpu.make_async_copy(k_ref.at[mine, :], k_tmp, sems.at[1]),
+        pltpu.make_async_copy(v_ref.at[mine, :], v_tmp, sems.at[2]),
+        pltpu.make_async_copy(w_ref.at[:, cuts[0]], w_tmp.at[:, cuts[0]], sems.at[3]),
+        pltpu.make_async_copy(w_ref.at[:, cuts[1]], w_tmp.at[:, cuts[1]], sems.at[7]),
     ]
     for copy in ids + copies:
         copy.start()
@@ -57,19 +60,25 @@
         copy.wait()
     picks = []
     for f in range(frames):
-        at = 7 + 2 * f
+        at = 8 + 2 * f
         picks += [
             pltpu.make_async_copy(key_ref.at[kb_tmp[f], :, head], key_tmp.at[f], sems.at[at]),
             pltpu.make_async_copy(mouse_ref.at[ms_tmp[f], :, head], mouse_tmp.at[f], sems.at[at + 1]),
         ]
     for copy in picks:
         copy.start()
-    for copy in copies:
+    for copy in copies[:2]:
         copy.wait()
     for h in range(heads):
         cols = slice(h * hd, (h + 1) * hd)
         out_ref[h, 0:rows, :] = q_tmp[:, cols]
         out_ref[h, rows : 2 * rows, :] = k_tmp[:, cols]
+    for copy in copies[2:4]:
+        copy.wait()
+    for h in range(heads):
+        if h == heads // 2:
+            copies[4].wait()
+        cols = slice(h * hd, (h + 1) * hd)
         projected = dot(v_tmp[:, cols], w_tmp[:, cols], ((1,), (1,)))
         projected = jnp.concatenate([projected[:half], projected[half:]], axis=1)
         out_ref[h, 2 * rows :, :] = projected.astype(BF)
@@ -109,7 +118,7 @@
         + [pltpu.SMEM((frames,), jnp.int32)] * 2
         + [pltpu.VMEM((frames, 2, HEAD_DIM), BF)] * 2
         + [pltpu.SMEM(guidance.shape, F32)]
-        + [pltpu.SemaphoreType.DMA((7 + 2 * frames,))],
+        + [pltpu.SemaphoreType.DMA((8 + 2 * frames,))],
         name="pack",
         compiler_params=GRANT,
     )(core[None], head[None], *(in_hbm(a) for a in arrays))
@@ -249,21 +258,22 @@
         functools.partial(guide_kernel, rows),
         in_specs=[VMEM] * (4 + len(arrays)),
         out_specs=VMEM,
-        out_shape=jax.ShapeDtypeStruct((heads, 3 * (rows // 2), 2 * outs), BF),
+        out_shape=pltpu.VMEM((heads, 3 * (rows // 2), 2 * outs), BF),
         name="guide",
         compiler_params=GRANT,
     )(lines, query, bias, term, *arrays)
 
 
 def decode_kernel(
-    index_ref, mine_ref, other_ref, noisy_ref, conv_in_ref, gain_ref, conv_out_ref, velocity_ref, out_ref
+    flag_ref, mine_ref, other_ref, noisy_ref, conv_in_ref, gain_ref, conv_out_ref,
+    velocity_out, colours_out, velocity_ref, out_ref, sems,
 ):
     outs = velocity_ref.shape[1]
     lat = outs // 4
     tokens = velocity_ref.shape[0]
     quarter = tokens // 4
-    first, last = index_ref[0] == 0, index_ref[0] == index_ref[1] - 1
-    low_core = index_ref[2] == 0
+    first, last = flag_ref[0:1, 0:1] > 0.5, flag_ref[1:2, 0:1] > 0.5
+    low_core = flag_ref[2:3, :] > 0.5
     left, right = [], []
     for side in range(3):
         place = slice(side * quarter, (side + 1) * quarter)
@@ -278,7 +288,10 @@
                 velocity_ref[at : at + quarter, :] = velocity[:, :outs]
                 velocity_ref[at + quarter : at + 2 * quarter, :] = velocity[:, outs:]
         block = jnp.concatenate(blocks, axis=0).astype(BF).astype(F32)
-        if side != 1:
+        if side == 1:
+            velocity_copy = pltpu.make_async_copy(velocity_ref, velocity_out, sems.at[0])
+            velocity_copy.start()
+        else:
             block = jnp.where(first if side == 0 else last, 0.0, block)
         edge = jnp.zeros_like(block[:1])
         earlier = jnp.concatenate([edge, block[:-1]], axis=0)
@@ -323,21 +336,30 @@
         colours = placed if colours is None else colours + placed
     out_ref[:, 0, :] = colours[:, : 2 * tokens]
     out_ref[:, 1, :] = colours[:, 2 * tokens :]
-
-
-def decode(index, mine, other, noisy, conv_in, gain, conv_out):
+    colours_copy = pltpu.make_async_copy(out_ref, colours_out, sems.at[1])
+    colours_copy.start()
+    velocity_copy.wait()
+    colours_copy.wait()
+
+
+def decode(flags, mine, other, noisy, conv_in, gain, conv_out):
     tokens, outs = 2 * noisy.shape[1], noisy.shape[2] // 2
     return pl.pallas_call(
         decode_kernel,
-        in_specs=[SMEM] + [VMEM] * 6,
-        out_specs=[VMEM, VMEM],
+        in_specs=[VMEM] * 7,
+        out_specs=[pl.BlockSpec(memory_space=pltpu.HBM)] * 2,
         out_shape=[
             jax.ShapeDtypeStruct((tokens, outs), F32),
             jax.ShapeDtypeStruct((3, 2, 2 * tokens), F32),
         ],
+        scratch_shapes=[
+            pltpu.VMEM((tokens, outs), F32),
+            pltpu.VMEM((3, 2, 2 * tokens), F32),
+            pltpu.SemaphoreType.DMA((2,)),
+        ],
         name="decode",
         compiler_params=GRANT,
-    )(index, mine, other, noisy, conv_in, gain, conv_out)
+    )(flags, mine, other, noisy, conv_in, gain, conv_out)
 
 
 def shards(
@@ -383,7 +405,10 @@
 
     count = wide * narrow * sets
     places = ("xl", "xh", "z")
-    index = jnp.stack([(xl * wide + xh) * sets + z, jnp.int32(count), core])
+    index = (xl * wide + xh) * sets + z
+    line = lax.broadcasted_iota(jnp.int32, (8, HEAD_DIM), 0)
+    flags = (line == 0) & (index == 0) | (line == 1) & (index == count - 1) | (line == 2) & (core == 0)
+    flags = flags.astype(F32)
     taps_in = conv_in.reshape(conv_in.shape[0], -1, conv_in.shape[3])
     taps_out = conv_out.transpose(1, 0, 3, 2).reshape(3, -1, conv_out.shape[2])
     taps_out = jnp.pad(taps_out, ((0, 0), (0, 16 - taps_out.shape[1]), (0, 0)))
@@ -393,11 +418,11 @@
     after = lax.ppermute(noisy, places, [(i + 1, i) for i in range(count - 1)])
     noisy = jnp.stack([before, noisy, after])
     mine = jnp.sum(returned.astype(F32), axis=0)
-    mine, noisy, taps_out, gain, index = lax.optimization_barrier(
-        (mine, noisy, taps_out, gain[None], index)
+    mine, noisy, taps_out, gain, flags = lax.optimization_barrier(
+        (mine, noisy, taps_out, gain[None], flags)
     )
     other = lax.ppermute(mine, "branch", swap)
-    return tuple(decode(index, mine, other, noisy, taps_in, gain, taps_out))
+    return tuple(decode(flags, mine, other, noisy, taps_in, gain, taps_out))
 
 
 def solution(mesh):

time: 133 us -> 133 us (level)
  no operation moved by 1% of the time
where the time goes in v8:
time: 133 us; the launch traced here: 131 us
  blocking collectives  90.9 us (68%)
  waiting for transfers between devices  14.7 us (11%)
  starting transfers between devices  14.5 us (11%)
  Pallas kernels  9.83 us (7%)
    all_to_all x1, blocking collectives, shards(): own = lax.all_to_all(packed, ('xh', 'z'), 0, 0, tiled=True)  69.6 us
    all_gather x1, blocking collectives, shards(): share = lax.all_gather(moving, 'xl')  21.3 us
    all_to_all x1, waiting for transfers between devices, shards(): returned = lax.all_to_all(part, ('xh', 'z'), 0, 0, tiled=True)  11 us
    all_to_all x1, starting transfers between devices, shards(): returned = lax.all_to_all(part, ('xh', 'z'), 0, 0, tiled=True)  4.78 us
    ppermute x1, starting transfers between devices, shards(): before = lax.ppermute(noisy, places, [(i, i + 1) for i in range(count - 1)])  4.59 us
  transfers between devices with their start and end apart: 5, of which 4 were waited for; matrix products, arithmetic and copies ran while one was open for 0% of the time, Pallas kernels for 2%

profile of v8, /device:TPU:80, one launch (start us, length us, event | category | flops | bytes accessed | tf_op | source)
XLA Modules:
  0.0 131.2 jit_solution(12725144889807866158)
XLA Ops:
  0.6 2.2 %pack.1 = (bf16[32,40,128]{2,1,0:T(8,128)(2,1)S(1)}, bf16[32,128]{1,0:T(8,128)(2,1)S(1)}, f32[16,64]{1,0:T(8,128)S(1)}, f32[4,128]{1,0:T(4,128)S(1)}) custom-call(s32[1]{0:T(128)} %bitcast.core_ref, s32[1]{0:T(128)} %bitcast.1.head_ref, bf16[32,4096]{1,0:T(8,128)(2,1)} %q_ref.1, bf16[32,4096]{1,0:T(8,128)(2,1)} %k_ref.1, bf16[32,4096]{1,0:T(8,128)(2,1)} %v_ref.1, ...), custom_call_target="tpu_custom_call" | custom-call | tf_op jit(solution)/shard_map/pack/pallas_call | solution.py:106
  2.8 69.6 %all_to_all.10.own_ref = bf16[32,40,128]{2,1,0:T(8,128)(2,1)S(1)} all-to-all(bf16[32,40,128]{2,1,0:T(8,128)(2,1)S(1)} %get-tuple-element.23), channel_id=1, replica_groups=mesh['groups'=2,'branch'=2,'xl'=4,'xh'=2,'z'=16] {'xh','z'}, dimensions={0} | all-to-all | bytes 655360 | tf_op jit(solution)/shard_map/all_to_all | solution.py:394
  72.5 21.3 %all-gather = bf16[136,24,128]{2,1,0:T(8,128)(2,1)S(1)} all-gather(bf16[34,24,128]{2,1,0:T(8,128)(2,1)S(1)} %pad_maximum_fusion), channel_id=2, replica_groups=mesh['groups'=2,'branch'=2,'xl'=4,'xh'=2,'z'=16] {'xl'}, dimensions={0}, use_global_device_ids=true | all-gather | bytes 1044480 | tf_op jit(solution)/shard_map/all_gather | solution.py:398
  93.8 1.9 %collective-permute-start = (bf16[4,34,24,128]{3,2,1,0:T(8,128)(2,1)S(1)}, bf16[4,34,24,128]{3,2,1,0:T(8,128)(2,1)S(1)}, u32[]{:S(2)}, u32[]{:S(2)}) collective-permute-start(bf16[4,34,24,128]{3,2,1,0:T(8,128)(2,1)S(1)} %bitcast.15), channel_id=1, source_target_pairs={{0,128},{128,0},{1,129},{129,1},{2,130},{130,2},{3,131},{131,3},{4... | collective-permute-start | bytes 2506760 | tf_op jit(solution)/shard_map/ppermute | solution.py:399
  95.8 2.0 %own_share.1 = (bf16[544,128]{1,0:T(8,128)(2,1)S(1)}, f32[8,64,544]{2,1,0:T(8,128)S(1)}, f32[8,544]{1,0:T(8,128)S(1)}, f32[8,544]{1,0:T(8,128)S(1)}) custom-call(s32[1]{0:T(128)} %bitcast.3.at_ref, bf16[32,40,128]{2,1,0:T(8,128)(2,1)S(1)} %all_to_all.10.own_ref, bf16[4,34,24,128]{3,2,1,0:T(8,128)(2,1)S(1)} %bitcast.16), custom_call_target="tpu_custom_call" | custom-call | flops 427819008 | bytes 1048576 | tf_op jit(solution)/shard_map/own_share/pallas_call | solution.py:194
  97.8 0.3 collective-permute-done.share_ref
  98.1 2.0 %other_share.1 = (f32[8,64,544]{2,1,0:T(8,128)S(1)}, f32[8,544]{1,0:T(8,128)S(1)}, f32[8,544]{1,0:T(8,128)S(1)}) custom-call(bf16[544,128]{1,0:T(8,128)(2,1)S(1)} %get-tuple-element.24.query_ref, bf16[4,34,24,128]{3,2,1,0:T(8,128)(2,1)S(1)} %collective-permute-done.share_ref), custom_call_target="tpu_custom_call" | custom-call | flops 427819008 | bytes 1048576 | tf_op jit(solution)/shard_map/other_share/pallas_call | solution.py:207
  100.1 0.0 copy-start.2
  100.1 0.0 copy-start.1
  100.1 0.0 copy-start.3
  100.1 0.0 copy-start
  100.2 1.5 %guide.1 = bf16[32,24,128]{2,1,0:T(8,128)(2,1)} custom-call(f32[4,128]{1,0:T(4,128)S(1)} %get-tuple-element.22.guide_ref, bf16[544,128]{1,0:T(8,128)(2,1)S(1)} %get-tuple-element.24.query_ref, bf16[32,128]{1,0:T(8,128)(2,1)S(1)} %get-tuple-element.25.bias_ref, f32[16,64]{1,0:T(8,128)S(1)} %get-tuple-element.26.term_ref, ...), custom_call_target="tpu_custom_call" | custom-call | tf_op jit(solution)/shard_map/guide/pallas_call | solution.py:257
  101.7 4.8 %all-to-all-start.1 = ((bf16[32,24,128]{2,1,0:T(8,128)(2,1)}), bf16[32,24,128]{2,1,0:T(8,128)(2,1)S(1)}, u32[]{:S(2)}, u32[]{:S(2)}) async-start(bf16[32,24,128]{2,1,0:T(8,128)(2,1)} %guide.1), calls=%async_computation.1 | async-start | bytes 393216 | tf_op jit(solution)/shard_map/all_to_all | solution.py:404
  106.5 0.0 copy-done.2
  106.5 0.1 reshape.20
  106.6 1.3 collective-permute-start.2
  107.9 4.6 %collective-permute-start.1 = (f32[16,128]{1,0:T(8,128)S(1)}, f32[16,128]{1,0:T(8,128)S(1)}, u32[]{:S(2)}, u32[]{:S(2)}) collective-permute-start(f32[16,128]{1,0:T(8,128)S(1)} %reshape.20), channel_id=1, source_target_pairs={{0,1},{1,2},{2,3},{3,4},{4,5},{5,6},{6,7},{7,8},{8,9},{9,10},{10,1... | collective-permute-start | bytes 24584 | tf_op jit(solution)/shard_map/ppermute | solution.py:417
  112.5 0.1 stack_reshape.3
  112.6 0.0 copy-done.1
  112.6 0.0 copy-done.3
  112.7 2.3 %collective-permute-done.2 = f32[16,128]{1,0:T(8,128)S(1)} collective-permute-done((f32[16,128]{1,0:T(8,128)S(1)}, f32[16,128]{1,0:T(8,128)S(1)}, u32[]{:S(2)}, u32[]{:S(2)}) %collective-permute-start.2) | collective-permute-done | bytes 8224 | tf_op jit(solution)/shard_map/ppermute | solution.py:418
  114.9 0.0 collective-permute-done.1
  114.9 11.0 %all-to-all-done.1 = bf16[32,24,128]{2,1,0:T(8,128)(2,1)S(1)} async-done(((bf16[32,24,128]{2,1,0:T(8,128)(2,1)}), bf16[32,24,128]{2,1,0:T(8,128)(2,1)S(1)}, u32[]{:S(2)}, u32[]{:S(2)}) %all-to-all-start.1) | async-done | bytes 196640 | tf_op jit(solution)/shard_map/all_to_all | solution.py:404
  126.0 0.1 iota.13.flag_ref
  126.0 1.9 %collective-permute-start.3 = (f32[24,128]{1,0:T(8,128)S(1)}, f32[24,128]{1,0:T(8,128)S(1)}, u32[]{:S(2)}, u32[]{:S(2)}) collective-permute-start(f32[24,128]{1,0:T(8,128)S(1)} %convert_reduce_fusion.mine_ref), channel_id=1, source_target_pairs={{0,128},{128,0},{1,129},{129,1},{2,130},{130,2},{3,131},{131,3},{4... | collective-permute-start | bytes 36872 | tf_op jit(solution)/shard_map/ppermute | solution.py:424
  128.0 1.1 collective-permute-done.3.other_ref
  129.1 0.0 copy-done
  129.1 2.1 %decode.1 = (f32[32,64]{1,0:T(8,128)}, f32[3,2,64]{2,1,0:T(2,128)}) custom-call(f32[8,128]{1,0:T(8,128)S(1)} %iota.13.flag_ref, f32[24,128]{1,0:T(8,128)S(1)} %convert_reduce_fusion.mine_ref, f32[24,128]{1,0:T(8,128)S(1)} %collective-permute-done.3.other_ref, f32[3,16,128]{2,1,0:T(8,128)S(1)} %pad_maximum_fusion.1.noisy_ref, ...), custom_call_target="tpu_custom_call" | custom-call | tf_op jit(solution)/shard_map/decode/pallas_call | solution.py:347
  (11 shorter events, 0.1 us)
Async XLA Ops:
  93.8 4.3 %collective-permute-start = (bf16[4,34,24,128]{3,2,1,0:T(8,128)(2,1)S(1)}, bf16[4,34,24,128]{3,2,1,0:T(8,128)(2,1)S(1)}, u32[]{:S(2)}, u32[]{:S(2)}) collective-permute-start(bf16[4,34,24,128]{3,2,1,0:T(8,128)(2,1)S(1)} %bitcast.15), channel_id=1, source_target_pairs={{0,128},{128,0},{1,129},{129,1},{2,130},{130,2},{3,131},{131,3},{4... | collective-permute-start | bytes 2506760 | tf_op jit(solution)/shard_map/ppermute | solution.py:399
  100.1 6.4 %copy-start.2 = (f32[32,64]{1,0:T(8,128)S(1)}, f32[32,64]{1,0:T(8,128)}, u32[]{:S(2)}) copy-start(f32[32,64]{1,0:T(8,128)} %param.22) | copy-start | bytes 24580
  100.1 12.5 %copy-start.1 = (bf16[3,3,384,3]{2,3,1,0:T(4,128)(2,1)S(1)}, bf16[3,3,384,3]{2,3,1,0:T(4,128)(2,1)}, u32[]{:S(2)}) copy-start(bf16[3,3,384,3]{2,3,1,0:T(4,128)(2,1)} %param.25) | copy-start | bytes 62212
  100.1 12.5 %copy-start.3 = (f32[384]{0:T(512)S(1)}, f32[384]{0:T(512)}, u32[]{:S(2)}) copy-start(f32[384]{0:T(512)} %param.24) | copy-start | bytes 4612
  100.1 29.0 %copy-start = (bf16[3,3,16,384]{3,2,1,0:T(8,128)(2,1)S(1)}, bf16[3,3,16,384]{3,2,1,0:T(8,128)(2,1)}, u32[]{:S(2)}) copy-start(bf16[3,3,16,384]{3,2,1,0:T(8,128)(2,1)} %param.23) | copy-start | bytes 331780
  101.7 24.2 %all-to-all-start.1 = ((bf16[32,24,128]{2,1,0:T(8,128)(2,1)}), bf16[32,24,128]{2,1,0:T(8,128)(2,1)S(1)}, u32[]{:S(2)}, u32[]{:S(2)}) async-start(bf16[32,24,128]{2,1,0:T(8,128)(2,1)} %guide.1), calls=%async_computation.1 | async-start | bytes 393216 | tf_op jit(solution)/shard_map/all_to_all | solution.py:404
  106.6 8.3 %collective-permute-start.2 = (f32[16,128]{1,0:T(8,128)S(1)}, f32[16,128]{1,0:T(8,128)S(1)}, u32[]{:S(2)}, u32[]{:S(2)}) collective-permute-start(f32[16,128]{1,0:T(8,128)S(1)} %reshape.20), channel_id=1, source_target_pairs={{1,0},{2,1},{3,2},{4,3},{5,4},{6,5},{7,6},{8,7},{9,8},{10,9},{11,1... | collective-permute-start | bytes 24584 | tf_op jit(solution)/shard_map/ppermute | solution.py:418
  107.9 7.0 %collective-permute-start.1 = (f32[16,128]{1,0:T(8,128)S(1)}, f32[16,128]{1,0:T(8,128)S(1)}, u32[]{:S(2)}, u32[]{:S(2)}) collective-permute-start(f32[16,128]{1,0:T(8,128)S(1)} %reshape.20), channel_id=1, source_target_pairs={{0,1},{1,2},{2,3},{3,4},{4,5},{5,6},{6,7},{7,8},{8,9},{9,10},{10,1... | collective-permute-start | bytes 24584 | tf_op jit(solution)/shard_map/ppermute | solution.py:417
  126.0 3.1 %collective-permute-start.3 = (f32[24,128]{1,0:T(8,128)S(1)}, f32[24,128]{1,0:T(8,128)S(1)}, u32[]{:S(2)}, u32[]{:S(2)}) collective-permute-start(f32[24,128]{1,0:T(8,128)S(1)} %convert_reduce_fusion.mine_ref), channel_id=1, source_target_pairs={{0,128},{128,0},{1,129},{129,1},{2,130},{130,2},{3,131},{131,3},{4... | collective-permute-start | bytes 36872 | tf_op jit(solution)/shard_map/ppermute | solution.py:424

commit v9 on v8

--- a/solution.py
+++ b/solution.py
@@ -18,6 +18,7 @@
 F32 = jnp.float32
 VMEM = pl.BlockSpec(memory_space=pltpu.VMEM)
 SMEM = pl.BlockSpec(memory_space=pltpu.SMEM)
+HBM = pl.BlockSpec(memory_space=pltpu.HBM)
 GRANT = pltpu.CompilerParams(vmem_limit_bytes=12 << 20)
 
 
@@ -29,99 +30,45 @@
     return lax.dot_general(a, b, (dims, ((), ())), preferred_element_type=F32, **kw)
 
 
-def pack_kernel(
-    core_ref, head_ref, q_ref, k_ref, v_ref, w_ref, kb_ref, ms_ref, key_ref, mouse_ref, guide_ref,
-    out_ref, bias_ref, term_ref, line_ref,
-    q_tmp, k_tmp, v_tmp, w_tmp, kb_tmp, ms_tmp, key_tmp, mouse_tmp, guide_tmp, sems,
-):
+def pack_kernel(core_ref, q_ref, k_ref, v_ref, w_ref, out_ref, q_tmp, k_tmp, v_tmp, w_tmp, sems):
     heads, _, hd = out_ref.shape
     rows = q_tmp.shape[0]
     half = rows // 2
-    frames = kb_tmp.shape[0]
     mine = pl.ds(pl.multiple_of(core_ref[0] * rows, rows), rows)
-    head = pl.ds(pl.multiple_of(head_ref[0] * hd, hd), hd)
-    ids = [
-        pltpu.make_async_copy(kb_ref, kb_tmp, sems.at[4]),
-        pltpu.make_async_copy(ms_ref, ms_tmp, sems.at[5]),
-        pltpu.make_async_copy(guide_ref, guide_tmp, sems.at[6]),
-    ]
-    width = w_tmp.shape[1]
-    cuts = [slice(n * width // 2, (n + 1) * width // 2) for n in range(2)]
     copies = [
         pltpu.make_async_copy(q_ref.at[mine, :], q_tmp, sems.at[0]),
         pltpu.make_async_copy(k_ref.at[mine, :], k_tmp, sems.at[1]),
         pltpu.make_async_copy(v_ref.at[mine, :], v_tmp, sems.at[2]),
-        pltpu.make_async_copy(w_ref.at[:, cuts[0]], w_tmp.at[:, cuts[0]], sems.at[3]),
-        pltpu.make_async_copy(w_ref.at[:, cuts[1]], w_tmp.at[:, cuts[1]], sems.at[7]),
+        pltpu.make_async_copy(w_ref, w_tmp, sems.at[3]),
     ]
-    for copy in ids + copies:
+    for copy in copies:
         copy.start()
-    for copy in ids:
+    for source, first, copy in ((q_tmp, 0, copies[0]), (k_tmp, rows, copies[1])):
         copy.wait()
-    picks = []
-    for f in range(frames):
-        at = 8 + 2 * f
-        picks += [
-            pltpu.make_async_copy(key_ref.at[kb_tmp[f], :, head], key_tmp.at[f], sems.at[at]),
-            pltpu.make_async_copy(mouse_ref.at[ms_tmp[f], :, head], mouse_tmp.at[f], sems.at[at + 1]),
-        ]
-    for copy in picks:
-        copy.start()
-    for copy in copies[:2]:
+        for h in range(heads):
+            out_ref[h, first : first + rows, :] = source[:, h * hd : (h + 1) * hd]
+    for copy in copies[2:]:
         copy.wait()
     for h in range(heads):
-        cols = slice(h * hd, (h + 1) * hd)
-        out_ref[h, 0:rows, :] = q_tmp[:, cols]
-        out_ref[h, rows : 2 * rows, :] = k_tmp[:, cols]
-    for copy in copies[2:4]:
-        copy.wait()
-    for h in range(heads):
-        if h == heads // 2:
-            copies[4].wait()
         cols = slice(h * hd, (h + 1) * hd)
         projected = dot(v_tmp[:, cols], w_tmp[:, cols], ((1,), (1,)))
         projected = jnp.concatenate([projected[:half], projected[half:]], axis=1)
         out_ref[h, 2 * rows :, :] = projected.astype(BF)
-    for copy in picks:
-        copy.wait()
-    rows_key = key_tmp[...].astype(F32)
-    rows_mouse = mouse_tmp[...].astype(F32)
-    bias_key, bias_mouse = rows_key[:, 0, :], rows_mouse[:, 0, :]
-    bias = [bias_key + bias_mouse, bias_mouse, bias_key, jnp.zeros_like(bias_key)]
-    bias_ref[...] = jnp.concatenate(bias, axis=0).astype(BF)
-    terms = jnp.concatenate([rows_key[:, 1, :], rows_mouse[:, 1, :]], axis=0).astype(BF)
-    term_ref[...] = dot(terms, w_tmp[:, head], ((1,), (1,)))
-    for b in range(line_ref.shape[0]):
-        line_ref[b : b + 1, :] = jnp.full((1, hd), guide_tmp[b], F32)
-
-
-def pack(
-    core, head, queries, keys, values, weight_t, keyboard, mouse, key_table, mouse_table, guidance, rows
-):
+
+
+def pack(core, queries, keys, values, weight_t, rows):
     width = queries.shape[1]
     heads = width // HEAD_DIM
-    frames = keyboard.shape[0]
-    outs = weight_t.shape[0]
-    arrays = (queries, keys, values, weight_t, keyboard, mouse, key_table, mouse_table, guidance)
     return pl.pallas_call(
         pack_kernel,
-        in_specs=[SMEM, SMEM] + [pl.BlockSpec(memory_space=pltpu.HBM)] * len(arrays),
-        out_specs=[VMEM] * 4,
-        out_shape=[
-            jax.ShapeDtypeStruct((heads, 2 * rows + rows // 2, HEAD_DIM), BF),
-            jax.ShapeDtypeStruct((4 * frames, HEAD_DIM), BF),
-            jax.ShapeDtypeStruct((2 * frames, outs), F32),
-            jax.ShapeDtypeStruct((guidance.shape[0], HEAD_DIM), F32),
-        ],
+        in_specs=[SMEM] + [HBM] * 4,
+        out_specs=VMEM,
+        out_shape=jax.ShapeDtypeStruct((heads, 2 * rows + rows // 2, HEAD_DIM), BF),
         scratch_shapes=[pltpu.VMEM((rows, width), BF)] * 3
-        + [pltpu.VMEM(weight_t.shape, BF)]
-        + [pltpu.SMEM((frames,), jnp.int32)] * 2
-        + [pltpu.VMEM((frames, 2, HEAD_DIM), BF)] * 2
-        + [pltpu.SMEM(guidance.shape, F32)]
-        + [pltpu.SemaphoreType.DMA((8 + 2 * frames,))],
+        + [pltpu.VMEM(weight_t.shape, BF), pltpu.SemaphoreType.DMA((4,))],
         name="pack",
         compiler_params=GRANT,
-    )(core[None], head[None], *(in_hbm(a) for a in arrays))
+    )(core[None], *(in_hbm(a) for a in (queries, keys, values, weight_t)))
 
 
 def share_body(rows, sets, heads, query, share_ref, sum_ref, top_ref, total_ref):
@@ -155,8 +102,24 @@
         sum_ref[frame] = dot(values, raised, ((0,), (0,)))
 
 
-def own_share_kernel(rows, sets, at_ref, own_ref, share_ref, query_ref, *out_refs):
+def own_share_kernel(
+    rows, sets, at_ref, head_ref, own_ref, share_ref, w_ref, kb_ref, ms_ref, key_ref, mouse_ref, guide_ref,
+    query_ref, sum_ref, top_ref, total_ref, bias_ref, term_ref, line_ref,
+    w_tmp, kb_tmp, ms_tmp, key_tmp, mouse_tmp, guide_tmp, sems,
+):
     heads, _, hd = own_ref.shape
+    frames = kb_tmp.shape[0]
+    head = pl.ds(pl.multiple_of(head_ref[0] * hd, hd), hd)
+    ids = [
+        pltpu.make_async_copy(kb_ref, kb_tmp, sems.at[0]),
+        pltpu.make_async_copy(ms_ref, ms_tmp, sems.at[1]),
+    ]
+    picks = [
+        pltpu.make_async_copy(guide_ref, guide_tmp, sems.at[2]),
+        pltpu.make_async_copy(w_ref.at[:, head], w_tmp, sems.at[3]),
+    ]
+    for copy in ids + picks:
+        copy.start()
     count = share_ref.shape[0]
     before, after = lax.rem(at_ref[0] + (count - 1), count), lax.rem(at_ref[0] + 1, count)
     earlier = share_ref[pl.ds(before, 1), heads + 1, 0:rows, :].reshape(rows, hd)
@@ -165,11 +128,28 @@
     query_ref[0:rows, :] = earlier
     query_ref[rows : rows + heads * rows, :] = query
     query_ref[rows + heads * rows :, :] = later
-    share_body(rows, sets, heads, query_ref[...], share_ref, *out_refs)
-
-
-def other_share_kernel(rows, sets, heads, query_ref, share_ref, *out_refs):
-    share_body(rows, sets, heads, query_ref[...], share_ref, *out_refs)
+    for copy in ids:
+        copy.wait()
+    for f in range(frames):
+        at = 4 + 2 * f
+        picks += [
+            pltpu.make_async_copy(key_ref.at[kb_tmp[f], :, head], key_tmp.at[f], sems.at[at]),
+            pltpu.make_async_copy(mouse_ref.at[ms_tmp[f], :, head], mouse_tmp.at[f], sems.at[at + 1]),
+        ]
+    for copy in picks[2:]:
+        copy.start()
+    share_body(rows, sets, heads, query_ref[...], share_ref, sum_ref, top_ref, total_ref)
+    for copy in picks:
+        copy.wait()
+    rows_key = key_tmp[...].astype(F32)
+    rows_mouse = mouse_tmp[...].astype(F32)
+    bias_key, bias_mouse = rows_key[:, 0, :], rows_mouse[:, 0, :]
+    bias = [bias_key + bias_mouse, bias_mouse, bias_key, jnp.zeros_like(bias_key)]
+    bias_ref[...] = jnp.concatenate(bias, axis=0).astype(BF)
+    terms = jnp.concatenate([rows_key[:, 1, :], rows_mouse[:, 1, :]], axis=0).astype(BF)
+    term_ref[...] = dot(terms, w_tmp[...], ((1,), (1,)))
+    for b in range(line_ref.shape[0]):
+        line_ref[b : b + 1, :] = jnp.full((1, hd), guide_tmp[b], F32)
 
 
 def share_shapes(share, heads, rows, sets, outs):
@@ -189,30 +169,32 @@
     return tokens, shapes, cost
 
 
-def own_share_attention(place, own, share, rows, sets, outs):
+def own_share_attention(
+    place, head, own, share, weight_t, keyboard, mouse, key_table, mouse_table, guidance, rows, sets
+):
+    outs = weight_t.shape[0]
+    frames = keyboard.shape[0]
     tokens, shapes, cost = share_shapes(share, own.shape[0], rows, sets, outs)
+    arrays = (weight_t, keyboard, mouse, key_table, mouse_table, guidance)
     return pl.pallas_call(
         functools.partial(own_share_kernel, rows, sets),
-        in_specs=[SMEM, VMEM, VMEM],
-        out_specs=[VMEM] * 4,
-        out_shape=[jax.ShapeDtypeStruct((tokens, HEAD_DIM), BF)] + shapes,
+        in_specs=[SMEM, SMEM, VMEM, VMEM] + [HBM] * len(arrays),
+        out_specs=[VMEM] * 7,
+        out_shape=[jax.ShapeDtypeStruct((tokens, HEAD_DIM), BF)]
+        + shapes
+        + [
+            jax.ShapeDtypeStruct((4 * frames, HEAD_DIM), BF),
+            jax.ShapeDtypeStruct((2 * frames, outs), F32),
+            jax.ShapeDtypeStruct((guidance.shape[0], HEAD_DIM), F32),
+        ],
+        scratch_shapes=[pltpu.VMEM((outs, HEAD_DIM), BF)]
+        + [pltpu.SMEM((frames,), jnp.int32)] * 2
+        + [pltpu.VMEM((frames, 2, HEAD_DIM), BF)] * 2
+        + [pltpu.SMEM(guidance.shape, F32), pltpu.SemaphoreType.DMA((4 + 2 * frames,))],
         cost_estimate=cost,
         name="own_share",
         compiler_params=GRANT,
-    )(place[None], own, share)
-
-
-def other_share_attention(query, share, heads, rows, sets, outs):
-    _, shapes, cost = share_shapes(share, heads, rows, sets, outs)
-    return pl.pallas_call(
-        functools.partial(other_share_kernel, rows, sets, heads),
-        in_specs=[VMEM, VMEM],
-        out_specs=[VMEM] * 3,
-        out_shape=shapes,
-        cost_estimate=cost,
-        name="other_share",
-        compiler_params=GRANT,
-    )(query, share)
+    )(place[None], head[None], own, share, *(in_hbm(a) for a in arrays))
 
 
 def guide_kernel(rows, guide_ref, query_ref, bias_ref, term_ref, *refs):
@@ -251,17 +233,29 @@
         out_ref[:, side * half : (side + 1) * half, :] = packed[side : side + heads]
 
 
-def guide(lines, query, bias, term, shares, rows, outs):
+def other_share_kernel(
+    rows, sets, query_ref, share_ref, line_ref, bias_ref, term_ref,
+    sum_ref, top_ref, total_ref, out_ref, sum_tmp, top_tmp, total_tmp,
+):
+    heads = out_ref.shape[0]
+    share_body(rows, sets, heads, query_ref[...], share_ref, sum_tmp, top_tmp, total_tmp)
+    shares = (sum_ref, top_ref, total_ref, sum_tmp, top_tmp, total_tmp)
+    guide_kernel(rows, line_ref, query_ref, bias_ref, term_ref, *shares, out_ref)
+
+
+def other_share_and_guide(query, share, lines, bias, term, first, rows, sets, outs):
     heads = query.shape[0] // rows - 2
-    arrays = [array for share in shares for array in share]
+    _, shapes, cost = share_shapes(share, heads, rows, sets, outs)
     return pl.pallas_call(
-        functools.partial(guide_kernel, rows),
-        in_specs=[VMEM] * (4 + len(arrays)),
+        functools.partial(other_share_kernel, rows, sets),
+        in_specs=[VMEM] * 8,
         out_specs=VMEM,
-        out_shape=pltpu.VMEM((heads, 3 * (rows // 2), 2 * outs), BF),
-        name="guide",
+        out_shape=jax.ShapeDtypeStruct((heads, 3 * (rows // 2), 2 * outs), BF),
+        scratch_shapes=[pltpu.VMEM(a.shape, a.dtype) for a in shapes],
+        cost_estimate=cost,
+        name="other_share",
         compiler_params=GRANT,
-    )(lines, query, bias, term, *arrays)
+    )(query, share, lines, bias, term, *first)
 
 
 def decode_kernel(
@@ -387,19 +381,18 @@
     swap = [(0, 1), (1, 0)]
 
     weight_t = out_weight.T
-    packed, bias, term, lines = pack(
-        core, xh * sets + z, queries, keys, values, weight_t,
-        keyboard, mouse, key_table, mouse_table, guidance, rows,
-    )
+    packed = pack(core, queries, keys, values, weight_t, rows)
     own = lax.all_to_all(packed, ("xh", "z"), 0, 0, tiled=True)
     moving = jnp.concatenate(
         [own[:, rows:], own[:1, : rows + rows // 2], own[-1:, : rows + rows // 2]], axis=0
     )
     share = lax.all_gather(moving, "xl")
     other_share = lax.ppermute(share, "branch", swap)
-    query, *first = own_share_attention(xl, own, share, rows, sets, outs)
-    second = other_share_attention(query, other_share, own.shape[0], rows, sets, outs)
-    part = guide(lines, query, bias, term, [first, second], rows, outs)
+    query, *first, bias, term, lines = own_share_attention(
+        xl, xh * sets + z, own, share, weight_t,
+        keyboard, mouse, key_table, mouse_table, guidance, rows, sets,
+    )
+    part = other_share_and_guide(query, other_share, lines, bias, term, first, rows, sets, outs)
     part, latent, conv_out, gain = lax.optimization_barrier((part, latent, conv_out, gain))
     returned = lax.all_to_all(part, ("xh", "z"), 0, 0, tiled=True)
 

time: 133 us -> 134 us (level)
  waiting for transfers between devices: 14.7 us -> 16.3 us
  starting transfers between devices: 14.5 us -> 12.9 us
    ppermute x1, waiting for transfers between devices: 2.26 us -> 4.14 us  [shards(): after = lax.ppermute(noisy, places, [(i + 1, i) for i in range(count - 1)])]
    pallas_call x1, Pallas kernels: 2.03 us -> 3.7 us  [own_share_attention(): pl.pallas_call(functools.partial(own_share_kernel, rows, sets), in_specs=...]
    ppermute x1, starting transfers between devices: 4.59 us -> 2.92 us  [shards(): before = lax.ppermute(noisy, places, [(i, i + 1) for i in range(count - 1)])]
    pallas_call x3 -> x2, Pallas kernels: 5.73 us -> 5.17 us  [the longest x1 3.43 us: other_share_and_guide(): pl.pallas_call(functools.partial(other_share_kernel, rows, sets), in_spec...]
  transfers between devices with their start and end apart: 5 -> 5, of which waited for: 4 -> 3; matrix products, arithmetic and copies ran while one was open for 0% -> 0% of each run, Pallas kernels for 2% -> 3%
where the time goes in v9:
time: 134 us; the launch traced here: 132 us
  blocking collectives  90.9 us (68%)
  waiting for transfers between devices  16.3 us (12%)
  starting transfers between devices  12.9 us (10%)
  Pallas kernels  10.9 us (8%)
    all_to_all x1, blocking collectives, shards(): own = lax.all_to_all(packed, ('xh', 'z'), 0, 0, tiled=True)  69.6 us
    all_gather x1, blocking collectives, shards(): share = lax.all_gather(moving, 'xl')  21.3 us
    all_to_all x1, waiting for transfers between devices, shards(): returned = lax.all_to_all(part, ('xh', 'z'), 0, 0, tiled=True)  11 us
    all_to_all x1, starting transfers between devices, shards(): returned = lax.all_to_all(part, ('xh', 'z'), 0, 0, tiled=True)  4.78 us
    ppermute x1, waiting for transfers between devices, shards(): after = lax.ppermute(noisy, places, [(i + 1, i) for i in range(count - 1)])  4.14 us
    pallas_call x1, Pallas kernels, own_share_attention(): pl.pallas_call(functools.partial(own_share_kernel, rows, sets), in_specs=...  3.7 us
    pallas_call x1, Pallas kernels, other_share_and_guide(): pl.pallas_call(functools.partial(other_share_kernel, rows, sets), in_spec...  3.43 us
    ppermute x1, starting transfers between devices, shards(): before = lax.ppermute(noisy, places, [(i, i + 1) for i in range(count - 1)])  2.92 us
  transfers between devices with their start and end apart: 5, of which 3 were waited for; matrix products, arithmetic and copies ran while one was open for 0% of the time, Pallas kernels for 3%

profile of v9, /device:TPU:80, one launch (start us, length us, event | category | flops | bytes accessed | tf_op | source)
XLA Modules:
  0.0 132.3 jit_solution(2687748221050527530)
XLA Ops:
  0.6 1.7 %pack.1 = bf16[32,40,128]{2,1,0:T(8,128)(2,1)S(1)} custom-call(s32[1]{0:T(128)} %bitcast.2.core_ref, bf16[32,4096]{1,0:T(8,128)(2,1)} %q_ref.1, bf16[32,4096]{1,0:T(8,128)(2,1)} %k_ref.1, bf16[32,4096]{1,0:T(8,128)(2,1)} %v_ref.1, bf16[64,4096]{1,0:T(8,128)(2,1)} %bitcast.19), custom_call_target="tpu_custom_call" | custom-call | tf_op jit(solution)/shard_map/pack/pallas_call | solution.py:62
  2.4 69.6 %all_to_all.10.own_ref = bf16[32,40,128]{2,1,0:T(8,128)(2,1)S(1)} all-to-all(bf16[32,40,128]{2,1,0:T(8,128)(2,1)S(1)} %pack.1), channel_id=1, replica_groups=mesh['groups'=2,'branch'=2,'xl'=4,'xh'=2,'z'=16] {'xh','z'}, dimensions={0} | all-to-all | bytes 655360 | tf_op jit(solution)/shard_map/all_to_all | solution.py:385
  72.0 21.3 %all-gather = bf16[136,24,128]{2,1,0:T(8,128)(2,1)S(1)} all-gather(bf16[34,24,128]{2,1,0:T(8,128)(2,1)S(1)} %pad_maximum_fusion), channel_id=2, replica_groups=mesh['groups'=2,'branch'=2,'xl'=4,'xh'=2,'z'=16] {'xl'}, dimensions={0}, use_global_device_ids=true | all-gather | bytes 1044480 | tf_op jit(solution)/shard_map/all_gather | solution.py:389
  93.4 1.9 %collective-permute-start = (bf16[4,34,24,128]{3,2,1,0:T(8,128)(2,1)S(1)}, bf16[4,34,24,128]{3,2,1,0:T(8,128)(2,1)S(1)}, u32[]{:S(2)}, u32[]{:S(2)}) collective-permute-start(bf16[4,34,24,128]{3,2,1,0:T(8,128)(2,1)S(1)} %bitcast.15), channel_id=1, source_target_pairs={{0,128},{128,0},{1,129},{129,1},{2,130},{130,2},{3,131},{131,3},{4... | collective-permute-start | bytes 2506760 | tf_op jit(solution)/shard_map/ppermute | solution.py:390
  95.3 3.7 %own_share.1 = (bf16[544,128]{1,0:T(8,128)(2,1)S(1)}, f32[8,64,544]{2,1,0:T(8,128)S(1)}, f32[8,544]{1,0:T(8,128)S(1)}, f32[8,544]{1,0:T(8,128)S(1)}, bf16[32,128...) custom-call(s32[1]{0:T(128)} %bitcast.at_ref, s32[1]{0:T(128)} %bitcast.1.head_ref, ...), custom_call_target="tpu_custom_call" | custom-call | flops 427819008 | bytes 1048576 | tf_op jit(solution)/shard_map/own_share/pallas_call | solution.py:179
  99.0 0.0 collective-permute-done.share_ref
  99.0 0.0 copy-start.2
  99.1 0.0 copy-start.1
  99.1 0.0 copy-start.3
  99.1 0.0 copy-start
  99.1 3.4 %other_share.1 = bf16[32,24,128]{2,1,0:T(8,128)(2,1)} custom-call(bf16[544,128]{1,0:T(8,128)(2,1)S(1)} %get-tuple-element.18.query_ref, bf16[4,34,24,128]{3,2,1,0:T(8,128)(2,1)S(1)} %collective-permute-done.share_ref, f32[4,128]{1,0:T(4,128)S(1)} %get-tuple-element.19.line_ref, bf16[32,128]{1,0:T(8,128)(2,1)S(1)} %get-tuple-element.20.bias_ref, ...), custom_call_target="tpu_custom_call" | custom-call | flops 427819008 | bytes 1048576 | tf_op jit(solution)/shard_map/other_share/pallas_call | solution.py:249
  102.5 4.8 %all-to-all-start.1 = ((bf16[32,24,128]{2,1,0:T(8,128)(2,1)}), bf16[32,24,128]{2,1,0:T(8,128)(2,1)S(1)}, u32[]{:S(2)}, u32[]{:S(2)}) async-start(bf16[32,24,128]{2,1,0:T(8,128)(2,1)} %other_share.1), calls=%async_computation.1 | async-start | bytes 393216 | tf_op jit(solution)/shard_map/all_to_all | solution.py:397
  107.3 0.0 copy-done.2
  107.4 0.1 reshape.20
  107.4 2.9 %collective-permute-start.1 = (f32[16,128]{1,0:T(8,128)S(1)}, f32[16,128]{1,0:T(8,128)S(1)}, u32[]{:S(2)}, u32[]{:S(2)}) collective-permute-start(f32[16,128]{1,0:T(8,128)S(1)} %reshape.20), channel_id=1, source_target_pairs={{0,1},{1,2},{2,3},{3,4},{4,5},{5,6},{6,7},{7,8},{8,9},{9,10},{10,1... | collective-permute-start | bytes 24584 | tf_op jit(solution)/shard_map/ppermute | solution.py:410
  110.4 1.3 collective-permute-start.2
  111.7 0.1 stack_reshape.3
  111.8 0.0 copy-done.1
  111.8 0.0 copy-done.3
  111.9 0.0 collective-permute-done.1
  111.9 4.1 %collective-permute-done.2 = f32[16,128]{1,0:T(8,128)S(1)} collective-permute-done((f32[16,128]{1,0:T(8,128)S(1)}, f32[16,128]{1,0:T(8,128)S(1)}, u32[]{:S(2)}, u32[]{:S(2)}) %collective-permute-start.2) | collective-permute-done | bytes 8224 | tf_op jit(solution)/shard_map/ppermute | solution.py:411
  116.0 11.0 %all-to-all-done.1 = bf16[32,24,128]{2,1,0:T(8,128)(2,1)S(1)} async-done(((bf16[32,24,128]{2,1,0:T(8,128)(2,1)}), bf16[32,24,128]{2,1,0:T(8,128)(2,1)S(1)}, u32[]{:S(2)}, u32[]{:S(2)}) %all-to-all-start.1) | async-done | bytes 196640 | tf_op jit(solution)/shard_map/all_to_all | solution.py:397
  127.1 0.1 iota.13.flag_ref
  127.1 1.9 %collective-permute-start.3 = (f32[24,128]{1,0:T(8,128)S(1)}, f32[24,128]{1,0:T(8,128)S(1)}, u32[]{:S(2)}, u32[]{:S(2)}) collective-permute-start(f32[24,128]{1,0:T(8,128)S(1)} %convert_reduce_fusion.mine_ref), channel_id=1, source_target_pairs={{0,128},{128,0},{1,129},{129,1},{2,130},{130,2},{3,131},{131,3},{4... | collective-permute-start | bytes 36872 | tf_op jit(solution)/shard_map/ppermute | solution.py:417
  129.1 1.1 collective-permute-done.3.other_ref
  130.2 0.0 copy-done
  130.2 2.1 %decode.1 = (f32[32,64]{1,0:T(8,128)}, f32[3,2,64]{2,1,0:T(2,128)}) custom-call(f32[8,128]{1,0:T(8,128)S(1)} %iota.13.flag_ref, f32[24,128]{1,0:T(8,128)S(1)} %convert_reduce_fusion.mine_ref, f32[24,128]{1,0:T(8,128)S(1)} %collective-permute-done.3.other_ref, f32[3,16,128]{2,1,0:T(8,128)S(1)} %pad_maximum_fusion.1.noisy_ref, ...), custom_call_target="tpu_custom_call" | custom-call | tf_op jit(solution)/shard_map/decode/pallas_call | solution.py:341
  (11 shorter events, 0.1 us)
Async XLA Ops:
  93.4 5.7 %collective-permute-start = (bf16[4,34,24,128]{3,2,1,0:T(8,128)(2,1)S(1)}, bf16[4,34,24,128]{3,2,1,0:T(8,128)(2,1)S(1)}, u32[]{:S(2)}, u32[]{:S(2)}) collective-permute-start(bf16[4,34,24,128]{3,2,1,0:T(8,128)(2,1)S(1)} %bitcast.15), channel_id=1, source_target_pairs={{0,128},{128,0},{1,129},{129,1},{2,130},{130,2},{3,131},{131,3},{4... | collective-permute-start | bytes 2506760 | tf_op jit(solution)/shard_map/ppermute | solution.py:390
  99.0 8.3 %copy-start.2 = (f32[32,64]{1,0:T(8,128)S(1)}, f32[32,64]{1,0:T(8,128)}, u32[]{:S(2)}) copy-start(f32[32,64]{1,0:T(8,128)} %param.22) | copy-start | bytes 24580
  99.1 12.7 %copy-start.1 = (bf16[3,3,384,3]{2,3,1,0:T(4,128)(2,1)S(1)}, bf16[3,3,384,3]{2,3,1,0:T(4,128)(2,1)}, u32[]{:S(2)}) copy-start(bf16[3,3,384,3]{2,3,1,0:T(4,128)(2,1)} %param.25) | copy-start | bytes 62212
  99.1 12.8 %copy-start.3 = (f32[384]{0:T(512)S(1)}, f32[384]{0:T(512)}, u32[]{:S(2)}) copy-start(f32[384]{0:T(512)} %param.24) | copy-start | bytes 4612
  99.1 31.1 %copy-start = (bf16[3,3,16,384]{3,2,1,0:T(8,128)(2,1)S(1)}, bf16[3,3,16,384]{3,2,1,0:T(8,128)(2,1)}, u32[]{:S(2)}) copy-start(bf16[3,3,16,384]{3,2,1,0:T(8,128)(2,1)} %param.23) | copy-start | bytes 331780
  102.5 24.5 %all-to-all-start.1 = ((bf16[32,24,128]{2,1,0:T(8,128)(2,1)}), bf16[32,24,128]{2,1,0:T(8,128)(2,1)S(1)}, u32[]{:S(2)}, u32[]{:S(2)}) async-start(bf16[32,24,128]{2,1,0:T(8,128)(2,1)} %other_share.1), calls=%async_computation.1 | async-start | bytes 393216 | tf_op jit(solution)/shard_map/all_to_all | solution.py:397
  107.4 4.4 %collective-permute-start.1 = (f32[16,128]{1,0:T(8,128)S(1)}, f32[16,128]{1,0:T(8,128)S(1)}, u32[]{:S(2)}, u32[]{:S(2)}) collective-permute-start(f32[16,128]{1,0:T(8,128)S(1)} %reshape.20), channel_id=1, source_target_pairs={{0,1},{1,2},{2,3},{3,4},{4,5},{5,6},{6,7},{7,8},{8,9},{9,10},{10,1... | collective-permute-start | bytes 24584 | tf_op jit(solution)/shard_map/ppermute | solution.py:410
  110.4 5.6 %collective-permute-start.2 = (f32[16,128]{1,0:T(8,128)S(1)}, f32[16,128]{1,0:T(8,128)S(1)}, u32[]{:S(2)}, u32[]{:S(2)}) collective-permute-start(f32[16,128]{1,0:T(8,128)S(1)} %reshape.20), channel_id=1, source_target_pairs={{1,0},{2,1},{3,2},{4,3},{5,4},{6,5},{7,6},{8,7},{9,8},{10,9},{11,1... | collective-permute-start | bytes 24584 | tf_op jit(solution)/shard_map/ppermute | solution.py:411
  127.1 3.1 %collective-permute-start.3 = (f32[24,128]{1,0:T(8,128)S(1)}, f32[24,128]{1,0:T(8,128)S(1)}, u32[]{:S(2)}, u32[]{:S(2)}) collective-permute-start(f32[24,128]{1,0:T(8,128)S(1)} %convert_reduce_fusion.mine_ref), channel_id=1, source_target_pairs={{0,128},{128,0},{1,129},{129,1},{2,130},{130,2},{3,131},{131,3},{4... | collective-permute-start | bytes 36872 | tf_op jit(solution)/shard_map/ppermute | solution.py:417

commit v10 on v9

--- a/solution.py
+++ b/solution.py
@@ -71,7 +71,7 @@
     )(core[None], *(in_hbm(a) for a in (queries, keys, values, weight_t)))
 
 
-def share_body(rows, sets, heads, query, share_ref, sum_ref, top_ref, total_ref):
+def share_body(rows, sets, heads, query, share_ref, sum_ref, top_ref, total_ref, midway=None):
     hd = query.shape[1]
     half = rows // 2
     outs = sum_ref.shape[1]
@@ -100,6 +100,8 @@
         high = raised[:, 1].reshape(sets * half, -1)
         raised = jnp.concatenate([low, high], axis=0).astype(BF)
         sum_ref[frame] = dot(values, raised, ((0,), (0,)))
+        if midway is not None and frame == frames // 2:
+            midway()
 
 
 def own_share_kernel(
@@ -128,17 +130,22 @@
     query_ref[0:rows, :] = earlier
     query_ref[rows : rows + heads * rows, :] = query
     query_ref[rows + heads * rows :, :] = later
-    for copy in ids:
-        copy.wait()
     for f in range(frames):
         at = 4 + 2 * f
         picks += [
-            pltpu.make_async_copy(key_ref.at[kb_tmp[f], :, head], key_tmp.at[f], sems.at[at]),
-            pltpu.make_async_copy(mouse_ref.at[ms_tmp[f], :, head], mouse_tmp.at[f], sems.at[at + 1]),
+            (key_ref, kb_tmp, key_tmp, f, sems.at[at]),
+            (mouse_ref, ms_tmp, mouse_tmp, f, sems.at[at + 1]),
         ]
-    for copy in picks[2:]:
-        copy.start()
-    share_body(rows, sets, heads, query_ref[...], share_ref, sum_ref, top_ref, total_ref)
+
+    def fetch():
+        for copy in ids:
+            copy.wait()
+        for n in range(2, len(picks)):
+            table, chosen, rows_tmp, f, sem = picks[n]
+            picks[n] = pltpu.make_async_copy(table.at[chosen[f], :, head], rows_tmp.at[f], sem)
+            picks[n].start()
+
+    share_body(rows, sets, heads, query_ref[...], share_ref, sum_ref, top_ref, total_ref, fetch)
     for copy in picks:
         copy.wait()
     rows_key = key_tmp[...].astype(F32)

time: 134 us -> 133 us (level)
  transfers between devices with their start and end apart: 5 -> 5, of which waited for: 3 -> 3; matrix products, arithmetic and copies ran while one was open for 0% -> 0% of each run, Pallas kernels for 3% -> 2%
where the time goes in v10:
time: 133 us; the launch traced here: 132 us
  blocking collectives  90.9 us (68%)
  waiting for transfers between devices  16.3 us (12%)
  starting transfers between devices  12.9 us (10%)
  Pallas kernels  10.4 us (8%)
    all_to_all x1, blocking collectives, shards(): own = lax.all_to_all(packed, ('xh', 'z'), 0, 0, tiled=True)  69.6 us
    all_gather x1, blocking collectives, shards(): share = lax.all_gather(moving, 'xl')  21.3 us
    all_to_all x1, waiting for transfers between devices, shards(): returned = lax.all_to_all(part, ('xh', 'z'), 0, 0, tiled=True)  11 us
    all_to_all x1, starting transfers between devices, shards(): returned = lax.all_to_all(part, ('xh', 'z'), 0, 0, tiled=True)  4.78 us
    ppermute x1, waiting for transfers between devices, shards(): after = lax.ppermute(noisy, places, [(i + 1, i) for i in range(count - 1)])  4.14 us
    pallas_call x1, Pallas kernels, other_share_and_guide(): pl.pallas_call(functools.partial(other_share_kernel, rows, sets), in_spec...  3.43 us
    pallas_call x1, Pallas kernels, own_share_attention(): pl.pallas_call(functools.partial(own_share_kernel, rows, sets), in_specs=...  3.17 us
    ppermute x1, starting transfers between devices, shards(): before = lax.ppermute(noisy, places, [(i, i + 1) for i in range(count - 1)])  2.92 us
  transfers between devices with their start and end apart: 5, of which 3 were waited for; matrix products, arithmetic and copies ran while one was open for 0% of the time, Pallas kernels for 2%

profile of v10, /device:TPU:80, one launch (start us, length us, event | category | flops | bytes accessed | tf_op | source)
XLA Modules:
  0.0 131.8 jit_solution(167108521072535687)
XLA Ops:
  0.6 1.7 %pack.1 = bf16[32,40,128]{2,1,0:T(8,128)(2,1)S(1)} custom-call(s32[1]{0:T(128)} %bitcast.2.core_ref, bf16[32,4096]{1,0:T(8,128)(2,1)} %q_ref.1, bf16[32,4096]{1,0:T(8,128)(2,1)} %k_ref.1, bf16[32,4096]{1,0:T(8,128)(2,1)} %v_ref.1, bf16[64,4096]{1,0:T(8,128)(2,1)} %bitcast.19), custom_call_target="tpu_custom_call" | custom-call | tf_op jit(solution)/shard_map/pack/pallas_call | solution.py:62
  2.4 69.6 %all_to_all.10.own_ref = bf16[32,40,128]{2,1,0:T(8,128)(2,1)S(1)} all-to-all(bf16[32,40,128]{2,1,0:T(8,128)(2,1)S(1)} %pack.1), channel_id=1, replica_groups=mesh['groups'=2,'branch'=2,'xl'=4,'xh'=2,'z'=16] {'xh','z'}, dimensions={0} | all-to-all | bytes 655360 | tf_op jit(solution)/shard_map/all_to_all | solution.py:392
  72.0 21.3 %all-gather = bf16[136,24,128]{2,1,0:T(8,128)(2,1)S(1)} all-gather(bf16[34,24,128]{2,1,0:T(8,128)(2,1)S(1)} %pad_maximum_fusion), channel_id=2, replica_groups=mesh['groups'=2,'branch'=2,'xl'=4,'xh'=2,'z'=16] {'xl'}, dimensions={0}, use_global_device_ids=true | all-gather | bytes 1044480 | tf_op jit(solution)/shard_map/all_gather | solution.py:396
  93.4 1.9 %collective-permute-start = (bf16[4,34,24,128]{3,2,1,0:T(8,128)(2,1)S(1)}, bf16[4,34,24,128]{3,2,1,0:T(8,128)(2,1)S(1)}, u32[]{:S(2)}, u32[]{:S(2)}) collective-permute-start(bf16[4,34,24,128]{3,2,1,0:T(8,128)(2,1)S(1)} %bitcast.15), channel_id=1, source_target_pairs={{0,128},{128,0},{1,129},{129,1},{2,130},{130,2},{3,131},{131,3},{4... | collective-permute-start | bytes 2506760 | tf_op jit(solution)/shard_map/ppermute | solution.py:397
  95.3 3.2 %own_share.1 = (bf16[544,128]{1,0:T(8,128)(2,1)S(1)}, f32[8,64,544]{2,1,0:T(8,128)S(1)}, f32[8,544]{1,0:T(8,128)S(1)}, f32[8,544]{1,0:T(8,128)S(1)}, bf16[32,128...) custom-call(s32[1]{0:T(128)} %bitcast.at_ref, s32[1]{0:T(128)} %bitcast.1.head_ref, ...), custom_call_target="tpu_custom_call" | custom-call | flops 427819008 | bytes 1048576 | tf_op jit(solution)/shard_map/own_share/pallas_call | solution.py:186
  98.5 0.0 collective-permute-done.share_ref
  98.5 0.0 copy-start.2
  98.5 0.0 copy-start.1
  98.5 0.0 copy-start.3
  98.5 0.0 copy-start
  98.6 3.4 %other_share.1 = bf16[32,24,128]{2,1,0:T(8,128)(2,1)} custom-call(bf16[544,128]{1,0:T(8,128)(2,1)S(1)} %get-tuple-element.18.query_ref, bf16[4,34,24,128]{3,2,1,0:T(8,128)(2,1)S(1)} %collective-permute-done.share_ref, f32[4,128]{1,0:T(4,128)S(1)} %get-tuple-element.19.line_ref, bf16[32,128]{1,0:T(8,128)(2,1)S(1)} %get-tuple-element.20.bias_ref, ...), custom_call_target="tpu_custom_call" | custom-call | flops 427819008 | bytes 1048576 | tf_op jit(solution)/shard_map/other_share/pallas_call | solution.py:256
  102.0 4.8 %all-to-all-start.1 = ((bf16[32,24,128]{2,1,0:T(8,128)(2,1)}), bf16[32,24,128]{2,1,0:T(8,128)(2,1)S(1)}, u32[]{:S(2)}, u32[]{:S(2)}) async-start(bf16[32,24,128]{2,1,0:T(8,128)(2,1)} %other_share.1), calls=%async_computation.1 | async-start | bytes 393216 | tf_op jit(solution)/shard_map/all_to_all | solution.py:404
  106.8 0.0 copy-done.2
  106.8 0.1 reshape.20
  106.9 2.9 %collective-permute-start.1 = (f32[16,128]{1,0:T(8,128)S(1)}, f32[16,128]{1,0:T(8,128)S(1)}, u32[]{:S(2)}, u32[]{:S(2)}) collective-permute-start(f32[16,128]{1,0:T(8,128)S(1)} %reshape.20), channel_id=1, source_target_pairs={{0,1},{1,2},{2,3},{3,4},{4,5},{5,6},{6,7},{7,8},{8,9},{9,10},{10,1... | collective-permute-start | bytes 24584 | tf_op jit(solution)/shard_map/ppermute | solution.py:417
  109.8 1.3 collective-permute-start.2
  111.2 0.1 stack_reshape.3
  111.2 0.0 copy-done.1
  111.3 0.0 copy-done.3
  111.3 0.0 collective-permute-done.1
  111.3 4.1 %collective-permute-done.2 = f32[16,128]{1,0:T(8,128)S(1)} collective-permute-done((f32[16,128]{1,0:T(8,128)S(1)}, f32[16,128]{1,0:T(8,128)S(1)}, u32[]{:S(2)}, u32[]{:S(2)}) %collective-permute-start.2) | collective-permute-done | bytes 8224 | tf_op jit(solution)/shard_map/ppermute | solution.py:418
  115.5 11.0 %all-to-all-done.1 = bf16[32,24,128]{2,1,0:T(8,128)(2,1)S(1)} async-done(((bf16[32,24,128]{2,1,0:T(8,128)(2,1)}), bf16[32,24,128]{2,1,0:T(8,128)(2,1)S(1)}, u32[]{:S(2)}, u32[]{:S(2)}) %all-to-all-start.1) | async-done | bytes 196640 | tf_op jit(solution)/shard_map/all_to_all | solution.py:404
  126.5 0.1 iota.13.flag_ref
  126.6 1.9 %collective-permute-start.3 = (f32[24,128]{1,0:T(8,128)S(1)}, f32[24,128]{1,0:T(8,128)S(1)}, u32[]{:S(2)}, u32[]{:S(2)}) collective-permute-start(f32[24,128]{1,0:T(8,128)S(1)} %convert_reduce_fusion.mine_ref), channel_id=1, source_target_pairs={{0,128},{128,0},{1,129},{129,1},{2,130},{130,2},{3,131},{131,3},{4... | collective-permute-start | bytes 36872 | tf_op jit(solution)/shard_map/ppermute | solution.py:424
  128.6 1.1 collective-permute-done.3.other_ref
  129.7 0.0 copy-done
  129.7 2.1 %decode.1 = (f32[32,64]{1,0:T(8,128)}, f32[3,2,64]{2,1,0:T(2,128)}) custom-call(f32[8,128]{1,0:T(8,128)S(1)} %iota.13.flag_ref, f32[24,128]{1,0:T(8,128)S(1)} %convert_reduce_fusion.mine_ref, f32[24,128]{1,0:T(8,128)S(1)} %collective-permute-done.3.other_ref, f32[3,16,128]{2,1,0:T(8,128)S(1)} %pad_maximum_fusion.1.noisy_ref, ...), custom_call_target="tpu_custom_call" | custom-call | tf_op jit(solution)/shard_map/decode/pallas_call | solution.py:348
  (11 shorter events, 0.1 us)
Async XLA Ops:
  93.4 5.1 %collective-permute-start = (bf16[4,34,24,128]{3,2,1,0:T(8,128)(2,1)S(1)}, bf16[4,34,24,128]{3,2,1,0:T(8,128)(2,1)S(1)}, u32[]{:S(2)}, u32[]{:S(2)}) collective-permute-start(bf16[4,34,24,128]{3,2,1,0:T(8,128)(2,1)S(1)} %bitcast.15), channel_id=1, source_target_pairs={{0,128},{128,0},{1,129},{129,1},{2,130},{130,2},{3,131},{131,3},{4... | collective-permute-start | bytes 2506760 | tf_op jit(solution)/shard_map/ppermute | solution.py:397
  98.5 8.3 %copy-start.2 = (f32[32,64]{1,0:T(8,128)S(1)}, f32[32,64]{1,0:T(8,128)}, u32[]{:S(2)}) copy-start(f32[32,64]{1,0:T(8,128)} %param.22) | copy-start | bytes 24580
  98.5 12.7 %copy-start.1 = (bf16[3,3,384,3]{2,3,1,0:T(4,128)(2,1)S(1)}, bf16[3,3,384,3]{2,3,1,0:T(4,128)(2,1)}, u32[]{:S(2)}) copy-start(bf16[3,3,384,3]{2,3,1,0:T(4,128)(2,1)} %param.25) | copy-start | bytes 62212
  98.5 12.8 %copy-start.3 = (f32[384]{0:T(512)S(1)}, f32[384]{0:T(512)}, u32[]{:S(2)}) copy-start(f32[384]{0:T(512)} %param.24) | copy-start | bytes 4612
  98.5 31.2 %copy-start = (bf16[3,3,16,384]{3,2,1,0:T(8,128)(2,1)S(1)}, bf16[3,3,16,384]{3,2,1,0:T(8,128)(2,1)}, u32[]{:S(2)}) copy-start(bf16[3,3,16,384]{3,2,1,0:T(8,128)(2,1)} %param.23) | copy-start | bytes 331780
  102.0 24.5 %all-to-all-start.1 = ((bf16[32,24,128]{2,1,0:T(8,128)(2,1)}), bf16[32,24,128]{2,1,0:T(8,128)(2,1)S(1)}, u32[]{:S(2)}, u32[]{:S(2)}) async-start(bf16[32,24,128]{2,1,0:T(8,128)(2,1)} %other_share.1), calls=%async_computation.1 | async-start | bytes 393216 | tf_op jit(solution)/shard_map/all_to_all | solution.py:404
  106.9 4.4 %collective-permute-start.1 = (f32[16,128]{1,0:T(8,128)S(1)}, f32[16,128]{1,0:T(8,128)S(1)}, u32[]{:S(2)}, u32[]{:S(2)}) collective-permute-start(f32[16,128]{1,0:T(8,128)S(1)} %reshape.20), channel_id=1, source_target_pairs={{0,1},{1,2},{2,3},{3,4},{4,5},{5,6},{6,7},{7,8},{8,9},{9,10},{10,1... | collective-permute-start | bytes 24584 | tf_op jit(solution)/shard_map/ppermute | solution.py:417
  109.8 5.6 %collective-permute-start.2 = (f32[16,128]{1,0:T(8,128)S(1)}, f32[16,128]{1,0:T(8,128)S(1)}, u32[]{:S(2)}, u32[]{:S(2)}) collective-permute-start(f32[16,128]{1,0:T(8,128)S(1)} %reshape.20), channel_id=1, source_target_pairs={{1,0},{2,1},{3,2},{4,3},{5,4},{6,5},{7,6},{8,7},{9,8},{10,9},{11,1... | collective-permute-start | bytes 24584 | tf_op jit(solution)/shard_map/ppermute | solution.py:418
  126.6 3.1 %collective-permute-start.3 = (f32[24,128]{1,0:T(8,128)S(1)}, f32[24,128]{1,0:T(8,128)S(1)}, u32[]{:S(2)}, u32[]{:S(2)}) collective-permute-start(f32[24,128]{1,0:T(8,128)S(1)} %convert_reduce_fusion.mine_ref), channel_id=1, source_target_pairs={{0,128},{128,0},{1,129},{129,1},{2,130},{130,2},{3,131},{131,3},{4... | collective-permute-start | bytes 36872 | tf_op jit(solution)/shard_map/ppermute | solution.py:424
